TPU v7x, 128 devices: a whole 4x4x4 slice. The times are simulated.
128 devices in a mesh: obs: 8 (over y, core), src: 16 (over x, z).
Axes of the slice: x: 4, y: 4, z: 4, core: 2. Of those that a mesh axis runs over, the one named last changes fastest.
Arguments:
- data: float32 [1024, 1536], P(('obs', 'src')), may hold values from -170 to 170
- obs_points: float32 [1024, 3, 256], P('obs'), may hold values from 0 to 32, as said below
- src_points: float32 [1024, 3, 256], P('src'), may hold values from -0.4 to 32, as said below
- obs_basis: float32 [1024, 64, 1536], P(('obs', 'src')), may hold values from -0.09375 to 0.09375
- src_basis: float32 [1024, 64, 256], P(('src', 'obs')), may hold values from -0.375 to 0.375
- couplings: float32 [8, 16, 320, 64, 64], P('obs', 'src'), may hold values from -0.75 to 0.75
- near_pairs: int32 [8, 16, 72], P('obs', 'src'), may hold values from -1 to 8191, as said below
- far_pairs: int32 [8, 16, 320], P('obs', 'src'), may hold values from -1 to 8191, as said below
Outputs:
- sources: float32 [1024, 256], P(('src', 'obs'))
- residual: float32 [1024, 1536], P(('obs', 'src'))
- normal_residual: float32 [1024, 256], P(('src', 'obs'))
- misfit: float32 [3], replicated
Inputs may be any that keep to these rules, and one draw needn't show every extreme that they name: Live entries of every block come first and -1 fills the remaining slots; a live entry o * 64 + s pairs local observation leaf o with local source leaf s; no pair is listed twice, and no pair is in both near_pairs and far_pairs. Leaves lie on surface tiles: observation leaf n on tile row (n // 32 + c) % 32, tile column n % 32, with one c of 0 to 3 for all leaves of a draw; source leaf m = j * 64 + h * 8 + l (0 <= h < 8, 0 <= l < 8) on tile row (l % 4) * 8 + h, tile column j * 2 + l // 4. A near pair joins two leaves whose tile rows differ by at most one and whose tile columns differ by at most one. `far_pairs`: live entries of every block come first and -1 fills the remaining slots; a live entry o * 64 + s pairs local observation leaf o with local source leaf s, coupled by the matrix in the same slot of couplings; no pair is listed twice; on the tiles described for near_pairs, the larger of its two leaves' tile row and tile column differences is two or three. `obs_points`: the third coordinate of every observation point lies in [0.5, 0.9]. `src_points`: the third coordinate of every source lies in [-0.4, -0.1].
All inputs are finite; a program needn't handle non-finite values.
Results may differ from a plain program's by a relative error of at most 0.0003.
Values sent between devices are 32-bit elements; how exact they have to be, the bound alone decides.
No kernel may reach another device: no remote copies, remote signals or barrier semaphores. Data moves between devices by JAX's collectives and lax.ppermute only.
A program may use at most 128 MiB of HBM per device.

v0:
```python
import jax
import jax.numpy as jnp
from jax import lax
from jax.sharding import Mesh
from jax.sharding import PartitionSpec as P

ITERS = 2
OBS_SRC = ("obs_0", "obs_1", "src_0", "src_1")
SRC = ("src_0", "src_1")
OBS = ("obs_0", "obs_1")
SRC_OBS = ("src_0", "src_1", "obs_0", "obs_1")


exact = lax.Precision.HIGHEST


def over_axes(value, axes):
    for axis in axes:
        value = lax.psum(value, axis)
    return value


def from_everyone(value, axis):
    copies = jnp.broadcast_to(value, (lax.axis_size(axis), *value.shape))
    return lax.all_to_all(copies, axis, split_axis=0, concat_axis=0, tiled=True)


def laid_out(pieces, dim):
    lengths = list(pieces.shape[1:])
    lengths[dim] *= pieces.shape[0]
    return jnp.moveaxis(pieces, 0, dim).reshape(lengths)


def gathered_copies(value, axis, dim):
    pieces = from_everyone(value, axis)
    return laid_out(pieces, dim)


def side_by_side(arrays, axis, dim, along):
    ends, at = ([], 0)
    for a in arrays[:-1]:
        at += a.shape[along]
        ends.append(at)
    both = jnp.concatenate(arrays, axis=along)
    return tuple(jnp.split(lax.all_gather(both, axis, axis=dim, tiled=True), ends, axis=along))


def cut_along(value, dim, devices):
    before, after = (value.shape[:dim], value.shape[dim + 1 :])
    return jnp.moveaxis(value.reshape(*before, devices, -1, *after), dim, 0)


def summed_on_arrival(value, axis, dim):
    pieces = cut_along(value, dim, lax.axis_size(axis))
    arrived = lax.all_to_all(pieces, axis, split_axis=0, concat_axis=0, tiled=True)
    return arrived.sum(axis=0)


def sent_together(arrays, axis, dim, along):
    widths = [a.shape[along] for a in arrays]
    both = jnp.concatenate(arrays, axis=along)
    out = summed_on_arrival(both, axis, dim)
    return tuple(jnp.split(out, [sum(widths[:k]) for k in range(1, len(widths))], axis=along))


def tensor_parts(obs_pts, src_pts):
    diff_x = obs_pts[:, 0, :, None] - src_pts[:, 0, None, :]
    diff_y = obs_pts[:, 1, :, None] - src_pts[:, 1, None, :]
    diff_z = obs_pts[:, 2, :, None] - src_pts[:, 2, None, :]
    inverse = lax.rsqrt(diff_x * diff_x + diff_y * diff_y + diff_z * diff_z)
    inv_cube = inverse * inverse * inverse / obs_pts.shape[-1]
    inv_fifth = 3.0 * inv_cube * inverse * inverse
    return (
        inv_fifth * diff_x * diff_x - inv_cube,
        inv_fifth * diff_x * diff_y,
        inv_fifth * diff_x * diff_z,
        inv_fifth * diff_y * diff_y - inv_cube,
        inv_fifth * diff_y * diff_z,
        inv_fifth * diff_z * diff_z - inv_cube,
    )


def near_loop(obs_ids, src_ids, pair_count, obs_pts, src_pts, source, target, forward, group_size):
    length = obs_ids.shape[0]
    padding = -length % group_size
    obs_ids = jnp.concatenate([obs_ids, jnp.zeros((padding,), jnp.int32)])
    src_ids = jnp.concatenate([src_ids, jnp.zeros((padding,), jnp.int32)])

    def one_group(group_index, running):
        first_slot = (group_index * group_size).astype(jnp.int32)
        obs_take = lax.dynamic_slice_in_dim(obs_ids, first_slot, group_size)
        src_take = lax.dynamic_slice_in_dim(src_ids, first_slot, group_size)
        in_range = first_slot + jnp.arange(group_size, dtype=jnp.int32) < pair_count
        tensor = tensor_parts(obs_pts[obs_take], src_pts[src_take])
        if forward:
            strengths = jnp.where(in_range[:, None], source[src_take], 0.0)[:, None, :]
            contributions = jnp.stack(
                [jnp.sum(component * strengths, axis=2) for component in tensor], axis=1
            )
            return running.at[obs_take].add(contributions.reshape(group_size, -1))
        residual_rows = jnp.where(in_range[:, None], source[obs_take], 0.0).reshape(
            group_size, 6, -1
        )
        weighted = tensor[0] * residual_rows[:, 0, :, None]
        for which in range(1, 6):
            weighted = weighted + tensor[which] * residual_rows[:, which, :, None]
        return running.at[src_take].add(jnp.sum(weighted, axis=1))

    groups = (pair_count + group_size - 1) // group_size
    return lax.fori_loop(0, groups, one_group, target)


def compact(chosen):
    length = chosen.shape[0]
    position = jnp.cumsum(chosen.astype(jnp.int32)) - 1
    target = jnp.where(chosen, position, length)
    picked = (
        jnp.zeros((length,), jnp.int32)
        .at[target]
        .set(jnp.arange(length, dtype=jnp.int32), mode="drop")
    )
    return (picked, jnp.sum(chosen.astype(jnp.int32)))


def global_total(value):
    return over_axes(value, OBS_SRC)


def paired_totals(first, second):
    return (over_axes(first, OBS_SRC), over_axes(second, OBS_SRC))


def shards(data, obs_points, src_points, obs_basis, src_basis, couplings, near_pairs, far_pairs):
    own_rows = data.shape[0]
    obs_sub = obs_points.shape[0]
    src_sub = src_points.shape[0]
    leaf_size = obs_points.shape[-1]
    rank_size = src_basis.shape[1]
    capacity = near_pairs.shape[-1]
    group_size = 8
    column = lax.axis_index(SRC)
    coupling = couplings[0, 0]
    far_list = far_pairs[0, 0]
    far_live = far_list >= 0
    far_safe = jnp.where(far_live, far_list, 0)
    far_obs = far_safe // src_sub
    far_src = far_safe % src_sub
    row_lists = gathered_copies(near_pairs, SRC, 1)[0].reshape(-1)
    all_points = lax.all_gather(src_points, SRC, axis=0, tiled=True)
    slot_ids = jnp.arange(row_lists.shape[0], dtype=jnp.int32)
    row_safe = jnp.where(row_lists >= 0, row_lists, 0)
    local_obs = row_safe // src_sub
    owned = (row_lists >= 0) & (local_obs // own_rows == column)
    picked, near_count = compact(owned)
    near_obs = jnp.clip(local_obs[picked] - column * own_rows, 0, own_rows - 1)
    near_src = slot_ids[picked] // capacity * src_sub + row_safe[picked] % src_sub
    own_points = lax.dynamic_slice_in_dim(obs_points, column * own_rows, own_rows)

    def far_adjoint(coeff_sub):
        chosen_coeffs = jnp.where(far_live[:, None], coeff_sub[far_obs], 0.0)
        far_terms = jnp.einsum("ckl,ck->cl", coupling, chosen_coeffs, precision=exact)
        return jnp.zeros((src_sub, rank_size), jnp.float32).at[far_src].add(far_terms)

    def apply_adjoint(values):
        coeff_own = jnp.einsum("nkm,nm->nk", obs_basis, values, precision=exact)
        coeff_sub = gathered_copies(coeff_own, SRC, 0)
        near_all = near_loop(
            near_obs,
            near_src,
            near_count,
            own_points,
            all_points,
            values,
            jnp.zeros((all_points.shape[0], leaf_size), jnp.float32),
            False,
            group_size,
        )
        near_block = summed_on_arrival(near_all, SRC, 0)
        coeff_src = far_adjoint(coeff_sub)
        near_own, coeff_back = sent_together((near_block, coeff_src), OBS, 0, 1)
        return near_own + jnp.einsum("nk,nkq->nq", coeff_back, src_basis, precision=exact)

    residual = data
    normal = apply_adjoint(residual)
    gamma_now = global_total(jnp.sum(normal * normal))
    misfit_now = global_total(jnp.sum(residual * residual))
    history = [misfit_now]
    direction = normal
    solution = jnp.zeros_like(normal)
    for iteration in range(ITERS):
        apply_coeff_own = jnp.einsum("nkq,nq->nk", src_basis, direction, precision=exact)
        gathered, apply_coeff_sub = side_by_side((direction, apply_coeff_own), OBS, 0, 1)
        far_chosen_coeffs = jnp.where(far_live[:, None], apply_coeff_sub[far_src], 0.0)
        far_far_terms = jnp.einsum("ckl,cl->ck", coupling, far_chosen_coeffs, precision=exact)
        coeff_obs = jnp.zeros((obs_sub, rank_size), jnp.float32).at[far_obs].add(far_far_terms)
        everything = gathered_copies(gathered, SRC, 0)
        apply_coeff_back = summed_on_arrival(coeff_obs, SRC, 0)
        apply_near_own = near_loop(
            near_obs,
            near_src,
            near_count,
            own_points,
            all_points,
            everything,
            jnp.zeros((own_rows, 6 * leaf_size), jnp.float32),
            True,
            group_size,
        )
        projected = apply_near_own + jnp.einsum(
            "nk,nkm->nm", apply_coeff_back, obs_basis, precision=exact
        )
        curvature, cross_term = paired_totals(
            jnp.sum(projected * projected), jnp.sum(residual * projected)
        )
        step_size = gamma_now / curvature
        solution = solution + step_size * direction
        residual = residual - step_size * projected
        misfit_now = misfit_now - 2.0 * step_size * cross_term + step_size * step_size * curvature
        history.append(misfit_now)
        normal = apply_adjoint(residual)
        gamma_next = global_total(jnp.sum(normal * normal))
        direction = normal + gamma_next / gamma_now * direction
        gamma_now = gamma_next
    return (solution, residual, normal, jnp.stack(history))


def solution(mesh):
    finer = Mesh(mesh.devices.reshape(4, 2, 4, 4), ("obs_0", "obs_1", "src_0", "src_1"))
    return jax.shard_map(
        shards,
        mesh=finer,
        in_specs=(
            P(OBS_SRC, None),
            P(OBS, None, None),
            P(SRC, None, None),
            P(OBS_SRC, None, None),
            P(SRC_OBS, None, None),
            P(OBS, SRC, None, None, None),
            P(OBS, SRC, None),
            P(OBS, SRC, None),
        ),
        out_specs=(P(SRC_OBS, None), P(OBS_SRC, None), P(SRC_OBS, None), P()),
        check_vma=False,
    )
```

profile of v0, /device:TPU:1, one launch (start us, length us, event | category | flops | bytes accessed | tf_op | source)
XLA Modules:
  0.0 794.1 jit_solution(15774144450242854606)
XLA Ops:
  9.4 8.4 %all-to-all-start = ((s32[16,1,1,72]{3,2,1,0:T(1,128)}), s32[16,1,1,72]{3,2,1,0:T(1,128)S(1)}, u32[]{:S(2)}, u32[]{:S(2)}) async-start(s32[16,1,1,72]{3,2,1,0:T(1,128)} %broadcast_in_dim.201), calls=%async_computation | async-start | bytes 16384 | tf_op jit(solution)/shard_map/all_to_all | solution.py:25
  67.9 56.3 %while.60 = (s32[]{:T(128)}, f32[1024,256]{1,0:T(8,128)}, s32[]{:T(128)}, s32[1152]{0:T(1024)S(1)}, s32[1152]{0:T(1024)S(1)}, /*index=5*/f32[8,3,256]{2,1,0:T(4,...) while((s32[]{:T(128)}, f32[1024,256]{1,0:T(8,128)}, ...), condition=%wide.region_7.8_spmd, body=%wide.region_4.7_spmd.sunk | while | flops 19937348 | bytes 729607 | solution.py:110
  129.7 12.4 %copy.31 = f32[320,64,64]{2,1,0:T(8,128)} copy(f32[320,64,64]{0,2,1:T(8,128)} %bitcast.404) | data formatting | bytes 10485760 | tf_op jit(solution)/shard_map/squeeze | solution.py:142
  142.1 12.5 %copy.38 = f32[320,64,64]{1,2,0:T(8,128)} copy(f32[320,64,64]{0,2,1:T(8,128)} %bitcast.405) | data formatting | bytes 10485760 | tf_op jit(solution)/shard_map/squeeze | solution.py:142
  157.2 11.5 %fusion.141 = f32[320,1,64]{2,1,0:T(1,128)S(1)} fusion(f32[320,64,1]{1,2,0:T(1,128)S(1)} %bitcast.416, f32[320,64,64]{2,1,0:T(8,128)} %copy.31), kind=kOutput, calls=%fused_computation.424 | convolution fusion | flops 15728640 | bytes 5406720 | tf_op jit(solution)/shard_map/ckl,ck->cl/dot_general | solution.py:161
  173.2 17.6 %all-to-all-start.3 = ((f32[8,8,320]{2,1,0:T(8,128)}), f32[8,8,320]{2,1,0:T(8,128)S(1)}, u32[]{:S(2)}, u32[]{:S(2)}) async-start(f32[8,8,320]{2,1,0:T(8,128)} %maximum_bitcast_fusion), calls=%async_computation.3 | async-start | bytes 196608 | tf_op jit(solution)/shard_map/all_to_all | solution.py:55
  199.4 13.8 %all_gather.10 = f32[64,320]{1,0:T(8,128)S(1)} all-gather(f32[8,320]{1,0:T(8,128)S(1)} %pad_maximum_fusion), channel_id=1, replica_groups=mesh['obs_0'=4,'obs_1'=2,'src_0'=4,'src_1'=4] {'obs_0','obs_1'}, dimensions={0}, use_global_device_ids=true | all-gather | bytes 92160 | tf_op jit(solution)/shard_map/all_gather | solution.py:45
  214.4 12.2 %fusion.143 = f32[320,1,64]{2,1,0:T(1,128)} fusion(f32[320,64,1]{1,2,0:T(1,128)S(1)} %bitcast.417, f32[320,64,64]{1,2,0:T(8,128)} %copy.38), kind=kOutput, calls=%fused_computation.426 | convolution fusion | flops 15728640 | bytes 5406720 | tf_op jit(solution)/shard_map/ckl,cl->ck/dot_general | solution.py:194
  251.0 12.9 %all-to-all-done.4 = f32[16,64,256]{2,1,0:T(8,128)} async-done(((f32[16,64,256]{2,1,0:T(8,128)}), f32[16,64,256]{2,1,0:T(8,128)}, u32[]{:S(2)}, u32[]{:S(2)}) %all-to-all-start.4) | async-done | bytes 1048608 | tf_op jit(solution)/shard_map/all_to_all | solution.py:25
  263.9 55.6 %while.61 = (s32[]{:T(128)}, f32[8,1536]{1,0:T(8,128)S(1)}, s32[]{:T(128)}, s32[1152]{0:T(1024)S(1)}, f32[8,3,256]{2,1,0:T(4,128)S(1)}, /*index=5*/s32[1152]{0:T...) while((s32[]{:T(128)}, f32[8,1536]{1,0:T(8,128)S(1)}, ...), condition=%wide.region_24.25_spmd, body=%wide.region_16.24_spmd.sunk | while | flops 19927108 | bytes 688647 | solution.py:110
  320.1 7.7 all-reduce.5
  334.2 13.9 %all-reduce.3 = (f32[]{:T(128)}, f32[]{:T(128)}) all-reduce(f32[]{:T(128)} %get-tuple-element.812, f32[]{:T(128)} %get-tuple-element.813), channel_id=1, replica_groups=mesh['obs_0'=4,'obs_1'=2,'src_0'=4,'src_1'=4] {'src_0'}, use_global_device_ids=true, to_apply=%region_14.15 | all-reduce | flops 2 | bytes 16 | tf_op jit(solution)/shard_map/psum | solution.py:19
  348.1 9.5 %all-reduce.1 = (f32[]{:T(128)}, f32[]{:T(128)}) all-reduce(f32[]{:T(128)} %get-tuple-element.800, f32[]{:T(128)} %get-tuple-element.801), channel_id=1, replica_groups=mesh['obs_0'=4,'obs_1'=2,'src_0'=4,'src_1'=4] {'src_1'}, use_global_device_ids=true, to_apply=%region_15.16 | all-reduce | flops 2 | bytes 16 | tf_op jit(solution)/shard_map/psum | solution.py:19
  367.1 56.8 %while.62 = (s32[]{:T(128)}, f32[1024,256]{1,0:T(8,128)}, s32[]{:T(128)}, s32[1152]{0:T(1024)S(1)}, s32[1152]{0:T(1024)S(1)}, /*index=5*/f32[8,3,256]{2,1,0:T(4,...) while((s32[]{:T(128)}, f32[1024,256]{1,0:T(8,128)}, ...), condition=%wide.region_35.36_spmd, body=%wide.region_32.35_spmd.sunk | while | flops 19937348 | bytes 729607 | solution.py:110
  423.9 6.7 all-to-all-start.6
  432.7 11.5 %fusion.145 = f32[320,1,64]{2,1,0:T(1,128)S(1)} fusion(f32[320,64,1]{1,2,0:T(1,128)S(1)} %bitcast.418, f32[320,64,64]{2,1,0:T(8,128)} %copy.31), kind=kOutput, calls=%fused_computation.428 | convolution fusion | flops 15728640 | bytes 5406720 | tf_op jit(solution)/shard_map/ckl,ck->cl/dot_general | solution.py:161
  448.2 23.1 %all_to_all.70 = f32[8,8,320]{2,1,0:T(8,128)S(1)} all-to-all(f32[8,8,320]{2,1,0:T(8,128)S(1)} %maximum_bitcast_fusion.1), channel_id=1, replica_groups=mesh['obs_0'=4,'obs_1'=2,'src_0'=4,'src_1'=4] {'obs_0','obs_1'}, dimensions={0} | all-to-all | bytes 163840 | tf_op jit(solution)/shard_map/all_to_all | solution.py:55
  473.3 7.5 psum.204
  486.4 9.1 %psum.206 = f32[]{:T(128)} all-reduce(f32[]{:T(128)} %psum.205), channel_id=1, replica_groups=mesh['obs_0'=4,'obs_1'=2,'src_0'=4,'src_1'=4] {'src_0'}, use_global_device_ids=true, to_apply=%region_42.43 | all-reduce | flops 1 | bytes 8 | tf_op jit(solution)/shard_map/psum | solution.py:19
  495.5 9.3 %psum.207 = f32[]{:T(128)} all-reduce(f32[]{:T(128)} %psum.206), channel_id=1, replica_groups=mesh['obs_0'=4,'obs_1'=2,'src_0'=4,'src_1'=4] {'src_1'}, use_global_device_ids=true, to_apply=%region_43.44 | all-reduce | flops 1 | bytes 8 | tf_op jit(solution)/shard_map/psum | solution.py:19
  507.8 17.2 %all_gather.11 = f32[64,320]{1,0:T(8,128)S(1)} all-gather(f32[8,320]{1,0:T(8,128)S(1)} %pad_maximum_fusion.1), channel_id=1, replica_groups=mesh['obs_0'=4,'obs_1'=2,'src_0'=4,'src_1'=4] {'obs_0','obs_1'}, dimensions={0}, use_global_device_ids=true | all-gather | bytes 92160 | tf_op jit(solution)/shard_map/all_gather | solution.py:45
  527.0 12.2 %fusion.147 = f32[320,1,64]{2,1,0:T(1,128)} fusion(f32[320,64,1]{1,2,0:T(1,128)S(1)} %bitcast.415, f32[320,64,64]{1,2,0:T(8,128)} %copy.38), kind=kOutput, calls=%fused_computation.430 | convolution fusion | flops 15728640 | bytes 5406720 | tf_op jit(solution)/shard_map/ckl,cl->ck/dot_general | solution.py:194
  560.5 13.1 %all-to-all-done.9 = f32[16,64,256]{2,1,0:T(8,128)} async-done(((f32[16,64,256]{2,1,0:T(8,128)}), f32[16,64,256]{2,1,0:T(8,128)}, u32[]{:S(2)}, u32[]{:S(2)}) %all-to-all-start.9) | async-done | bytes 1048608 | tf_op jit(solution)/shard_map/all_to_all | solution.py:25
  573.5 55.6 %while.63 = (s32[]{:T(128)}, f32[8,1536]{1,0:T(8,128)S(1)}, s32[]{:T(128)}, s32[1152]{0:T(1024)S(1)}, f32[8,3,256]{2,1,0:T(4,128)S(1)}, /*index=5*/s32[1152]{0:T...) while((s32[]{:T(128)}, f32[8,1536]{1,0:T(8,128)S(1)}, ...), condition=%wide.region_52.53_spmd, body=%wide.region_44.52_spmd.sunk | while | flops 19927108 | bytes 688647 | solution.py:110
  629.7 7.3 all-reduce.4
  637.0 6.8 all-reduce.6
  643.9 13.5 %all-reduce.2 = (f32[]{:T(128)}, f32[]{:T(128)}, f32[]{:T(128)}, f32[]{:T(128)}) all-reduce(f32[]{:T(128)} %get-tuple-element.808, f32[]{:T(128)} %get-tuple-element.809, f32[]{:T(128)} %get-tuple-element.810, f32[]{:T(128)} %get-tuple-element.811), channel_id=1, replica_groups=mesh['obs_0'=4,'obs_1'=2,'src_0'=4,'src_1'=4] {'src_0'}, use_global_device_ids=true, to_apply=%region_58.59 | all-reduce | flops 4 | bytes 32 | tf_op jit(solution)/shard_map/psum | solution.py:19
  657.4 9.6 %all-reduce = (f32[]{:T(128)}, f32[]{:T(128)}, f32[]{:T(128)}, f32[]{:T(128)}) all-reduce(f32[]{:T(128)} %get-tuple-element.796, f32[]{:T(128)} %get-tuple-element.797, f32[]{:T(128)} %get-tuple-element.798, f32[]{:T(128)} %get-tuple-element.799), channel_id=1, replica_groups=mesh['obs_0'=4,'obs_1'=2,'src_0'=4,'src_1'=4] {'src_1'}, use_global_device_ids=true, to_apply=%region_59.60 | all-reduce | flops 4 | bytes 32 | tf_op jit(solution)/shard_map/psum | solution.py:19
  676.3 56.3 %while.64 = (s32[]{:T(128)}, f32[1024,256]{1,0:T(8,128)}, s32[]{:T(128)}, s32[1152]{0:T(1024)S(1)}, s32[1152]{0:T(1024)S(1)}, /*index=5*/f32[8,3,256]{2,1,0:T(4,...) while((s32[]{:T(128)}, f32[1024,256]{1,0:T(8,128)}, ...), condition=%wide.region_63.64_spmd, body=%wide.region_60.63_spmd.sunk | while | flops 19937348 | bytes 729607 | solution.py:110
  732.6 6.7 all-to-all-start.11
  745.1 11.5 %fusion.149 = f32[320,1,64]{2,1,0:T(1,128)S(1)} fusion(f32[320,64,1]{1,2,0:T(1,128)S(1)} %bitcast.414, f32[320,64,64]{2,1,0:T(8,128)} %copy.31), kind=kOutput, calls=%fused_computation.432 | convolution fusion | flops 15728640 | bytes 5406720 | tf_op jit(solution)/shard_map/ckl,ck->cl/dot_general | solution.py:161
  761.1 18.6 %all-to-all-start.13 = ((f32[8,8,320]{2,1,0:T(8,128)}), f32[8,8,320]{2,1,0:T(8,128)S(1)}, u32[]{:S(2)}, u32[]{:S(2)}) async-start(f32[8,8,320]{2,1,0:T(8,128)} %maximum_bitcast_fusion.2), calls=%async_computation.13 | async-start | bytes 196608 | tf_op jit(solution)/shard_map/all_to_all | solution.py:55
  (694 shorter events, 451.7 us)
Async XLA Ops:
  7.2 10.6 %copy-start = (f32[8,64,1536]{2,1,0:T(8,128)S(1)}, f32[8,64,1536]{2,1,0:T(8,128)}, u32[]{:S(2)}) copy-start(f32[8,64,1536]{2,1,0:T(8,128)} %param.21) | copy-start | bytes 9437188
  7.2 53.7 %all-gather.2.cloned.1.call-start = ((), (), s32[]{:S(2)}) async-start(), calls=%async_computation.14 | async-start | bytes 3342336 | tf_op jit(solution)/shard_map/all_gather | solution.py:149
  9.4 14.8 %all-to-all-start = ((s32[16,1,1,72]{3,2,1,0:T(1,128)}), s32[16,1,1,72]{3,2,1,0:T(1,128)S(1)}, u32[]{:S(2)}, u32[]{:S(2)}) async-start(s32[16,1,1,72]{3,2,1,0:T(1,128)} %broadcast_in_dim.201), calls=%async_computation | async-start | bytes 16384 | tf_op jit(solution)/shard_map/all_to_all | solution.py:25
  24.2 100.1 %all-to-all-start.2 = ((f32[16,1,512]{2,1,0:T(1,128)}), f32[16,1,512]{2,1,0:T(1,128)S(1)}, u32[]{:S(2)}, u32[]{:S(2)}) async-start(f32[16,1,512]{2,1,0:T(1,128)} %reshape.846), calls=%async_computation.2 | async-start | bytes 65536 | tf_op jit(solution)/shard_map/all_to_all | solution.py:25
  59.1 8.8 %copy-start.1 = (f32[8,1536]{1,0:T(8,128)S(1)}, f32[8,1536]{1,0:T(8,128)}, u32[]{:S(2)}) copy-start(f32[8,1536]{1,0:T(8,128)} %param.18) | copy-start | bytes 147460
  124.2 17.9 %copy-start.3 = (s32[1152]{0:T(1024)}, s32[1152]{0:T(1024)S(1)}, u32[]{:S(2)}) copy-start(s32[1152]{0:T(1024)S(1)} %get-tuple-element.1530) | copy-start | bytes 13828
  124.2 5.4 copy-start.16
  124.2 47.0 %all-to-all-start.1 = ((f32[16,64,256]{2,1,0:T(8,128)}), f32[16,64,256]{2,1,0:T(8,128)}, u32[]{:S(2)}, u32[]{:S(2)}) async-start(f32[16,64,256]{2,1,0:T(8,128)} %bitcast.406), calls=%async_computation.1 | async-start | bytes 2097152 | tf_op jit(solution)/shard_map/all_to_all | solution.py:55
  129.7 61.1 %copy-start.14 = (s32[320]{0:T(512)}, s32[320]{0:T(512)S(1)}, u32[]{:S(2)}) copy-start(s32[320]{0:T(512)S(1)} %get-tuple-element.699) | copy-start | bytes 3844
  129.7 96.9 %copy-start.15 = (s32[320]{0:T(512)}, s32[320]{0:T(512)S(1)}, u32[]{:S(2)}) copy-start(s32[320]{0:T(512)S(1)} %get-tuple-element.698) | copy-start | bytes 3844
  154.7 14.1 %copy-start.7 = (s32[1024]{0:T(1024)}, s32[1024]{0:T(1024)S(1)}, u32[]{:S(2)}) copy-start(s32[1024]{0:T(1024)S(1)} %pad_clamp_fusion.12) | copy-start | bytes 12292
  154.7 59.6 %copy-start.10 = (pred[320]{0:T(512)(128)(4,1)}, pred[320]{0:T(512)(128)(4,1)S(1)}, u32[]{:S(2)}) copy-start(pred[320]{0:T(512)(128)(4,1)S(1)} %compare_reduce_fusion) | copy-start | bytes 964
  173.2 22.6 %all-to-all-start.3 = ((f32[8,8,320]{2,1,0:T(8,128)}), f32[8,8,320]{2,1,0:T(8,128)S(1)}, u32[]{:S(2)}, u32[]{:S(2)}) async-start(f32[8,8,320]{2,1,0:T(8,128)} %maximum_bitcast_fusion), calls=%async_computation.3 | async-start | bytes 196608 | tf_op jit(solution)/shard_map/all_to_all | solution.py:55
  190.8 35.8 %copy-start.13 = (s32[1024]{0:T(1024)}, s32[1024]{0:T(1024)S(1)}, u32[]{:S(2)}) copy-start(s32[1024]{0:T(1024)S(1)} %pad_clamp_fusion.11) | copy-start | bytes 12292
  230.1 13.0 %all-to-all-start.5 = ((f32[16,1,512]{2,1,0:T(1,128)}), f32[16,1,512]{2,1,0:T(1,128)S(1)}, u32[]{:S(2)}, u32[]{:S(2)}) async-start(f32[16,1,512]{2,1,0:T(1,128)} %reshape.848), calls=%async_computation.5 | async-start | bytes 65536 | tf_op jit(solution)/shard_map/all_to_all | solution.py:55
  244.2 19.7 %all-to-all-start.4 = ((f32[16,64,256]{2,1,0:T(8,128)}), f32[16,64,256]{2,1,0:T(8,128)}, u32[]{:S(2)}, u32[]{:S(2)}) async-start(f32[16,64,256]{2,1,0:T(8,128)} %broadcast_in_dim.208), calls=%async_computation.4 | async-start | bytes 2097152 | tf_op jit(solution)/shard_map/all_to_all | solution.py:25
  248.5 15.4 %copy-start.4 = (s32[1152]{0:T(1024)S(1)}, s32[1152]{0:T(1024)}, u32[]{:S(2)}) copy-start(s32[1152]{0:T(1024)} %copy-done.3) | copy-start | bytes 13828
  362.4 61.6 %all-to-all-start.7 = ((f32[16,1,512]{2,1,0:T(1,128)}), f32[16,1,512]{2,1,0:T(1,128)S(1)}, u32[]{:S(2)}, u32[]{:S(2)}) async-start(f32[16,1,512]{2,1,0:T(1,128)} %reshape.850), calls=%async_computation.7 | async-start | bytes 65536 | tf_op jit(solution)/shard_map/all_to_all | solution.py:25
  423.9 20.3 %copy-start.5 = (s32[1152]{0:T(1024)}, s32[1152]{0:T(1024)S(1)}, u32[]{:S(2)}) copy-start(s32[1152]{0:T(1024)S(1)} %get-tuple-element.1532) | copy-start | bytes 13828
  423.9 7.5 copy-start.8
  423.9 8.6 %copy-start.11 = (pred[320]{0:T(512)(128)(4,1)S(1)}, pred[320]{0:T(512)(128)(4,1)}, u32[]{:S(2)}) copy-start(pred[320]{0:T(512)(128)(4,1)} %copy-done.10) | copy-start | bytes 964
  423.9 22.9 %all-to-all-start.6 = ((f32[16,64,256]{2,1,0:T(8,128)}), f32[16,64,256]{2,1,0:T(8,128)}, u32[]{:S(2)}, u32[]{:S(2)}) async-start(f32[16,64,256]{2,1,0:T(8,128)} %bitcast.407), calls=%async_computation.6 | async-start | bytes 2097152 | tf_op jit(solution)/shard_map/all_to_all | solution.py:55
  542.7 9.9 %all-to-all-start.10 = ((f32[16,1,512]{2,1,0:T(1,128)}), f32[16,1,512]{2,1,0:T(1,128)S(1)}, u32[]{:S(2)}, u32[]{:S(2)}) async-start(f32[16,1,512]{2,1,0:T(1,128)} %reshape.852), calls=%async_computation.10 | async-start | bytes 65536 | tf_op jit(solution)/shard_map/all_to_all | solution.py:55
  553.7 19.8 %all-to-all-start.9 = ((f32[16,64,256]{2,1,0:T(8,128)}), f32[16,64,256]{2,1,0:T(8,128)}, u32[]{:S(2)}, u32[]{:S(2)}) async-start(f32[16,64,256]{2,1,0:T(8,128)} %broadcast_in_dim.210), calls=%async_computation.9 | async-start | bytes 2097152 | tf_op jit(solution)/shard_map/all_to_all | solution.py:25
  558.0 15.5 %copy-start.6 = (s32[1152]{0:T(1024)S(1)}, s32[1152]{0:T(1024)}, u32[]{:S(2)}) copy-start(s32[1152]{0:T(1024)} %copy-done.5) | copy-start | bytes 13828
  671.7 60.9 %all-to-all-start.12 = ((f32[16,1,512]{2,1,0:T(1,128)}), f32[16,1,512]{2,1,0:T(1,128)S(1)}, u32[]{:S(2)}, u32[]{:S(2)}) async-start(f32[16,1,512]{2,1,0:T(1,128)} %reshape.854), calls=%async_computation.12 | async-start | bytes 65536 | tf_op jit(solution)/shard_map/all_to_all | solution.py:25
  732.6 24.0 %copy-start.2 = (f32[8,1536]{1,0:T(8,128)}, f32[8,1536]{1,0:T(8,128)S(1)}, u32[]{:S(2)}) copy-start(f32[8,1536]{1,0:T(8,128)S(1)} %get-tuple-element.1496) | copy-start | bytes 147460
  732.6 11.2 %copy-start.9 = (s32[1024]{0:T(1024)S(1)}, s32[1024]{0:T(1024)}, u32[]{:S(2)}) copy-start(s32[1024]{0:T(1024)} %copy-done.7) | copy-start | bytes 12292
  732.6 12.3 %copy-start.12 = (pred[320]{0:T(512)(128)(4,1)S(1)}, pred[320]{0:T(512)(128)(4,1)}, u32[]{:S(2)}) copy-start(pred[320]{0:T(512)(128)(4,1)} %copy-done.10) | copy-start | bytes 964
  732.6 26.6 %all-to-all-start.11 = ((f32[16,64,256]{2,1,0:T(8,128)}), f32[16,64,256]{2,1,0:T(8,128)}, u32[]{:S(2)}, u32[]{:S(2)}) async-start(f32[16,64,256]{2,1,0:T(8,128)} %bitcast.408), calls=%async_computation.11 | async-start | bytes 2097152 | tf_op jit(solution)/shard_map/all_to_all | solution.py:55
  761.1 23.6 %all-to-all-start.13 = ((f32[8,8,320]{2,1,0:T(8,128)}), f32[8,8,320]{2,1,0:T(8,128)S(1)}, u32[]{:S(2)}, u32[]{:S(2)}) async-start(f32[8,8,320]{2,1,0:T(8,128)} %maximum_bitcast_fusion.2), calls=%async_computation.13 | async-start | bytes 196608 | tf_op jit(solution)/shard_map/all_to_all | solution.py:55
Sparse Core Ops, SparseCore 0:
  10.2 50.6 all-gather.1
where the time goes:
time: 808 us; the launch traced here: 794 us
  other arithmetic  196 us (24%)
  local copies, waits for them, and re-layouts  187 us (23%)
  blocking collectives  160 us (20%)
  starting transfers between devices  94.6 us (12%)
  matrix products  78.4 us (10%)
  waiting for transfers between devices  51.3 us (6%)
  between operations  22.9 us (3%)
    psum x12, blocking collectives, over_axes(): value = lax.psum(value, axis)  106 us
    gather x50, local copies, waits for them, and re-layouts, one_group(): tensor = tensor_parts(obs_pts[obs_take], src_pts[src_take])  83.5 us
    all_to_all x7, starting transfers between devices, summed_on_arrival(): lax.all_to_all(pieces, axis, split_axis=0, concat_axis=0, tiled=True)  65 us
    reduce_sum x15, other arithmetic, one_group(): return running.at[src_take].add(jnp.sum(weighted, axis=1))  53.6 us
    scatter-add x15, other arithmetic, one_group(): return running.at[src_take].add(jnp.sum(weighted, axis=1))  42.2 us
    reduce_sum x10, other arithmetic, one_group(): jnp.sum(component * strengths, axis=2)  42.1 us
    dot_general x3, matrix products, far_adjoint(): jnp.einsum('ckl,ck->cl', coupling, chosen_coeffs, precision=exact)  34.6 us
    all_gather x2, blocking collectives, side_by_side(): lax.all_gather(both, axis, axis=dim, tiled=True)  31 us
  transfers between devices with their start and end apart: 14, of which 8 were waited for; matrix products, arithmetic and copies ran while one was open for 37% of the time, Pallas kernels for 0%

commit v1 on v0

v1 whole, which is shorter than its diff:
```python
import functools

import jax
import jax.numpy as jnp
from jax import lax
from jax.experimental import pallas as pl
from jax.experimental.pallas import tpu as pltpu
from jax.sharding import Mesh
from jax.sharding import PartitionSpec as P

OBS_SRC = ("obs_0", "obs_1", "src_0", "src_1")
SRC = ("src_0", "src_1")
OBS = ("obs_0", "obs_1")
SRC_OBS = ("src_0", "src_1", "obs_0", "obs_1")

F32 = jnp.float32
BF16 = jnp.bfloat16
PAIRS = 72
ROWS = 16
MIB = 1 << 20


def split(value):
    high = value.astype(BF16)
    return high, (value - high.astype(F32)).astype(BF16)


def mm(a, b):
    return lax.dot_general(a, b, (((1,), (0,)), ((), ())), preferred_element_type=F32)


def mm_nt(a, b):
    return lax.dot_general(a, b, (((1,), (1,)), ((), ())), preferred_element_type=F32)


def iota(shape, dim):
    return lax.broadcasted_iota(jnp.int32, shape, dim)


def lane_scalar(block, which):
    lanes = iota(block.shape, 1)
    return jnp.sum(jnp.where(lanes == 64 + which, block, 0.0), axis=1, keepdims=True)


def total(value):
    return jnp.sum(jnp.sum(value, axis=1, keepdims=True), axis=0, keepdims=True)


def with_scalars(block, scalars):
    lanes = iota(block.shape, 1)
    for which, value in enumerate(scalars):
        block = jnp.where(lanes == 64 + which, value, block)
    return block


def setup_near(slots, column, near_row, far_row, obs, src, kh, kl, pq, count, oo, oot, ost, os, fo, fot, fs, fst):
    j = column[0]
    f = near_row[...]
    live = f >= 0
    o = lax.shift_right_arithmetic(f, 6)
    s = jnp.where(live, f & 63, -1)
    oc = jnp.where(live, lax.shift_right_arithmetic(o, 5) * 4 + (o & 31) - (2 * j - 1), -1)
    a = (iota((16, 128), 0) == oc).astype(F32)
    oot[...] = a.astype(BF16)
    oo[...] = a.T.astype(BF16)
    a = (iota((64, 128), 0) == s).astype(F32)
    ost[...] = a.astype(BF16)
    os[...] = a.T.astype(BF16)
    f = far_row[...]
    live = f >= 0
    o = jnp.where(live, lax.shift_right_arithmetic(f, 6), -1)
    s = jnp.where(live, f & 63, -1)
    a = (iota((128, 384), 0) == o).astype(F32)
    fot[...] = a.astype(BF16)
    fo[...] = a.T.astype(BF16)
    a = (iota((64, 384), 0) == s).astype(F32)
    fst[...] = a.astype(BF16)
    fs[...] = a.T.astype(BF16)
    pq[...] = jnp.zeros_like(pq)

    n = lax.fori_loop(0, PAIRS, lambda t, c: c + jnp.where(slots[t] >= 0, 1, 0), 0)
    count[0] = n

    def one(t, carry):
        name = slots[t]
        p = obs[lax.shift_right_arithmetic(name, 6)]
        q = src[name & 63]
        centre = 0.5 * (jnp.mean(p, axis=1, keepdims=True) + jnp.mean(q, axis=1, keepdims=True))
        p = p - centre
        q = q - centre
        for c in range(3):
            pq[c, pl.ds(t, 1), :] = p[c : c + 1]
            pq[3 + c, pl.ds(t, 1), :] = q[c : c + 1]
        pt = jnp.concatenate([p, jnp.zeros((5, 256), F32)], axis=0).T
        for r in range(0, 256, 32):
            dx = pt[r : r + 32, 0:1] - q[0:1]
            dy = pt[r : r + 32, 1:2] - q[1:2]
            dz = pt[r : r + 32, 2:3] - q[2:3]
            inverse = lax.rsqrt(dx * dx + dy * dy + dz * dz)
            square = inverse * inverse
            fifth = square * square * (inverse * (1.0 / 256.0))
            high, low = split(fifth)
            kh[t, r : r + 32, :] = high
            kl[t, r : r + 32, :] = low
        return carry

    lax.fori_loop(0, n, one, 0)


def setup_far(c, wh, wl):
    for g in range(4):
        high, low = split(jnp.concatenate([c[4 * g + n] for n in range(4)], axis=1))
        wh[0, 64 * g : 64 * g + 64, :] = high
        wl[0, 64 * g : 64 * g + 64, :] = low


def far_matrices(x, pick, place, wh, wl, forward):
    half = jnp.where(iota(x.shape, 1) < 64, x, 0.0)
    half = half + pltpu.roll(half, 64, 1)
    high, low = split(jnp.concatenate([half, half], axis=1))
    lanes = lax.shift_right_logical(iota((16, 256), 1), 6)
    slot = iota((16, 256), 0)
    row_group = lanes == lax.shift_right_logical(slot, 2)
    col_group = lanes == (slot & 3)
    enter, leave = (col_group, row_group) if forward else (row_group, col_group)
    multiply = mm_nt if forward else mm
    picked_high = mm(pick, high)
    picked_low = mm(pick, low)
    terms = []
    for t in range(20):
        at = slice(16 * t, 16 * t + 16)
        h = jnp.where(enter, picked_high[at], 0.0).astype(BF16)
        l = jnp.where(enter, picked_low[at], 0.0).astype(BF16)
        both = multiply(jnp.concatenate([h, l], axis=0), wh[t])
        terms.append(jnp.where(leave, both[:16] + both[16:] + multiply(h, wl[t]), 0.0))
    high, low = split(jnp.concatenate(terms, axis=0))
    out = mm(place, high) + mm(place, low)
    out = out[:, :128] + out[:, 128:]
    return out + pltpu.roll(out, 64, 1)


def near_products(n, moments, results, kh, kl, multiply):
    def four(g, carry):
        for b in range(4):
            t = 4 * g + b
            at = pl.ds(pl.multiple_of(t * ROWS, ROWS), ROWS)
            high, low = split(jnp.concatenate([moments[0, at, :], moments[1, at, :]], axis=1))
            both = multiply(jnp.concatenate([high, low], axis=0), kh[t])
            both = both[:ROWS] + both[ROWS:] + multiply(high, kl[t])
            results[0, at, :] = both[:, :128]
            results[1, at, :] = both[:, 128:]
        return carry

    lax.fori_loop(0, lax.shift_right_logical(n + 3, 2), four, 0)


def store_moment(moments, g, c, value):
    at = pl.ds(g * (8 * ROWS) + c, 8, ROWS)
    moments.at[0][at, :] = value[:, :128]
    moments.at[1][at, :] = value[:, 128:]


def load_result(results, g, c):
    at = pl.ds(g * (8 * ROWS) + c, 8, ROWS)
    return jnp.concatenate([results.at[0][at, :], results.at[1][at, :]], axis=1)


def adjoint_block(count, column, recv, kh, kl, pq, oo, ost, fo, fst, wh, wl, out, yb, yp, moments, results, values):
    n = count[0]
    j = column[0]
    for t in range(4):
        col = 2 * j - 1 + t
        inside = jnp.logical_and(col >= 0, col < 32)
        holder = lax.shift_right_logical(jnp.clip(col, 0, 31), 3)
        for row in range(4):
            for half in range(2):
                piece = recv[row * 4 + holder, 2 * t + half : 2 * t + half + 1, 0:768]
                if t in (0, 3):
                    piece = jnp.where(inside, piece, 0.0)
                yb[4 * row + t : 4 * row + t + 1, 768 * half : 768 * half + 768] = piece
    high, low = split(yb[...])
    yp[...] = mm(oo[0:80, :], high) + mm(oo[0:80, :], low)
    values[...] = jnp.zeros_like(values)
    groups = lax.shift_right_logical(n + 7, 3)

    def enter(g, carry):
        at = pl.ds(pl.multiple_of(g * 8, 8), 8)
        y = [yp[at, 256 * a : 256 * a + 256] for a in range(6)]
        px, py, pz = (pq[c, at, :] for c in range(3))
        trace = y[0] + y[3] + y[5]
        hxx, hyy, hzz = (3.0 * y[a] - trace for a in (0, 3, 5))
        hxy, hxz, hyz = (3.0 * y[a] for a in (1, 2, 4))
        ax, ay, az = hxx * px, hyy * py, hzz * pz
        bx, by, bz = hxy * py + hxz * pz, hxy * px + hyz * pz, hxz * px + hyz * py
        constant = px * (ax + hxy * py) + py * (ay + hyz * pz) + pz * (az + hxz * px)
        rows = (constant, 2.0 * ax + bx, 2.0 * ay + by, 2.0 * az + bz, hxx, hxy, hxz, hyy, hyz, hzz)
        for c, row in enumerate(rows):
            store_moment(moments, g, c, row)
        return carry

    lax.fori_loop(0, groups, enter, 0)
    near_products(n, moments, results, kh, kl, mm)

    def leave(g, carry):
        at = pl.ds(pl.multiple_of(g * 8, 8), 8)
        w = [load_result(results, g, c) for c in range(10)]
        qx, qy, qz = (pq[3 + c, at, :] for c in range(3))
        z = w[0] + qx * (w[4] * qx + w[5] * qy - w[1]) + qy * (w[7] * qy + w[8] * qz - w[2])
        z = z + qz * (w[9] * qz + w[6] * qx - w[3])
        values[at, :] = jnp.where(iota((8, 256), 0) + g * 8 < n, z, 0.0)
        return carry

    lax.fori_loop(0, groups, leave, 0)
    high, low = split(values[...])
    out[:, 0:256] = mm(ost[...], high) + mm(ost[...], low)
    tails = [recv[k, :, 768:896] for k in range(16)]
    coeffs = far_matrices(jnp.concatenate(tails, axis=0), fo[0:320, :], fst[:, 0:320], wh, wl, False)
    sums = functools.reduce(jnp.add, tails)
    for k in range(8):
        part = coeffs[8 * k : 8 * k + 8]
        out[8 * k : 8 * k + 8, 256:384] = jnp.where(iota((8, 128), 1) < 64, part, sums)


def forward_block(count, column, recv, kh, kl, pq, os, oot, fs, fot, wh, wl, out, xp, moments, results, values, yb):
    n = count[0]
    j = column[0]
    high, low = split(recv[:, 0:256])
    xp[...] = mm(os[0:80, :], high) + mm(os[0:80, :], low)
    values[...] = jnp.zeros_like(values)
    groups = lax.shift_right_logical(n + 7, 3)

    def enter(g, carry):
        at = pl.ds(pl.multiple_of(g * 8, 8), 8)
        x = xp[at, :]
        qx, qy, qz = (pq[3 + c, at, :] for c in range(3))
        x1, x2, x3 = x * qx, x * qy, x * qz
        rows = (x, x1, x2, x3, x1 * qx, x1 * qy, x1 * qz, x2 * qy, x2 * qz, x3 * qz)
        for c, row in enumerate(rows):
            store_moment(moments, g, c, row)
        return carry

    lax.fori_loop(0, groups, enter, 0)
    near_products(n, moments, results, kh, kl, mm_nt)

    def leave(g, carry):
        at = pl.ds(pl.multiple_of(g * 8, 8), 8)
        s = [load_result(results, g, c) for c in range(10)]
        px, py, pz = (pq[c, at, :] for c in range(3))
        ax, ay, az = px * s[0] - s[1], py * s[0] - s[2], pz * s[0] - s[3]
        xx = px * (ax - s[1]) + s[4]
        xy = py * ax - px * s[2] + s[5]
        xz = pz * ax - px * s[3] + s[6]
        yy = py * (ay - s[2]) + s[7]
        yz = pz * ay - py * s[3] + s[8]
        zz = pz * (az - s[3]) + s[9]
        trace = xx + yy + zz
        inside = iota((8, 256), 0) + g * 8 < n
        parts = (3.0 * xx - trace, 3.0 * xy, 3.0 * xz, 3.0 * yy - trace, 3.0 * yz, 3.0 * zz - trace)
        for a, part in enumerate(parts):
            values[at, 256 * a : 256 * a + 256] = jnp.where(inside, part, 0.0)
        return carry

    lax.fori_loop(0, groups, leave, 0)
    high, low = split(values[...])
    yb[...] = mm(oot[...], high) + mm(oot[...], low)
    for t in range(4):
        holder = lax.shift_right_logical(jnp.clip(2 * j - 1 + t, 0, 31), 3)
        for row in range(4):
            for half in range(2):
                piece = yb[4 * row + t : 4 * row + t + 1, 768 * half : 768 * half + 768]
                out[row * 4 + holder, 2 * t + half : 2 * t + half + 1, 0:768] = piece
    tails = [recv[8 * k : 8 * k + 8, 256:384] for k in range(8)]
    coeffs = far_matrices(recv[:, 256:384], fs[0:320, :], fot[:, 0:320], wh, wl, True)
    sums = functools.reduce(jnp.add, tails)
    for k in range(16):
        out[k, :, 768:896] = jnp.where(iota((8, 128), 1) < 64, coeffs[8 * k : 8 * k + 8], sums)


def send_residual(zone, values, basis, out, scalars):
    lanes = iota((64, 128), 1)
    columns = jnp.zeros((64, 128), F32)
    for r in range(8):
        column = jnp.sum(basis[r] * values[r : r + 1, :], axis=1, keepdims=True)
        columns = jnp.where(lanes == r, column, columns)
    columns = jnp.concatenate([columns, jnp.zeros((64, 128), F32)], axis=0)
    tail = with_scalars(columns.T[0:8, :], scalars)
    for k in range(16):
        out[k, :, 768:896] = tail

    def rows(d):
        for t in range(4):
            r = 2 * d - 1 + t
            if 0 <= r < 8:
                for half in range(2):
                    piece = values[r : r + 1, 768 * half : 768 * half + 768]
                    out[4 * zone + d, 2 * t + half : 2 * t + half + 1, 0:768] = piece

    for d in range(4):
        rows(d)

    @pl.when(zone > 0)
    def _():
        rows(-1)

    @pl.when(zone < 3)
    def _():
        rows(4)


def start_obs(zone, data, basis, out):
    send_residual(zone[0], data, basis, out, (total(data[...] * data[...]),))


def gather_projected(zone, recv, basis, p):
    tail = functools.reduce(jnp.add, [recv[k, :, 768:896] for k in range(16)])
    columns = jnp.where(iota((8, 128), 1) < 64, tail, 0.0).T
    for r in range(8):
        far = jnp.sum(basis[r] * columns[0:64, r : r + 1], axis=0, keepdims=True)
        for half in range(2):
            value = far[:, 768 * half : 768 * half + 768]
            for t in range(4):
                if (r + 1 - t) % 2 == 0:
                    d = (r + 1 - t) // 2
                    piece = recv[jnp.clip(4 * zone + d, 0, 15), 2 * t + half : 2 * t + half + 1, 0:768]
                    if d == -1:
                        piece = jnp.where(zone > 0, piece, 0.0)
                    if d == 4:
                        piece = jnp.where(zone < 3, piece, 0.0)
                    value = value + piece
            p[r : r + 1, 768 * half : 768 * half + 768] = value
    return tail


def first_obs(zone, recv, data, basis, p, gammas, out):
    z = zone[0]
    gammas[...] = gather_projected(z, recv, basis, p)
    pv, dv = p[...], data[...]
    send_residual(z, p, basis, out, (total(pv * pv), total(dv * pv)))


def second_obs(zone, recv, data, p0, gamma0, sums1, basis, p, r, gammas, out):
    z = zone[0]
    tail = gather_projected(z, recv, basis, p)
    gammas[...] = tail
    g0 = lane_scalar(gamma0[...], 0)
    pv = p[...] + (lane_scalar(tail, 0) / g0) * p0[...]
    rv = data[...] - (g0 / lane_scalar(sums1[...], 0)) * p0[...]
    p[...] = pv
    r[...] = rv
    send_residual(z, p, basis, out, (total(pv * pv), total(rv * pv)))


def gather_normal(recv, basis, q):
    block = functools.reduce(jnp.add, [recv[k] for k in range(8)])
    tail = block[:, 256:384]
    columns = jnp.where(iota((8, 128), 1) < 64, tail, 0.0).T
    for r in range(8):
        far = jnp.sum(basis[r] * columns[0:64, r : r + 1], axis=0, keepdims=True)
        q[r : r + 1, :] = block[r : r + 1, 0:256] + far
    return tail


def send_direction(x, basis, out):
    lanes = iota((64, 128), 1)
    columns = jnp.zeros((64, 128), F32)
    for r in range(8):
        column = jnp.sum(basis[r] * x[r : r + 1], axis=1, keepdims=True)
        columns = jnp.where(lanes == r, column, columns)
    columns = jnp.concatenate([columns, jnp.zeros((64, 128), F32)], axis=0)
    tail = with_scalars(columns.T[0:8, :], (total(x * x),))
    for k in range(8):
        out[k, :, 0:256] = x
        out[k, :, 256:384] = tail


def first_src(recv, basis, n0, sums, out):
    sums[...] = gather_normal(recv, basis, n0)
    send_direction(n0[...], basis, out)


def second_src(recv, basis, n0, gamma0, n1, sums, out):
    tail = gather_normal(recv, basis, n1)
    sums[...] = tail
    x = n0[...] - (lane_scalar(gamma0[...], 0) / lane_scalar(tail, 0)) * n1[...]
    n1[...] = x
    send_direction(x, basis, out)


def last_src(recv, basis, n0, n1, gamma0, gamma1, sums0, sums1, r1, p1, found, residual, normal, misfit):
    tail = gather_normal(recv, basis, normal)
    g0, g1 = lane_scalar(gamma0[...], 0), lane_scalar(gamma1[...], 0)
    s1 = sums1[...]
    curve0, cross0 = lane_scalar(s1, 0), lane_scalar(s1, 1)
    curve1, cross1 = lane_scalar(tail, 0), lane_scalar(tail, 1)
    step0, step1 = g0 / curve0, g1 / curve1
    normal[...] = n1[...] - step1 * normal[...]
    found[...] = step0 * n0[...] + step1 * (n1[...] + (g1 / g0) * n0[...])
    residual[...] = r1[...] - step1 * p1[...]
    m0 = lane_scalar(sums0[...], 0)
    m1 = m0 - 2.0 * step0 * cross0 + step0 * step0 * curve0
    m2 = m1 - 2.0 * step1 * cross1 + step1 * step1 * curve1
    lanes = iota((8, 128), 1)
    misfit[...] = jnp.where(lanes == 0, m0, jnp.where(lanes == 1, m1, m2))


VM = pl.BlockSpec(memory_space=pltpu.VMEM)
SM = pl.BlockSpec(memory_space=pltpu.SMEM)


def shape(*dims, dtype=F32):
    return jax.ShapeDtypeStruct(dims, dtype)


def call(kernel, outs, ins, scratch=(), out_specs=None, scalars=0, limit=16):
    return pl.pallas_call(
        kernel,
        out_shape=outs,
        in_specs=[SM] * scalars + [VM] * (len(ins) - scalars),
        out_specs=out_specs or [VM] * len(outs),
        scratch_shapes=list(scratch),
        compiler_params=pltpu.CompilerParams(vmem_limit_bytes=limit * MIB),
    )(*ins)


def exchange(value, axes):
    return lax.all_to_all(value, axes, split_axis=0, concat_axis=0, tiled=True)


def shards(data, obs_points, src_points, obs_basis, src_basis, couplings, near_pairs, far_pairs):
    index = lax.axis_index(SRC).astype(jnp.int32)
    column = index.reshape(1)
    zone = (index % 4).reshape(1)
    near = near_pairs.reshape(-1)
    near_row = jnp.pad(near_pairs.reshape(1, -1), ((0, 0), (0, 56)), constant_values=-1)
    far_row = jnp.pad(far_pairs.reshape(1, -1), ((0, 0), (0, 64)), constant_values=-1)
    obs_message = shape(16, 8, 896)
    src_message = shape(8, 8, 384)
    row = shape(8, 128)

    (message,) = call(start_obs, [obs_message], [zone, data, obs_basis], scalars=1)
    received = exchange(message, SRC)

    def bf(*dims):
        return shape(*dims, dtype=BF16)

    kh, kl, pq, count, oo, oot, ost, os, fo, fot, fs, fst = call(
        setup_near,
        [
            bf(PAIRS, 256, 256), bf(PAIRS, 256, 256), shape(6, PAIRS, 256), shape(1, dtype=jnp.int32),
            bf(128, 16), bf(16, 128), bf(64, 128), bf(128, 64), bf(384, 128), bf(128, 384), bf(384, 64), bf(64, 384),
        ],
        [near, column, near_row, far_row, obs_points, src_points],
        scalars=2,
        out_specs=[VM] * 3 + [SM] + [VM] * 8,
        limit=28,
    )
    tile = pl.BlockSpec((1, 256, 256), lambda t: (t, 0, 0))
    wh, wl = pl.pallas_call(
        setup_far,
        grid=(20,),
        out_shape=[bf(20, 256, 256), bf(20, 256, 256)],
        in_specs=[pl.BlockSpec((16, 64, 64), lambda t: (t, 0, 0))],
        out_specs=[tile, tile],
        compiler_params=pltpu.CompilerParams(vmem_limit_bytes=16 * MIB),
    )(couplings.reshape(320, 64, 64))

    def adjoint(message):
        (out,) = call(
            adjoint_block,
            [shape(64, 384)],
            [count, column, message, kh, kl, pq, oo, ost, fo, fst, wh, wl],
            scalars=2,
            scratch=[
                pltpu.VMEM((16, 1536), F32), pltpu.VMEM((80, 1536), F32), pltpu.VMEM((2, 80 * ROWS, 128), F32),
                pltpu.VMEM((2, 80 * ROWS, 128), F32), pltpu.VMEM((128, 256), F32),
            ],
            limit=36,
        )
        return exchange(out.reshape(8, 8, 384), OBS)

    def forward(message):
        (out,) = call(
            forward_block,
            [obs_message],
            [count, column, exchange(message, OBS).reshape(64, 384), kh, kl, pq, os, oot, fs, fot, wh, wl],
            scalars=2,
            scratch=[
                pltpu.VMEM((80, 256), F32), pltpu.VMEM((2, 80 * ROWS, 128), F32), pltpu.VMEM((2, 80 * ROWS, 128), F32),
                pltpu.VMEM((128, 1536), F32), pltpu.VMEM((16, 1536), F32),
            ],
            limit=36,
        )
        return exchange(out, SRC)

    plane, line = shape(8, 1536), shape(8, 256)
    n0, sums0, message = call(first_src, [line, row, src_message], [adjoint(received), src_basis])
    p0, gamma0, message = call(
        first_obs, [plane, row, obs_message], [zone, forward(message), data, obs_basis], scalars=1
    )
    n1, sums1, message = call(
        second_src, [line, row, src_message], [adjoint(exchange(message, SRC)), src_basis, n0, gamma0]
    )
    p1, r1, gamma1, message = call(
        second_obs,
        [plane, plane, row, obs_message],
        [zone, forward(message), data, p0, gamma0, sums1, obs_basis],
        scalars=1,
    )
    found, residual, normal, misfit = call(
        last_src,
        [line, plane, line, row],
        [adjoint(exchange(message, SRC)), src_basis, n0, n1, gamma0, gamma1, sums0, sums1, r1, p1],
    )
    return found, residual, normal, misfit[0, 0:3]


def solution(mesh):
    finer = Mesh(mesh.devices.reshape(4, 2, 4, 4), ("obs_0", "obs_1", "src_0", "src_1"))
    return jax.shard_map(
        shards,
        mesh=finer,
        in_specs=(
            P(OBS_SRC, None),
            P(OBS, None, None),
            P(SRC, None, None),
            P(OBS_SRC, None, None),
            P(SRC_OBS, None, None),
            P(OBS, SRC, None, None, None),
            P(OBS, SRC, None),
            P(OBS, SRC, None),
        ),
        out_specs=(P(SRC_OBS, None), P(OBS_SRC, None), P(SRC_OBS, None), P()),
        check_vma=False,
    )
```

time: 808 us -> 234 us (0.29); the launches traced: 794 us -> 232 us
  other arithmetic: 196 us -> 0 us
  local copies, waits for them, and re-layouts: 187 us -> 46.8 us
  starting transfers between devices: 94.6 us -> 8.41 us
  matrix products: 78.4 us -> 0 us
  Pallas kernels: 0 us -> 72.4 us
  blocking collectives: 160 us -> 103 us
  waiting for transfers between devices: 51.3 us -> 0.01 us
  between operations: 22.9 us -> 0.88 us
    gather x83 -> x0, local copies, waits for them, and re-layouts: 135 us -> none  [the longest x50 83.5 us: one_group(): tensor = tensor_parts(obs_pts[obs_take], src_pts[src_take])]
    psum x12 -> x0, blocking collectives: 106 us -> none  [over_axes(): value = lax.psum(value, axis)]
    reduce_sum x37 -> x0, other arithmetic: 102 us -> none  [the longest x15 53.6 us: one_group(): return running.at[src_take].add(jnp.sum(weighted, axis=1))]
    all_to_all x13 -> x1, starting transfers between devices: 94.6 us -> 8.41 us  [exchange(): return lax.all_to_all(value, axes, split_axis=0, concat_axis=0, tiled=True)]
    all_to_all x1 -> x9, blocking collectives: 23.1 us -> 103 us  [exchange(): return lax.all_to_all(value, axes, split_axis=0, concat_axis=0, tiled=True)]
    dot_general x15 -> x0, matrix products: 78.4 us -> none  [the longest x3 34.6 us: far_adjoint(): jnp.einsum('ckl,ck->cl', coupling, chosen_coeffs, precision=exact)]
    pallas_call x0 -> x13, Pallas kernels: none -> 72.4 us  [the longest x12 69.5 us: call(): pl.pallas_call(kernel, out_shape=outs, in_specs=[SM] * scalars + [VM] * (...]
    scatter-add x30 -> x0, other arithmetic: 62.5 us -> none  [the longest x15 42.2 us: one_group(): return running.at[src_take].add(jnp.sum(weighted, axis=1))]
  transfers between devices with their start and end apart: 14 -> 1, of which waited for: 8 -> 0; matrix products, arithmetic and copies ran while one was open for 37% -> 8% of each run, Pallas kernels for 0% -> 9%
where the time goes in v1:
time: 234 us; the launch traced here: 232 us
  blocking collectives  103 us (44%)
  Pallas kernels  72.4 us (31%)
  local copies, waits for them, and re-layouts  46.8 us (20%)
  starting transfers between devices  8.41 us (4%)
    all_to_all x9, blocking collectives, exchange(): return lax.all_to_all(value, axes, split_axis=0, concat_axis=0, tiled=True)  103 us
    pallas_call x12, Pallas kernels, call(): pl.pallas_call(kernel, out_shape=outs, in_specs=[SM] * scalars + [VM] * (...  69.5 us
    unnamed x71, local copies, waits for them, and re-layouts  43.9 us
    all_to_all x1, starting transfers between devices, exchange(): return lax.all_to_all(value, axes, split_axis=0, concat_axis=0, tiled=True)  8.41 us
  transfers between devices with their start and end apart: 1, of which 0 were waited for; matrix products, arithmetic and copies ran while one was open for 8% of the time, Pallas kernels for 9%

profile of v1, /device:TPU:1, one launch (start us, length us, event | category | flops | bytes accessed | tf_op | source)
XLA Modules:
  0.0 231.8 jit_solution(12888789179242249695)
XLA Ops:
  0.7 1.9 copy-done.7
  3.3 1.2 shard_map.112
  4.5 8.4 %all-to-all-start = ((f32[16,8,896]{2,1,0:T(8,128)}), f32[16,8,896]{2,1,0:T(8,128)S(1)}, u32[]{:S(2)}, u32[]{:S(2)}) async-start(f32[16,8,896]{2,1,0:T(8,128)} %shard_map.112), calls=%async_computation | async-start | bytes 917504 | tf_op jit(solution)/shard_map/all_to_all | solution.py:426
  12.9 1.2 pad.8.near_row
  14.1 1.2 pad.9.far_row
  15.3 1.8 copy.13.src
  17.1 2.1 copy.12.obs
  19.2 12.3 %copy.14 = f32[1,1,320,64,64]{4,3,2,1,0:T(8,128)} copy(f32[1,1,320,64,64]{2,4,3,1,0:T(8,128)} %param.13) | data formatting | bytes 10485760 | tf_op args[5]
  31.5 4.0 %copy-done.6 = f32[1,1,320,64,64]{4,3,2,1,0:T(8,128)S(1)} copy-done((f32[1,1,320,64,64]{4,3,2,1,0:T(8,128)S(1)}, f32[1,1,320,64,64]{4,3,2,1,0:T(8,128)}, u32[]{:S(2)}) %copy-start.6) | copy-done | bytes 5242904
  35.5 2.9 %shard_map.113 = (bf16[20,256,256]{2,1,0:T(8,128)(2,1)S(1)}, bf16[20,256,256]{2,1,0:T(8,128)(2,1)S(1)}) custom-call(f32[320,64,64]{2,1,0:T(8,128)S(1)} %bitcast.13), custom_call_target="tpu_custom_call" | custom-call | tf_op jit(solution)/shard_map/pallas_call | solution.py:458
  38.4 1.5 copy-done.3
  40.0 17.0 %shard_map.111 = (bf16[72,256,256]{2,1,0:T(8,128)(2,1)S(1)}, bf16[72,256,256]{2,1,0:T(8,128)(2,1)S(1)}, f32[6,72,256]{2,1,0:T(8,128)S(1)}, s32[1]{0:T(128)}, bf1...) custom-call(s32[72]{0:T(128)S(1)} %bitcast.20, ...), custom_call_target="tpu_custom_call" | custom-call | tf_op jit(solution)/shard_map/pallas_call | solution.py:415
  57.0 3.6 %copy-done = bf16[72,256,256]{2,1,0:T(8,128)(2,1)} copy-done((bf16[72,256,256]{2,1,0:T(8,128)(2,1)}, bf16[72,256,256]{2,1,0:T(8,128)(2,1)S(1)}, u32[]{:S(2)}) %copy-start) | copy-done | bytes 9437208
  60.6 3.6 %copy-done.2 = bf16[72,256,256]{2,1,0:T(8,128)(2,1)} copy-done((bf16[72,256,256]{2,1,0:T(8,128)(2,1)}, bf16[72,256,256]{2,1,0:T(8,128)(2,1)S(1)}, u32[]{:S(2)}) %copy-start.2) | copy-done | bytes 9437208
  68.6 3.7 %copy-done.1 = bf16[72,256,256]{2,1,0:T(8,128)(2,1)S(1)} copy-done((bf16[72,256,256]{2,1,0:T(8,128)(2,1)S(1)}, bf16[72,256,256]{2,1,0:T(8,128)(2,1)}, u32[]{:S(2)}) %copy-start.1) | copy-done | bytes 9437208
  72.3 1.7 copy-done.4
  76.5 9.0 %shard_map.114 = f32[64,384]{1,0:T(8,128)S(1)} custom-call(s32[1]{0:T(128)} %get-tuple-element.35.count, s32[1]{0:T(128)} %bitcast.1.column, f32[16,8,896]{2,1,0:T(8,128)S(1)} %all-to-all-done.recv, bf16[72,256,256]{2,1,0:T(8,128)(2,1)S(1)} %copy-done.1, bf16[72,256,256]{2,1,0:T(8,128)(2,1)} %copy-done.2, f32[6,72,256]{2,1,0:T(8,128)S(1)} %get-tuple-element.38.pq, ...), custom_call_target="tpu_custom_call" | custom-call | tf_op jit(solution)/shard_map/pallas_call | solution.py:415
  85.5 9.0 %all_to_all.50.recv = f32[8,8,384]{2,1,0:T(8,128)S(1)} all-to-all(f32[8,8,384]{2,1,0:T(8,128)S(1)} %bitcast.17), channel_id=1, replica_groups=mesh['obs_0'=4,'obs_1'=2,'src_0'=4,'src_1'=4] {'obs_0','obs_1'}, dimensions={0} | all-to-all | bytes 196608 | tf_op jit(solution)/shard_map/all_to_all | solution.py:426
  94.9 8.2 %all_to_all.51 = f32[8,8,384]{2,1,0:T(8,128)S(1)} all-to-all(f32[8,8,384]{2,1,0:T(8,128)S(1)} %get-tuple-element.45), channel_id=1, replica_groups=mesh['obs_0'=4,'obs_1'=2,'src_0'=4,'src_1'=4] {'obs_0','obs_1'}, dimensions={0} | all-to-all | bytes 196608 | tf_op jit(solution)/shard_map/all_to_all | solution.py:426
  103.2 10.8 %shard_map.116 = f32[16,8,896]{2,1,0:T(8,128)S(1)} custom-call(s32[1]{0:T(128)} %get-tuple-element.35.count, s32[1]{0:T(128)} %bitcast.1.column, f32[64,384]{1,0:T(8,128)S(1)} %bitcast.16, bf16[72,256,256]{2,1,0:T(8,128)(2,1)S(1)} %copy-done.1, bf16[72,256,256]{2,1,0:T(8,128)(2,1)} %copy-done.2, f32[6,72,256]{2,1,0:T(8,128)S(1)} %get-tuple-element.38.pq, ...), custom_call_target="tpu_custom_call" | custom-call | tf_op jit(solution)/shard_map/pallas_call | solution.py:415
  114.0 19.4 %all_to_all.52.recv = f32[16,8,896]{2,1,0:T(8,128)S(1)} all-to-all(f32[16,8,896]{2,1,0:T(8,128)S(1)} %shard_map.116), channel_id=1, replica_groups=mesh['obs_0'=4,'obs_1'=2,'src_0'=4,'src_1'=4] {'src_0','src_1'}, dimensions={0} | all-to-all | bytes 917504 | tf_op jit(solution)/shard_map/all_to_all | solution.py:426
  133.4 0.9 shard_map.117
  134.4 13.0 %all_to_all.53.recv = f32[16,8,896]{2,1,0:T(8,128)S(1)} all-to-all(f32[16,8,896]{2,1,0:T(8,128)S(1)} %get-tuple-element.50), channel_id=1, replica_groups=mesh['obs_0'=4,'obs_1'=2,'src_0'=4,'src_1'=4] {'src_0','src_1'}, dimensions={0} | all-to-all | bytes 917504 | tf_op jit(solution)/shard_map/all_to_all | solution.py:426
  147.4 8.7 %shard_map.118 = f32[64,384]{1,0:T(8,128)S(1)} custom-call(s32[1]{0:T(128)} %get-tuple-element.35.count, s32[1]{0:T(128)} %bitcast.1.column, f32[16,8,896]{2,1,0:T(8,128)S(1)} %all_to_all.53.recv, bf16[72,256,256]{2,1,0:T(8,128)(2,1)S(1)} %copy-done.1, bf16[72,256,256]{2,1,0:T(8,128)(2,1)} %copy-done.2, f32[6,72,256]{2,1,0:T(8,128)S(1)} %get-tuple-element.38.pq, ...), custom_call_target="tpu_custom_call" | custom-call | tf_op jit(solution)/shard_map/pallas_call | solution.py:415
  156.1 10.1 %all_to_all.54.recv = f32[8,8,384]{2,1,0:T(8,128)S(1)} all-to-all(f32[8,8,384]{2,1,0:T(8,128)S(1)} %bitcast.18), channel_id=1, replica_groups=mesh['obs_0'=4,'obs_1'=2,'src_0'=4,'src_1'=4] {'obs_0','obs_1'}, dimensions={0} | all-to-all | bytes 196608 | tf_op jit(solution)/shard_map/all_to_all | solution.py:426
  166.7 8.2 %all_to_all.55 = f32[8,8,384]{2,1,0:T(8,128)S(1)} all-to-all(f32[8,8,384]{2,1,0:T(8,128)S(1)} %get-tuple-element.53), channel_id=1, replica_groups=mesh['obs_0'=4,'obs_1'=2,'src_0'=4,'src_1'=4] {'obs_0','obs_1'}, dimensions={0} | all-to-all | bytes 196608 | tf_op jit(solution)/shard_map/all_to_all | solution.py:426
  174.8 10.5 %shard_map.120 = f32[16,8,896]{2,1,0:T(8,128)S(1)} custom-call(s32[1]{0:T(128)} %get-tuple-element.35.count, s32[1]{0:T(128)} %bitcast.1.column, f32[64,384]{1,0:T(8,128)S(1)} %bitcast.15, bf16[72,256,256]{2,1,0:T(8,128)(2,1)S(1)} %copy-done.1, bf16[72,256,256]{2,1,0:T(8,128)(2,1)} %copy-done.2, f32[6,72,256]{2,1,0:T(8,128)S(1)} %get-tuple-element.38.pq, ...), custom_call_target="tpu_custom_call" | custom-call | tf_op jit(solution)/shard_map/pallas_call | solution.py:415
  185.3 13.2 %all_to_all.56.recv = f32[16,8,896]{2,1,0:T(8,128)S(1)} all-to-all(f32[16,8,896]{2,1,0:T(8,128)S(1)} %shard_map.120), channel_id=1, replica_groups=mesh['obs_0'=4,'obs_1'=2,'src_0'=4,'src_1'=4] {'src_0','src_1'}, dimensions={0} | all-to-all | bytes 917504 | tf_op jit(solution)/shard_map/all_to_all | solution.py:426
  198.6 0.9 shard_map.121
  199.5 12.1 %all_to_all.57.recv = f32[16,8,896]{2,1,0:T(8,128)S(1)} all-to-all(f32[16,8,896]{2,1,0:T(8,128)S(1)} %get-tuple-element.56), channel_id=1, replica_groups=mesh['obs_0'=4,'obs_1'=2,'src_0'=4,'src_1'=4] {'src_0','src_1'}, dimensions={0} | all-to-all | bytes 917504 | tf_op jit(solution)/shard_map/all_to_all | solution.py:426
  211.6 8.7 %shard_map.122 = f32[64,384]{1,0:T(8,128)S(1)} custom-call(s32[1]{0:T(128)} %get-tuple-element.35.count, s32[1]{0:T(128)} %bitcast.1.column, f32[16,8,896]{2,1,0:T(8,128)S(1)} %all_to_all.57.recv, bf16[72,256,256]{2,1,0:T(8,128)(2,1)S(1)} %copy-done.1, bf16[72,256,256]{2,1,0:T(8,128)(2,1)} %copy-done.2, f32[6,72,256]{2,1,0:T(8,128)S(1)} %get-tuple-element.38.pq, ...), custom_call_target="tpu_custom_call" | custom-call | tf_op jit(solution)/shard_map/pallas_call | solution.py:415
  220.3 10.1 %all_to_all.58.recv = f32[8,8,384]{2,1,0:T(8,128)S(1)} all-to-all(f32[8,8,384]{2,1,0:T(8,128)S(1)} %bitcast.14), channel_id=1, replica_groups=mesh['obs_0'=4,'obs_1'=2,'src_0'=4,'src_1'=4] {'obs_0','obs_1'}, dimensions={0} | all-to-all | bytes 196608 | tf_op jit(solution)/shard_map/all_to_all | solution.py:426
  (66 shorter events, 10.0 us)
Async XLA Ops:
  0.6 1.9 copy-start.7
  2.5 0.8 copy-start.15
  4.5 64.1 %all-to-all-start = ((f32[16,8,896]{2,1,0:T(8,128)}), f32[16,8,896]{2,1,0:T(8,128)S(1)}, u32[]{:S(2)}, u32[]{:S(2)}) async-start(f32[16,8,896]{2,1,0:T(8,128)} %shard_map.112), calls=%async_computation | async-start | bytes 917504 | tf_op jit(solution)/shard_map/all_to_all | solution.py:426
  31.5 8.4 %copy-start.31 = (s32[1,384]{1,0:T(1,128)S(1)}, s32[1,384]{1,0:T(1,128)}, u32[]{:S(2)}) copy-start(s32[1,384]{1,0:T(1,128)} %pad.9.far_row) | copy-start | bytes 4612
  31.5 4.0 %copy-start.6 = (f32[1,1,320,64,64]{4,3,2,1,0:T(8,128)S(1)}, f32[1,1,320,64,64]{4,3,2,1,0:T(8,128)}, u32[]{:S(2)}) copy-start(f32[1,1,320,64,64]{4,3,2,1,0:T(8,128)} %copy.14) | copy-start | bytes 15728644
  35.5 4.4 %copy-start.10 = (f32[128,3,256]{2,1,0:T(4,128)S(1)}, f32[128,3,256]{2,1,0:T(4,128)}, u32[]{:S(2)}) copy-start(f32[128,3,256]{2,1,0:T(4,128)} %copy.12.obs) | copy-start | bytes 1179652
  35.5 4.4 %copy-start.11 = (f32[64,3,256]{2,1,0:T(4,128)S(1)}, f32[64,3,256]{2,1,0:T(4,128)}, u32[]{:S(2)}) copy-start(f32[64,3,256]{2,1,0:T(4,128)} %copy.13.src) | copy-start | bytes 589828
  35.5 4.4 %copy-start.32 = (s32[1,1,72]{2,1,0:T(1,128)S(1)}, s32[1,1,72]{2,1,0:T(1,128)}, u32[]{:S(2)}) copy-start(s32[1,1,72]{2,1,0:T(1,128)} %param.14) | copy-start | bytes 868
  35.5 4.5 %copy-start.33 = (s32[1,128]{1,0:T(1,128)S(1)}, s32[1,128]{1,0:T(1,128)}, u32[]{:S(2)}) copy-start(s32[1,128]{1,0:T(1,128)} %pad.8.near_row) | copy-start | bytes 1540
  38.4 1.5 copy-start.3
  57.0 3.6 %copy-start = (bf16[72,256,256]{2,1,0:T(8,128)(2,1)}, bf16[72,256,256]{2,1,0:T(8,128)(2,1)S(1)}, u32[]{:S(2)}) copy-start(bf16[72,256,256]{2,1,0:T(8,128)(2,1)S(1)} %get-tuple-element.36.kh) | copy-start | bytes 28311556
  60.6 3.6 %copy-start.2 = (bf16[72,256,256]{2,1,0:T(8,128)(2,1)}, bf16[72,256,256]{2,1,0:T(8,128)(2,1)S(1)}, u32[]{:S(2)}) copy-start(bf16[72,256,256]{2,1,0:T(8,128)(2,1)S(1)} %get-tuple-element.37.kl) | copy-start | bytes 28311556
  64.2 0.7 copy-start.12
  65.5 0.6 copy-start.20
  66.2 0.6 copy-start.22
  67.4 0.6 copy-start.27
  68.6 3.7 %copy-start.1 = (bf16[72,256,256]{2,1,0:T(8,128)(2,1)S(1)}, bf16[72,256,256]{2,1,0:T(8,128)(2,1)}, u32[]{:S(2)}) copy-start(bf16[72,256,256]{2,1,0:T(8,128)(2,1)} %copy-done) | copy-start | bytes 28311556
  72.3 1.7 copy-start.4
  74.0 0.9 copy-start.13
  74.9 0.8 copy-start.18
  75.7 0.7 copy-start.25
  76.4 18.0 %copy-start.9 = (f32[8,64,256]{2,1,0:T(8,128)S(1)}, f32[8,64,256]{2,1,0:T(8,128)}, u32[]{:S(2)}) copy-start(f32[8,64,256]{2,1,0:T(8,128)} %basis.11) | copy-start | bytes 1572868
  76.4 26.7 %copy-start.5 = (bf16[20,256,256]{2,1,0:T(8,128)(2,1)S(1)}, bf16[20,256,256]{2,1,0:T(8,128)(2,1)}, u32[]{:S(2)}) copy-start(bf16[20,256,256]{2,1,0:T(8,128)(2,1)} %copy-done.3) | copy-start | bytes 7864324
  76.4 26.7 %copy-start.21 = (bf16[128,384]{1,0:T(8,128)(2,1)S(1)}, bf16[128,384]{1,0:T(8,128)(2,1)}, u32[]{:S(2)}) copy-start(bf16[128,384]{1,0:T(8,128)(2,1)} %copy-done.20) | copy-start | bytes 294916
  76.5 26.7 %copy-start.23 = (bf16[384,64]{1,0:T(8,128)(2,1)S(1)}, bf16[384,64]{1,0:T(8,128)(2,1)}, u32[]{:S(2)}) copy-start(bf16[384,64]{1,0:T(8,128)(2,1)} %copy-done.22) | copy-start | bytes 147460
  76.5 26.7 %copy-start.28 = (bf16[128,64]{1,0:T(8,128)(2,1)S(1)}, bf16[128,64]{1,0:T(8,128)(2,1)}, u32[]{:S(2)}) copy-start(bf16[128,64]{1,0:T(8,128)(2,1)} %copy-done.27) | copy-start | bytes 49156
  76.5 26.7 %copy-start.30 = (bf16[16,128]{1,0:T(8,128)(2,1)S(1)}, bf16[16,128]{1,0:T(8,128)(2,1)}, u32[]{:S(2)}) copy-start(bf16[16,128]{1,0:T(8,128)(2,1)} %copy-done.29) | copy-start | bytes 12292
  103.2 30.3 %copy-start.8 = (f32[8,64,1536]{2,1,0:T(8,128)S(1)}, f32[8,64,1536]{2,1,0:T(8,128)}, u32[]{:S(2)}) copy-start(f32[8,64,1536]{2,1,0:T(8,128)} %basis.10) | copy-start | bytes 9437188
  103.2 30.3 %copy-start.16 = (f32[8,1536]{1,0:T(8,128)S(1)}, f32[8,1536]{1,0:T(8,128)}, u32[]{:S(2)}) copy-start(f32[8,1536]{1,0:T(8,128)} %data.5) | copy-start | bytes 147460
  103.2 44.2 %copy-start.14 = (bf16[384,128]{1,0:T(8,128)(2,1)S(1)}, bf16[384,128]{1,0:T(8,128)(2,1)}, u32[]{:S(2)}) copy-start(bf16[384,128]{1,0:T(8,128)(2,1)} %copy-done.12) | copy-start | bytes 294916
  103.2 44.2 %copy-start.19 = (bf16[64,384]{1,0:T(8,128)(2,1)S(1)}, bf16[64,384]{1,0:T(8,128)(2,1)}, u32[]{:S(2)}) copy-start(bf16[64,384]{1,0:T(8,128)(2,1)} %copy-done.17) | copy-start | bytes 147460
  103.2 44.2 %copy-start.26 = (bf16[64,128]{1,0:T(8,128)(2,1)S(1)}, bf16[64,128]{1,0:T(8,128)(2,1)}, u32[]{:S(2)}) copy-start(bf16[64,128]{1,0:T(8,128)(2,1)} %copy-done.24) | copy-start | bytes 49156
  (3 other events, 1.8 us)

commit v2 on v1

--- a/solution.py
+++ b/solution.py
@@ -18,6 +18,8 @@
 PAIRS = 72
 ROWS = 16
 MIB = 1 << 20
+LIMIT0 = 4
+LIMIT = 10
 
 
 def split(value):
@@ -53,10 +55,16 @@
     return block
 
 
-def setup_near(slots, column, near_row, far_row, obs, src, kh, kl, pq, count, oo, oot, ost, os, fo, fot, fs, fst):
+def setup_near(slots, column, near, far, obs, src, kh, kl, pq, count, oo, oot, ost, os, fot, fst, near_row, far_row):
     j = column[0]
+    near_row[...] = jnp.full_like(near_row, -1)
+    near_row[:, 0:72] = near[...]
+    far_row[...] = jnp.full_like(far_row, -1)
+    far_row[:, 0:320] = far[...]
     f = near_row[...]
     live = f >= 0
+    n = jnp.sum(jnp.where(live, 1.0, 0.0)).astype(jnp.int32)
+    count[0] = n
     o = lax.shift_right_arithmetic(f, 6)
     s = jnp.where(live, f & 63, -1)
     oc = jnp.where(live, lax.shift_right_arithmetic(o, 5) * 4 + (o & 31) - (2 * j - 1), -1)
@@ -70,83 +78,98 @@
     live = f >= 0
     o = jnp.where(live, lax.shift_right_arithmetic(f, 6), -1)
     s = jnp.where(live, f & 63, -1)
-    a = (iota((128, 384), 0) == o).astype(F32)
-    fot[...] = a.astype(BF16)
-    fo[...] = a.T.astype(BF16)
-    a = (iota((64, 384), 0) == s).astype(F32)
-    fst[...] = a.astype(BF16)
-    fs[...] = a.T.astype(BF16)
-    pq[...] = jnp.zeros_like(pq)
-
-    n = lax.fori_loop(0, PAIRS, lambda t, c: c + jnp.where(slots[t] >= 0, 1, 0), 0)
-    count[0] = n
-
-    def one(t, carry):
-        name = slots[t]
-        p = obs[lax.shift_right_arithmetic(name, 6)]
-        q = src[name & 63]
-        centre = 0.5 * (jnp.mean(p, axis=1, keepdims=True) + jnp.mean(q, axis=1, keepdims=True))
-        p = p - centre
-        q = q - centre
+    fot[...] = (iota((128, 384), 0) == o).astype(F32).astype(BF16)
+    fst[...] = (iota((64, 384), 0) == s).astype(F32).astype(BF16)
+
+    def eight(g, carry):
+        for b in range(8):
+            t = 8 * g + b
+            name = jnp.maximum(slots[t], 0)
+            for c in range(3):
+                pq[c, pl.ds(t, 1), :] = obs[c, pl.ds(lax.shift_right_logical(name, 6), 1), :]
+                pq[3 + c, pl.ds(t, 1), :] = src[c, pl.ds(name & 63, 1), :]
+        at = pl.ds(pl.multiple_of(8 * g, 8), 8)
+        p, q = [], []
         for c in range(3):
-            pq[c, pl.ds(t, 1), :] = p[c : c + 1]
-            pq[3 + c, pl.ds(t, 1), :] = q[c : c + 1]
-        pt = jnp.concatenate([p, jnp.zeros((5, 256), F32)], axis=0).T
-        for r in range(0, 256, 32):
-            dx = pt[r : r + 32, 0:1] - q[0:1]
-            dy = pt[r : r + 32, 1:2] - q[1:2]
-            dz = pt[r : r + 32, 2:3] - q[2:3]
-            inverse = lax.rsqrt(dx * dx + dy * dy + dz * dz)
-            square = inverse * inverse
-            fifth = square * square * (inverse * (1.0 / 256.0))
-            high, low = split(fifth)
-            kh[t, r : r + 32, :] = high
-            kl[t, r : r + 32, :] = low
-        return carry
-
-    lax.fori_loop(0, n, one, 0)
-
-
-def setup_far(c, wh, wl):
-    for g in range(4):
-        high, low = split(jnp.concatenate([c[4 * g + n] for n in range(4)], axis=1))
-        wh[0, 64 * g : 64 * g + 64, :] = high
-        wl[0, 64 * g : 64 * g + 64, :] = low
-
-
-def far_matrices(x, pick, place, wh, wl, forward):
-    half = jnp.where(iota(x.shape, 1) < 64, x, 0.0)
-    half = half + pltpu.roll(half, 64, 1)
-    high, low = split(jnp.concatenate([half, half], axis=1))
-    lanes = lax.shift_right_logical(iota((16, 256), 1), 6)
-    slot = iota((16, 256), 0)
-    row_group = lanes == lax.shift_right_logical(slot, 2)
-    col_group = lanes == (slot & 3)
-    enter, leave = (col_group, row_group) if forward else (row_group, col_group)
-    multiply = mm_nt if forward else mm
-    picked_high = mm(pick, high)
-    picked_low = mm(pick, low)
-    terms = []
-    for t in range(20):
-        at = slice(16 * t, 16 * t + 16)
-        h = jnp.where(enter, picked_high[at], 0.0).astype(BF16)
-        l = jnp.where(enter, picked_low[at], 0.0).astype(BF16)
-        both = multiply(jnp.concatenate([h, l], axis=0), wh[t])
-        terms.append(jnp.where(leave, both[:16] + both[16:] + multiply(h, wl[t]), 0.0))
-    high, low = split(jnp.concatenate(terms, axis=0))
-    out = mm(place, high) + mm(place, low)
-    out = out[:, :128] + out[:, 128:]
-    return out + pltpu.roll(out, 64, 1)
-
-
-def near_products(n, moments, results, kh, kl, multiply):
+            pc, qc = pq[c, at, :], pq[3 + c, at, :]
+            centre = 0.5 * (jnp.mean(pc, axis=1, keepdims=True) + jnp.mean(qc, axis=1, keepdims=True))
+            pc, qc = pc - centre, qc - centre
+            pq[c, at, :] = pc
+            pq[3 + c, at, :] = qc
+            p.append(pc.T)
+            q.append(qc)
+
+        def one(b):
+            for r in range(0, 256, 32):
+                dx, dy, dz = (p[c][r : r + 32, b : b + 1] - q[c][b : b + 1] for c in range(3))
+                inverse = lax.rsqrt(dx * dx + dy * dy + dz * dz)
+                square = inverse * inverse
+                fifth = square * square * (inverse * (1.0 / 256.0))
+                high, low = split(fifth)
+                kh[8 * g + b, r : r + 32, :] = high
+                kl[8 * g + b, r : r + 32, :] = low
+
+        for b in range(4):
+            one(b)
+
+        @pl.when(n > 8 * g + 4)
+        def _():
+            for b in range(4, 8):
+                one(b)
+
+        return carry
+
+    lax.fori_loop(0, lax.shift_right_logical(n + 7, 3), eight, 0)
+
+
+def far_inputs(x, pick):
+    high, low = split(x.T[0:64, :])
+    return mm(high, pick) + mm(low, pick)
+
+
+def far_outputs(terms, place):
+    high, low = split(terms)
+    return mm_nt(place, high) + mm_nt(place, low)
+
+
+def far_forward(x, pick, place, c, terms):
+    v = far_inputs(x, pick)[:, 0:320]
+    terms[...] = jnp.zeros_like(terms)
+
+    def eight(g, carry):
+        rows = [jnp.sum(c[8 * g + b] * v, axis=0, keepdims=True) for b in range(8)]
+        terms[pl.ds(pl.multiple_of(8 * g, 8), 8), 0:320] = jnp.concatenate(rows, axis=0)
+        return carry
+
+    lax.fori_loop(0, 8, eight, 0)
+    return far_outputs(terms[...], place)
+
+
+def far_adjoint(x, pick, place, c, terms, held):
+    held[...] = far_inputs(x, pick)
+    terms[...] = jnp.zeros_like(terms)
+
+    def eight(g, carry):
+        for b in range(8):
+            carry = carry + c[8 * g + b] * held[pl.ds(8 * g + b, 1), 0:320]
+        return carry
+
+    terms[0:64, 0:320] = lax.fori_loop(0, 8, eight, jnp.zeros((64, 320), F32))
+    return far_outputs(terms[...], place)
+
+
+def near_products(n, moments, results, kh, kl, forward):
     def four(g, carry):
         for b in range(4):
             t = 4 * g + b
             at = pl.ds(pl.multiple_of(t * ROWS, ROWS), ROWS)
             high, low = split(jnp.concatenate([moments[0, at, :], moments[1, at, :]], axis=1))
-            both = multiply(jnp.concatenate([high, low], axis=0), kh[t])
-            both = both[:ROWS] + both[ROWS:] + multiply(high, kl[t])
+            both = jnp.concatenate([high, low], axis=0)
+            if forward:
+                both = (mm_nt(kh[t], both) + mm_nt(kl[t], both)).T
+            else:
+                both = mm(both, kh[t]) + mm(both, kl[t])
+            both = both[:ROWS] + both[ROWS:]
             results[0, at, :] = both[:, :128]
             results[1, at, :] = both[:, 128:]
         return carry
@@ -165,7 +188,9 @@
     return jnp.concatenate([results.at[0][at, :], results.at[1][at, :]], axis=1)
 
 
-def adjoint_block(count, column, recv, kh, kl, pq, oo, ost, fo, fst, wh, wl, out, yb, yp, moments, results, values):
+def adjoint_block(
+    count, column, recv, kh, kl, pq, oo, ost, fot, fst, c, out, yb, yp, moments, results, values, terms, held
+):
     n = count[0]
     j = column[0]
     for t in range(4):
@@ -199,7 +224,7 @@
         return carry
 
     lax.fori_loop(0, groups, enter, 0)
-    near_products(n, moments, results, kh, kl, mm)
+    near_products(n, moments, results, kh, kl, False)
 
     def leave(g, carry):
         at = pl.ds(pl.multiple_of(g * 8, 8), 8)
@@ -214,14 +239,16 @@
     high, low = split(values[...])
     out[:, 0:256] = mm(ost[...], high) + mm(ost[...], low)
     tails = [recv[k, :, 768:896] for k in range(16)]
-    coeffs = far_matrices(jnp.concatenate(tails, axis=0), fo[0:320, :], fst[:, 0:320], wh, wl, False)
+    coeffs = far_adjoint(jnp.concatenate(tails, axis=0), fot[...], fst[...], c, terms, held)
     sums = functools.reduce(jnp.add, tails)
     for k in range(8):
         part = coeffs[8 * k : 8 * k + 8]
         out[8 * k : 8 * k + 8, 256:384] = jnp.where(iota((8, 128), 1) < 64, part, sums)
 
 
-def forward_block(count, column, recv, kh, kl, pq, os, oot, fs, fot, wh, wl, out, xp, moments, results, values, yb):
+def forward_block(
+    count, column, recv, kh, kl, pq, os, oot, fot, fst, c, out, xp, moments, results, values, yb, terms
+):
     n = count[0]
     j = column[0]
     high, low = split(recv[:, 0:256])
@@ -240,7 +267,7 @@
         return carry
 
     lax.fori_loop(0, groups, enter, 0)
-    near_products(n, moments, results, kh, kl, mm_nt)
+    near_products(n, moments, results, kh, kl, True)
 
     def leave(g, carry):
         at = pl.ds(pl.multiple_of(g * 8, 8), 8)
@@ -270,7 +297,7 @@
                 piece = yb[4 * row + t : 4 * row + t + 1, 768 * half : 768 * half + 768]
                 out[row * 4 + holder, 2 * t + half : 2 * t + half + 1, 0:768] = piece
     tails = [recv[8 * k : 8 * k + 8, 256:384] for k in range(8)]
-    coeffs = far_matrices(recv[:, 256:384], fs[0:320, :], fot[:, 0:320], wh, wl, True)
+    coeffs = far_forward(recv[:, 256:384], fst[...], fot[...], c, terms)
     sums = functools.reduce(jnp.add, tails)
     for k in range(16):
         out[k, :, 768:896] = jnp.where(iota((8, 128), 1) < 64, coeffs[8 * k : 8 * k + 8], sums)
@@ -307,7 +334,7 @@
         rows(4)
 
 
-def start_obs(zone, data, basis, out):
+def start_obs(zone, count, data, basis, out):
     send_residual(zone[0], data, basis, out, (total(data[...] * data[...]),))
 
 
@@ -411,7 +438,7 @@
     return jax.ShapeDtypeStruct(dims, dtype)
 
 
-def call(kernel, outs, ins, scratch=(), out_specs=None, scalars=0, limit=16):
+def call(kernel, outs, ins, scratch=(), out_specs=None, scalars=0, limit=4):
     return pl.pallas_call(
         kernel,
         out_shape=outs,
@@ -431,50 +458,44 @@
     column = index.reshape(1)
     zone = (index % 4).reshape(1)
     near = near_pairs.reshape(-1)
-    near_row = jnp.pad(near_pairs.reshape(1, -1), ((0, 0), (0, 56)), constant_values=-1)
-    far_row = jnp.pad(far_pairs.reshape(1, -1), ((0, 0), (0, 64)), constant_values=-1)
     obs_message = shape(16, 8, 896)
     src_message = shape(8, 8, 384)
     row = shape(8, 128)
 
-    (message,) = call(start_obs, [obs_message], [zone, data, obs_basis], scalars=1)
-    received = exchange(message, SRC)
-
     def bf(*dims):
         return shape(*dims, dtype=BF16)
 
-    kh, kl, pq, count, oo, oot, ost, os, fo, fot, fs, fst = call(
+    kh, kl, pq, count, oo, oot, ost, os, fot, fst = call(
         setup_near,
         [
             bf(PAIRS, 256, 256), bf(PAIRS, 256, 256), shape(6, PAIRS, 256), shape(1, dtype=jnp.int32),
-            bf(128, 16), bf(16, 128), bf(64, 128), bf(128, 64), bf(384, 128), bf(128, 384), bf(384, 64), bf(64, 384),
+            bf(128, 16), bf(16, 128), bf(64, 128), bf(128, 64), bf(128, 384), bf(64, 384),
         ],
-        [near, column, near_row, far_row, obs_points, src_points],
+        [
+            near, column, near_pairs.reshape(1, 72), far_pairs.reshape(1, 320),
+            jnp.transpose(obs_points, (1, 0, 2)), jnp.transpose(src_points, (1, 0, 2)),
+        ],
         scalars=2,
-        out_specs=[VM] * 3 + [SM] + [VM] * 8,
-        limit=28,
+        out_specs=[VM] * 3 + [SM] + [VM] * 6,
+        scratch=[pltpu.VMEM((1, 128), jnp.int32), pltpu.VMEM((1, 384), jnp.int32)],
+        limit=LIMIT0,
     )
-    tile = pl.BlockSpec((1, 256, 256), lambda t: (t, 0, 0))
-    wh, wl = pl.pallas_call(
-        setup_far,
-        grid=(20,),
-        out_shape=[bf(20, 256, 256), bf(20, 256, 256)],
-        in_specs=[pl.BlockSpec((16, 64, 64), lambda t: (t, 0, 0))],
-        out_specs=[tile, tile],
-        compiler_params=pltpu.CompilerParams(vmem_limit_bytes=16 * MIB),
-    )(couplings.reshape(320, 64, 64))
+    matrices = jnp.transpose(couplings[0, 0], (1, 2, 0))
+    (message,) = call(start_obs, [obs_message], [zone, count, data, obs_basis], scalars=2)
+    received = exchange(message, SRC)
 
     def adjoint(message):
         (out,) = call(
             adjoint_block,
             [shape(64, 384)],
-            [count, column, message, kh, kl, pq, oo, ost, fo, fst, wh, wl],
+            [count, column, message, kh, kl, pq, oo, ost, fot, fst, matrices],
             scalars=2,
             scratch=[
                 pltpu.VMEM((16, 1536), F32), pltpu.VMEM((80, 1536), F32), pltpu.VMEM((2, 80 * ROWS, 128), F32),
-                pltpu.VMEM((2, 80 * ROWS, 128), F32), pltpu.VMEM((128, 256), F32),
+                pltpu.VMEM((2, 80 * ROWS, 128), F32), pltpu.VMEM((128, 256), F32), pltpu.VMEM((128, 384), F32),
+                pltpu.VMEM((64, 384), F32),
             ],
-            limit=36,
+            limit=LIMIT,
         )
         return exchange(out.reshape(8, 8, 384), OBS)
 
@@ -482,13 +503,13 @@
         (out,) = call(
             forward_block,
             [obs_message],
-            [count, column, exchange(message, OBS).reshape(64, 384), kh, kl, pq, os, oot, fs, fot, wh, wl],
+            [count, column, exchange(message, OBS).reshape(64, 384), kh, kl, pq, os, oot, fot, fst, matrices],
             scalars=2,
             scratch=[
                 pltpu.VMEM((80, 256), F32), pltpu.VMEM((2, 80 * ROWS, 128), F32), pltpu.VMEM((2, 80 * ROWS, 128), F32),
-                pltpu.VMEM((128, 1536), F32), pltpu.VMEM((16, 1536), F32),
+                pltpu.VMEM((128, 1536), F32), pltpu.VMEM((16, 1536), F32), pltpu.VMEM((128, 384), F32),
             ],
-            limit=36,
+            limit=LIMIT,
         )
         return exchange(out, SRC)
 

time: 234 us -> 172 us (0.74)
  local copies, waits for them, and re-layouts: 46.8 us -> 9.25 us
  Pallas kernels: 72.4 us -> 36.6 us
  blocking collectives: 103 us -> 123 us
  starting transfers between devices: 8.41 us -> 0 us
    unnamed x71 -> x24, local copies, waits for them, and re-layouts: 43.9 us -> 8.74 us
    pallas_call x12, Pallas kernels: 69.5 us -> 36.6 us  [call(): pl.pallas_call(kernel, out_shape=outs, in_specs=[SM] * scalars + [VM] * (...]
    all_to_all x9 -> x10, blocking collectives: 103 us -> 123 us  [exchange(): return lax.all_to_all(value, axes, split_axis=0, concat_axis=0, tiled=True)]
    all_to_all x1 -> x0, starting transfers between devices: 8.41 us -> none  [exchange(): return lax.all_to_all(value, axes, split_axis=0, concat_axis=0, tiled=True)]
    pallas_call x1 -> x0, Pallas kernels: 2.91 us -> none  [shards(): pl.pallas_call(setup_far, grid=(20,), out_shape=[bf(20, 256, 256), bf(20,...]
    pad x2 -> x0, local copies, waits for them, and re-layouts: 2.42 us -> none  [the longest x1 1.25 us: shards(): jnp.pad(far_pairs.reshape(1, -1), ((0, 0), (0, 64)), constant_values=-1)]
  transfers between devices with their start and end apart: 1 -> 0, of which waited for: 0 -> 0; matrix products, arithmetic and copies ran while one was open for 8% -> 0% of each run, Pallas kernels for 9% -> 0%
where the time goes in v2:
time: 172 us; the launch traced here: 170 us
  blocking collectives  123 us (72%)
  Pallas kernels  36.6 us (21%)
  local copies, waits for them, and re-layouts  9.25 us (5%)
    all_to_all x10, blocking collectives, exchange(): return lax.all_to_all(value, axes, split_axis=0, concat_axis=0, tiled=True)  123 us
    pallas_call x12, Pallas kernels, call(): pl.pallas_call(kernel, out_shape=outs, in_specs=[SM] * scalars + [VM] * (...  36.6 us
    unnamed x24, local copies, waits for them, and re-layouts  8.74 us

profile of v2, /device:TPU:1, one launch (start us, length us, event | category | flops | bytes accessed | tf_op | source)
XLA Modules:
  0.0 169.6 jit_solution(6103458516589755483)
XLA Ops:
  0.7 1.0 copy-done.6
  1.6 0.9 copy-done.7
  2.6 0.7 copy-done.8
  3.2 0.7 copy-done.9
  3.9 7.4 %shard_map.111 = (bf16[72,256,256]{2,1,0:T(8,128)(2,1)S(1)}, bf16[72,256,256]{2,1,0:T(8,128)(2,1)S(1)}, f32[6,72,256]{2,1,0:T(8,128)S(1)}, s32[1]{0:T(128)}, bf1...) custom-call(s32[72]{0:T(128)S(1)} %bitcast.31, ...), custom_call_target="tpu_custom_call" | custom-call | tf_op jit(solution)/shard_map/pallas_call | solution.py:442
  11.3 0.0 copy-start.1
  11.3 1.9 %copy-done.1 = f32[8,64,1536]{2,1,0:T(8,128)S(1)} copy-done((f32[8,64,1536]{2,1,0:T(8,128)S(1)}, f32[8,64,1536]{2,1,0:T(8,128)}, u32[]{:S(2)}) %copy-start.1) | copy-done | bytes 3145752
  13.2 0.8 copy-done.4
  14.0 1.1 shard_map.112
  15.1 19.0 %all_to_all.50.recv = f32[16,8,896]{2,1,0:T(8,128)S(1)} all-to-all(f32[16,8,896]{2,1,0:T(8,128)S(1)} %shard_map.112), channel_id=1, replica_groups=mesh['obs_0'=4,'obs_1'=2,'src_0'=4,'src_1'=4] {'src_0','src_1'}, dimensions={0} | all-to-all | bytes 917504 | tf_op jit(solution)/shard_map/all_to_all | solution.py:453
  34.1 2.8 %copy-done = f32[1,1,320,64,64]{2,4,3,1,0:T(8,128)S(1)} copy-done((f32[1,1,320,64,64]{2,4,3,1,0:T(8,128)S(1)}, f32[1,1,320,64,64]{2,4,3,1,0:T(8,128)}, u32[]{:S(2)}) %copy-start) | copy-done | bytes 5242904
  36.9 4.4 %shard_map.113 = f32[64,384]{1,0:T(8,128)S(1)} custom-call(s32[1]{0:T(128)} %get-tuple-element.31.count, s32[1]{0:T(128)} %bitcast.1.column, f32[16,8,896]{2,1,0:T(8,128)S(1)} %all_to_all.50.recv, bf16[72,256,256]{2,1,0:T(8,128)(2,1)S(1)} %get-tuple-element.32.kh, bf16[72,256,256]{2,1,0:T(8,128)(2,1)S(1)} %get-tuple-element.33.kl, ...), custom_call_target="tpu_custom_call" | custom-call | tf_op jit(solution)/shard_map/pallas_call | solution.py:442
  41.2 12.5 %all_to_all.51.recv = f32[8,8,384]{2,1,0:T(8,128)S(1)} all-to-all(f32[8,8,384]{2,1,0:T(8,128)S(1)} %bitcast.27), channel_id=1, replica_groups=mesh['obs_0'=4,'obs_1'=2,'src_0'=4,'src_1'=4] {'obs_0','obs_1'}, dimensions={0} | all-to-all | bytes 196608 | tf_op jit(solution)/shard_map/all_to_all | solution.py:453
  53.8 0.5 shard_map.114
  54.2 8.2 %all_to_all.52 = f32[8,8,384]{2,1,0:T(8,128)S(1)} all-to-all(f32[8,8,384]{2,1,0:T(8,128)S(1)} %get-tuple-element.39), channel_id=1, replica_groups=mesh['obs_0'=4,'obs_1'=2,'src_0'=4,'src_1'=4] {'obs_0','obs_1'}, dimensions={0} | all-to-all | bytes 196608 | tf_op jit(solution)/shard_map/all_to_all | solution.py:453
  62.4 0.0 copy-start.5
  62.4 5.8 %shard_map.115 = f32[16,8,896]{2,1,0:T(8,128)S(1)} custom-call(s32[1]{0:T(128)} %get-tuple-element.31.count, s32[1]{0:T(128)} %bitcast.1.column, f32[64,384]{1,0:T(8,128)S(1)} %bitcast.26, bf16[72,256,256]{2,1,0:T(8,128)(2,1)S(1)} %get-tuple-element.32.kh, bf16[72,256,256]{2,1,0:T(8,128)(2,1)S(1)} %get-tuple-element.33.kl, ...), custom_call_target="tpu_custom_call" | custom-call | tf_op jit(solution)/shard_map/pallas_call | solution.py:442
  68.2 13.9 %all_to_all.53.recv = f32[16,8,896]{2,1,0:T(8,128)S(1)} all-to-all(f32[16,8,896]{2,1,0:T(8,128)S(1)} %shard_map.115), channel_id=1, replica_groups=mesh['obs_0'=4,'obs_1'=2,'src_0'=4,'src_1'=4] {'src_0','src_1'}, dimensions={0} | all-to-all | bytes 917504 | tf_op jit(solution)/shard_map/all_to_all | solution.py:453
  82.1 1.0 shard_map.116
  83.1 13.0 %all_to_all.54.recv = f32[16,8,896]{2,1,0:T(8,128)S(1)} all-to-all(f32[16,8,896]{2,1,0:T(8,128)S(1)} %get-tuple-element.42), channel_id=1, replica_groups=mesh['obs_0'=4,'obs_1'=2,'src_0'=4,'src_1'=4] {'src_0','src_1'}, dimensions={0} | all-to-all | bytes 917504 | tf_op jit(solution)/shard_map/all_to_all | solution.py:453
  96.1 4.2 %shard_map.117 = f32[64,384]{1,0:T(8,128)S(1)} custom-call(s32[1]{0:T(128)} %get-tuple-element.31.count, s32[1]{0:T(128)} %bitcast.1.column, f32[16,8,896]{2,1,0:T(8,128)S(1)} %all_to_all.54.recv, bf16[72,256,256]{2,1,0:T(8,128)(2,1)S(1)} %get-tuple-element.32.kh, bf16[72,256,256]{2,1,0:T(8,128)(2,1)S(1)} %get-tuple-element.33.kl, ...), custom_call_target="tpu_custom_call" | custom-call | tf_op jit(solution)/shard_map/pallas_call | solution.py:442
  100.4 10.8 %all_to_all.55.recv = f32[8,8,384]{2,1,0:T(8,128)S(1)} all-to-all(f32[8,8,384]{2,1,0:T(8,128)S(1)} %bitcast.28), channel_id=1, replica_groups=mesh['obs_0'=4,'obs_1'=2,'src_0'=4,'src_1'=4] {'obs_0','obs_1'}, dimensions={0} | all-to-all | bytes 196608 | tf_op jit(solution)/shard_map/all_to_all | solution.py:453
  111.1 0.5 shard_map.118
  111.6 8.2 %all_to_all.56 = f32[8,8,384]{2,1,0:T(8,128)S(1)} all-to-all(f32[8,8,384]{2,1,0:T(8,128)S(1)} %get-tuple-element.45), channel_id=1, replica_groups=mesh['obs_0'=4,'obs_1'=2,'src_0'=4,'src_1'=4] {'obs_0','obs_1'}, dimensions={0} | all-to-all | bytes 196608 | tf_op jit(solution)/shard_map/all_to_all | solution.py:453
  119.8 5.7 %shard_map.119 = f32[16,8,896]{2,1,0:T(8,128)S(1)} custom-call(s32[1]{0:T(128)} %get-tuple-element.31.count, s32[1]{0:T(128)} %bitcast.1.column, f32[64,384]{1,0:T(8,128)S(1)} %bitcast.25, bf16[72,256,256]{2,1,0:T(8,128)(2,1)S(1)} %get-tuple-element.32.kh, bf16[72,256,256]{2,1,0:T(8,128)(2,1)S(1)} %get-tuple-element.33.kl, ...), custom_call_target="tpu_custom_call" | custom-call | tf_op jit(solution)/shard_map/pallas_call | solution.py:442
  125.4 13.7 %all_to_all.57.recv = f32[16,8,896]{2,1,0:T(8,128)S(1)} all-to-all(f32[16,8,896]{2,1,0:T(8,128)S(1)} %shard_map.119), channel_id=1, replica_groups=mesh['obs_0'=4,'obs_1'=2,'src_0'=4,'src_1'=4] {'src_0','src_1'}, dimensions={0} | all-to-all | bytes 917504 | tf_op jit(solution)/shard_map/all_to_all | solution.py:453
  139.2 1.0 shard_map.120
  140.2 13.0 %all_to_all.58.recv = f32[16,8,896]{2,1,0:T(8,128)S(1)} all-to-all(f32[16,8,896]{2,1,0:T(8,128)S(1)} %get-tuple-element.48), channel_id=1, replica_groups=mesh['obs_0'=4,'obs_1'=2,'src_0'=4,'src_1'=4] {'src_0','src_1'}, dimensions={0} | all-to-all | bytes 917504 | tf_op jit(solution)/shard_map/all_to_all | solution.py:453
  153.2 4.2 %shard_map.121 = f32[64,384]{1,0:T(8,128)S(1)} custom-call(s32[1]{0:T(128)} %get-tuple-element.31.count, s32[1]{0:T(128)} %bitcast.1.column, f32[16,8,896]{2,1,0:T(8,128)S(1)} %all_to_all.58.recv, bf16[72,256,256]{2,1,0:T(8,128)(2,1)S(1)} %get-tuple-element.32.kh, bf16[72,256,256]{2,1,0:T(8,128)(2,1)S(1)} %get-tuple-element.33.kl, ...), custom_call_target="tpu_custom_call" | custom-call | tf_op jit(solution)/shard_map/pallas_call | solution.py:442
  157.4 10.8 %all_to_all.59.recv = f32[8,8,384]{2,1,0:T(8,128)S(1)} all-to-all(f32[8,8,384]{2,1,0:T(8,128)S(1)} %bitcast.24), channel_id=1, replica_groups=mesh['obs_0'=4,'obs_1'=2,'src_0'=4,'src_1'=4] {'obs_0','obs_1'}, dimensions={0} | all-to-all | bytes 196608 | tf_op jit(solution)/shard_map/all_to_all | solution.py:453
  168.2 0.9 shard_map.122
  169.1 0.5 slice_bitcast_fusion
  (16 shorter events, 0.0 us)
Async XLA Ops:
  0.6 1.0 copy-start.6
  1.6 0.9 copy-start.7
  2.6 0.7 copy-start.8
  3.2 0.7 copy-start.9
  3.9 58.5 %slice-start = ((s8[6291456]{0:T(1024)(128)(4,1)}), s8[2097152]{0:T(1024)(128)(4,1)S(1)}, s32[]{:S(2)}) async-start(s8[6291456]{0:T(1024)(128)(4,1)} %bitcast.18), calls=%async_computation.10 | async-start | bytes 4194304
  11.3 1.9 %copy-start.1 = (f32[8,64,1536]{2,1,0:T(8,128)S(1)}, f32[8,64,1536]{2,1,0:T(8,128)}, u32[]{:S(2)}) copy-start(f32[8,64,1536]{2,1,0:T(8,128)} %basis.10) | copy-start | bytes 9437188
  13.2 0.8 copy-start.4
  34.1 2.8 %copy-start = (f32[1,1,320,64,64]{2,4,3,1,0:T(8,128)S(1)}, f32[1,1,320,64,64]{2,4,3,1,0:T(8,128)}, u32[]{:S(2)}) copy-start(f32[1,1,320,64,64]{2,4,3,1,0:T(8,128)} %param.13) | copy-start | bytes 15728644
  36.9 16.9 %copy-start.3 = (f32[8,64,256]{2,1,0:T(8,128)S(1)}, f32[8,64,256]{2,1,0:T(8,128)}, u32[]{:S(2)}) copy-start(f32[8,64,256]{2,1,0:T(8,128)} %basis.11) | copy-start | bytes 1572868
  36.9 25.5 %slice-start.1 = ((s8[6291456]{0:T(1024)(128)(4,1)}), s8[4194304]{0:T(1024)(128)(4,1)S(1)}, s32[]{:S(2)}) async-start(s8[6291456]{0:T(1024)(128)(4,1)} %bitcast.18), calls=%async_computation.11 | async-start | bytes 8388608
  62.4 19.7 %copy-start.2 = (f32[8,64,1536]{2,1,0:T(8,128)S(1)}, f32[8,64,1536]{2,1,0:T(8,128)}, u32[]{:S(2)}) copy-start(f32[8,64,1536]{2,1,0:T(8,128)} %basis.10) | copy-start | bytes 9437188
  62.4 19.7 %copy-start.5 = (f32[8,1536]{1,0:T(8,128)S(1)}, f32[8,1536]{1,0:T(8,128)}, u32[]{:S(2)}) copy-start(f32[8,1536]{1,0:T(8,128)} %data.5) | copy-start | bytes 147460

commit v3 on v2

--- a/solution.py
+++ b/solution.py
@@ -18,13 +18,20 @@
 PAIRS = 72
 ROWS = 16
 MIB = 1 << 20
-LIMIT0 = 4
-LIMIT = 10
+LIMIT0 = 8
+LIMIT = 18
 
 
 def split(value):
     high = value.astype(BF16)
     return high, (value - high.astype(F32)).astype(BF16)
+
+
+def thirds(value):
+    first = value.astype(BF16).astype(F32)
+    rest = value - first
+    second = rest.astype(BF16).astype(F32)
+    return first, second, (rest - second).astype(BF16).astype(F32)
 
 
 def mm(a, b):
@@ -55,16 +62,32 @@
     return block
 
 
-def setup_near(slots, column, near, far, obs, src, kh, kl, pq, count, oo, oot, ost, os, fot, fst, near_row, far_row):
+def setup_near(
+    column, near, far, obs, src, kh, kl, pq, count, oo, oot, ost, os, fot, fst,
+    slots, near_part, far_part, near_row, far_row, points, sources, left, right, built, sems, out_sems
+):
+    copies = [
+        pltpu.make_async_copy(a, b, sems.at[k])
+        for k, (a, b) in enumerate(
+            ((near, slots), (near, near_part), (far, far_part), (obs, points), (src, sources))
+        )
+    ]
+    for copy in copies:
+        copy.start()
     j = column[0]
     near_row[...] = jnp.full_like(near_row, -1)
-    near_row[:, 0:72] = near[...]
     far_row[...] = jnp.full_like(far_row, -1)
-    far_row[:, 0:320] = far[...]
+    left[...] = jnp.zeros_like(left)
+    right[...] = jnp.zeros_like(right)
+    for copy in copies:
+        copy.wait()
+    near_row[:, 0:72] = near_part[...]
+    far_row[:, 0:320] = far_part[...]
     f = near_row[...]
     live = f >= 0
     n = jnp.sum(jnp.where(live, 1.0, 0.0)).astype(jnp.int32)
     count[0] = n
+    count[1] = jnp.sum(jnp.where(far_row[...] >= 0, 1.0, 0.0)).astype(jnp.int32)
     o = lax.shift_right_arithmetic(f, 6)
     s = jnp.where(live, f & 63, -1)
     oc = jnp.where(live, lax.shift_right_arithmetic(o, 5) * 4 + (o & 31) - (2 * j - 1), -1)
@@ -80,34 +103,57 @@
     s = jnp.where(live, f & 63, -1)
     fot[...] = (iota((128, 384), 0) == o).astype(F32).astype(BF16)
     fst[...] = (iota((64, 384), 0) == s).astype(F32).astype(BF16)
+    groups = lax.shift_right_logical(n + 7, 3)
+
+    def leaving(g):
+        at = pl.ds(8 * g, 8)
+        return [
+            pltpu.make_async_copy(built.at[g & 1, k], out.at[at], out_sems.at[g & 1, k])
+            for k, out in enumerate((kh, kl))
+        ]
 
     def eight(g, carry):
-        for b in range(8):
+        @pl.when(g >= 2)
+        def _():
+            for copy in leaving(g - 2):
+                copy.wait()
+
+        def one(b):
             t = 8 * g + b
-            name = jnp.maximum(slots[t], 0)
+            name = jnp.maximum(slots[0, t], 0)
+            own = slice(8 * b, 8 * b + 8)
             for c in range(3):
-                pq[c, pl.ds(t, 1), :] = obs[c, pl.ds(lax.shift_right_logical(name, 6), 1), :]
-                pq[3 + c, pl.ds(t, 1), :] = src[c, pl.ds(name & 63, 1), :]
-        at = pl.ds(pl.multiple_of(8 * g, 8), 8)
-        p, q = [], []
-        for c in range(3):
-            pc, qc = pq[c, at, :], pq[3 + c, at, :]
-            centre = 0.5 * (jnp.mean(pc, axis=1, keepdims=True) + jnp.mean(qc, axis=1, keepdims=True))
-            pc, qc = pc - centre, qc - centre
-            pq[c, at, :] = pc
-            pq[3 + c, at, :] = qc
-            p.append(pc.T)
-            q.append(qc)
-
-        def one(b):
-            for r in range(0, 256, 32):
-                dx, dy, dz = (p[c][r : r + 32, b : b + 1] - q[c][b : b + 1] for c in range(3))
-                inverse = lax.rsqrt(dx * dx + dy * dy + dz * dz)
+                left[8 * b + c : 8 * b + c + 1, :] = points[c, pl.ds(lax.shift_right_logical(name, 6), 1), :]
+                right[8 * b + c : 8 * b + c + 1, :] = sources[c, pl.ds(name & 63, 1), :]
+            p, q = left[own, :], right[own, :]
+            centre = 0.5 * (jnp.mean(p, axis=1, keepdims=True) + jnp.mean(q, axis=1, keepdims=True))
+            p, q = p - centre, q - centre
+            for c in range(3):
+                pq[c, pl.ds(t, 1), :] = p[c : c + 1]
+                pq[3 + c, pl.ds(t, 1), :] = q[c : c + 1]
+            p1, p2, p3 = thirds(p)
+            q1, q2, q3 = thirds(-2.0 * q)
+            at = iota((8, 256), 0)
+            end_p = jnp.where(at < 6, 1.0, 0.0)
+            end_q = end_p
+            for k, (x, y) in enumerate(
+                zip(
+                    thirds(jnp.sum(p * p, axis=0, keepdims=True)),
+                    thirds(jnp.sum(q * q, axis=0, keepdims=True)),
+                )
+            ):
+                end_p = jnp.where(at == k, x, end_p)
+                end_q = jnp.where(at == k + 3, y, end_q)
+            factor_p = jnp.concatenate([p1, p1, p2, p2, p1, p3, end_p, jnp.zeros((8, 256), F32)], axis=0)
+            factor_q = jnp.concatenate([q1, q2, q1, q2, q3, q1, end_q, jnp.zeros((8, 256), F32)], axis=0)
+            factor_q = factor_q.astype(BF16)
+            factor_p = factor_p.T.astype(BF16)
+            for r in range(0, 256, 64):
+                inverse = lax.rsqrt(mm(factor_p[r : r + 64], factor_q))
                 square = inverse * inverse
-                fifth = square * square * (inverse * (1.0 / 256.0))
-                high, low = split(fifth)
-                kh[8 * g + b, r : r + 32, :] = high
-                kl[8 * g + b, r : r + 32, :] = low
+                high, low = split(square * square * inverse)
+                built[g & 1, 0, b, r : r + 64, :] = high
+                built[g & 1, 1, b, r : r + 64, :] = low
 
         for b in range(4):
             one(b)
@@ -117,9 +163,17 @@
             for b in range(4, 8):
                 one(b)
 
+        for copy in leaving(g):
+            copy.start()
         return carry
 
-    lax.fori_loop(0, lax.shift_right_logical(n + 7, 3), eight, 0)
+    lax.fori_loop(0, groups, eight, 0)
+    for back in (2, 1):
+
+        @pl.when(groups >= back)
+        def _():
+            for copy in leaving(groups - back):
+                copy.wait()
 
 
 def far_inputs(x, pick):
@@ -132,36 +186,67 @@
     return mm_nt(place, high) + mm_nt(place, low)
 
 
-def far_forward(x, pick, place, c, terms):
-    v = far_inputs(x, pick)[:, 0:320]
+WIDE = 256
+
+
+def far_copies(n, c, matrices, sem, act):
+    @pl.when(n <= WIDE)
+    def _():
+        act(pltpu.make_async_copy(c.at[:, :, pl.ds(0, WIDE)], matrices.at[:, :, pl.ds(0, WIDE)], sem))
+
+    @pl.when(n > WIDE)
+    def _():
+        act(pltpu.make_async_copy(c, matrices, sem))
+
+
+def far_forward(n, x, pick, place, c, terms):
+    v = far_inputs(x, pick)
     terms[...] = jnp.zeros_like(terms)
 
-    def eight(g, carry):
-        rows = [jnp.sum(c[8 * g + b] * v, axis=0, keepdims=True) for b in range(8)]
-        terms[pl.ds(pl.multiple_of(8 * g, 8), 8), 0:320] = jnp.concatenate(rows, axis=0)
-        return carry
-
-    lax.fori_loop(0, 8, eight, 0)
+    def part(lanes):
+        def eight(g, carry):
+            rows = [jnp.sum(c[8 * g + b, :, lanes] * v[:, lanes], axis=0, keepdims=True) for b in range(8)]
+            terms[pl.ds(pl.multiple_of(8 * g, 8), 8), lanes] = jnp.concatenate(rows, axis=0)
+            return carry
+
+        lax.fori_loop(0, 8, eight, 0)
+
+    part(slice(0, WIDE))
+
+    @pl.when(n > WIDE)
+    def _():
+        part(slice(WIDE, 320))
+
     return far_outputs(terms[...], place)
 
 
-def far_adjoint(x, pick, place, c, terms, held):
+def far_adjoint(n, x, pick, place, c, terms, held):
     held[...] = far_inputs(x, pick)
     terms[...] = jnp.zeros_like(terms)
 
-    def eight(g, carry):
-        for b in range(8):
-            carry = carry + c[8 * g + b] * held[pl.ds(8 * g + b, 1), 0:320]
-        return carry
-
-    terms[0:64, 0:320] = lax.fori_loop(0, 8, eight, jnp.zeros((64, 320), F32))
+    def part(lanes):
+        def eight(g, carry):
+            rows = held[pl.ds(pl.multiple_of(8 * g, 8), 8), lanes.start : (lanes.stop + 127) // 128 * 128]
+            for b in range(8):
+                carry = carry + c[8 * g + b, :, lanes] * rows[b : b + 1, 0 : lanes.stop - lanes.start]
+            return carry
+
+        zeros = jnp.zeros((64, lanes.stop - lanes.start), F32)
+        terms[0:64, lanes] = lax.fori_loop(0, 8, eight, zeros)
+
+    part(slice(0, WIDE))
+
+    @pl.when(n > WIDE)
+    def _():
+        part(slice(WIDE, 320))
+
     return far_outputs(terms[...], place)
 
 
-def near_products(n, moments, results, kh, kl, forward):
-    def four(g, carry):
+def near_products(n, moments, results, kh, kl, forward, arrive=None):
+    def four(first):
         for b in range(4):
-            t = 4 * g + b
+            t = first + b
             at = pl.ds(pl.multiple_of(t * ROWS, ROWS), ROWS)
             high, low = split(jnp.concatenate([moments[0, at, :], moments[1, at, :]], axis=1))
             both = jnp.concatenate([high, low], axis=0)
@@ -172,9 +257,26 @@
             both = both[:ROWS] + both[ROWS:]
             results[0, at, :] = both[:, :128]
             results[1, at, :] = both[:, 128:]
+
+    def eight(g, carry):
+        if arrive is not None:
+            arrive(g)
+        four(8 * g)
+        four(8 * g + 4)
         return carry
 
-    lax.fori_loop(0, lax.shift_right_logical(n + 3, 2), four, 0)
+    whole = lax.shift_right_logical(n, 3)
+    lax.fori_loop(0, whole, eight, 0)
+
+    @pl.when((n & 7) > 0)
+    def _():
+        if arrive is not None:
+            arrive(whole)
+        four(8 * whole)
+
+        @pl.when((n & 7) > 4)
+        def _():
+            four(8 * whole + 4)
 
 
 def store_moment(moments, g, c, value):
@@ -188,9 +290,40 @@
     return jnp.concatenate([results.at[0][at, :], results.at[1][at, :]], axis=1)
 
 
+def first_adjoint_block(
+    count, column, recv, kh_far, kl_far, pq, oo, ost, fot, fst, c, out, kh, kl,
+    yb, yp, moments, results, values, terms, held, matrices, sem, sems
+):
+    n = count[0]
+
+    def arriving(g):
+        at = pl.ds(8 * g, 8)
+        return [
+            pltpu.make_async_copy(a.at[at], b.at[at], sems.at[k, g])
+            for k, (a, b) in enumerate(((kh_far, kh), (kl_far, kl)))
+        ]
+
+    def start(g, carry):
+        for copy in arriving(g):
+            copy.start()
+        return carry
+
+    def arrive(g):
+        for copy in arriving(g):
+            copy.wait()
+
+    lax.fori_loop(0, lax.shift_right_logical(n + 7, 3), start, 0)
+    adjoint_block(
+        count, column, recv, kh, kl, pq, oo, ost, fot, fst, c, out,
+        yb, yp, moments, results, values, terms, held, matrices, sem, arrive=arrive
+    )
+
+
 def adjoint_block(
-    count, column, recv, kh, kl, pq, oo, ost, fot, fst, c, out, yb, yp, moments, results, values, terms, held
+    count, column, recv, kh, kl, pq, oo, ost, fot, fst, c, out,
+    yb, yp, moments, results, values, terms, held, matrices, sem, arrive=None
 ):
+    far_copies(count[1], c, matrices, sem, lambda copy: copy.start())
     n = count[0]
     j = column[0]
     for t in range(4):
@@ -224,7 +357,7 @@
         return carry
 
     lax.fori_loop(0, groups, enter, 0)
-    near_products(n, moments, results, kh, kl, False)
+    near_products(n, moments, results, kh, kl, False, arrive)
 
     def leave(g, carry):
         at = pl.ds(pl.multiple_of(g * 8, 8), 8)
@@ -232,14 +365,15 @@
         qx, qy, qz = (pq[3 + c, at, :] for c in range(3))
         z = w[0] + qx * (w[4] * qx + w[5] * qy - w[1]) + qy * (w[7] * qy + w[8] * qz - w[2])
         z = z + qz * (w[9] * qz + w[6] * qx - w[3])
-        values[at, :] = jnp.where(iota((8, 256), 0) + g * 8 < n, z, 0.0)
+        values[at, :] = jnp.where(iota((8, 256), 0) + g * 8 < n, z * (1.0 / 256.0), 0.0)
         return carry
 
     lax.fori_loop(0, groups, leave, 0)
     high, low = split(values[...])
     out[:, 0:256] = mm(ost[...], high) + mm(ost[...], low)
     tails = [recv[k, :, 768:896] for k in range(16)]
-    coeffs = far_adjoint(jnp.concatenate(tails, axis=0), fot[...], fst[...], c, terms, held)
+    far_copies(count[1], c, matrices, sem, lambda copy: copy.wait())
+    coeffs = far_adjoint(count[1], jnp.concatenate(tails, axis=0), fot[...], fst[...], matrices, terms, held)
     sums = functools.reduce(jnp.add, tails)
     for k in range(8):
         part = coeffs[8 * k : 8 * k + 8]
@@ -247,8 +381,10 @@
 
 
 def forward_block(
-    count, column, recv, kh, kl, pq, os, oot, fot, fst, c, out, xp, moments, results, values, yb, terms
+    count, column, recv, kh, kl, pq, os, oot, fot, fst, c, out,
+    xp, moments, results, values, yb, terms, matrices, sem
 ):
+    far_copies(count[1], c, matrices, sem, lambda copy: copy.start())
     n = count[0]
     j = column[0]
     high, low = split(recv[:, 0:256])
@@ -284,7 +420,7 @@
         inside = iota((8, 256), 0) + g * 8 < n
         parts = (3.0 * xx - trace, 3.0 * xy, 3.0 * xz, 3.0 * yy - trace, 3.0 * yz, 3.0 * zz - trace)
         for a, part in enumerate(parts):
-            values[at, 256 * a : 256 * a + 256] = jnp.where(inside, part, 0.0)
+            values[at, 256 * a : 256 * a + 256] = jnp.where(inside, part * (1.0 / 256.0), 0.0)
         return carry
 
     lax.fori_loop(0, groups, leave, 0)
@@ -297,16 +433,19 @@
                 piece = yb[4 * row + t : 4 * row + t + 1, 768 * half : 768 * half + 768]
                 out[row * 4 + holder, 2 * t + half : 2 * t + half + 1, 0:768] = piece
     tails = [recv[8 * k : 8 * k + 8, 256:384] for k in range(8)]
-    coeffs = far_forward(recv[:, 256:384], fst[...], fot[...], c, terms)
+    far_copies(count[1], c, matrices, sem, lambda copy: copy.wait())
+    coeffs = far_forward(count[1], recv[:, 256:384], fst[...], fot[...], matrices, terms)
     sums = functools.reduce(jnp.add, tails)
     for k in range(16):
         out[k, :, 768:896] = jnp.where(iota((8, 128), 1) < 64, coeffs[8 * k : 8 * k + 8], sums)
 
 
-def send_residual(zone, values, basis, out, scalars):
+def send_residual(zone, values, basis, out, scalars, copies=()):
     lanes = iota((64, 128), 1)
     columns = jnp.zeros((64, 128), F32)
     for r in range(8):
+        if copies:
+            copies[r].wait()
         column = jnp.sum(basis[r] * values[r : r + 1, :], axis=1, keepdims=True)
         columns = jnp.where(lanes == r, column, columns)
     columns = jnp.concatenate([columns, jnp.zeros((64, 128), F32)], axis=0)
@@ -334,8 +473,14 @@
         rows(4)
 
 
-def start_obs(zone, count, data, basis, out):
-    send_residual(zone[0], data, basis, out, (total(data[...] * data[...]),))
+def start_obs(zone, data_far, basis_far, out, data, basis, sem, sems):
+    first = pltpu.make_async_copy(data_far, data, sem)
+    first.start()
+    copies = [pltpu.make_async_copy(basis_far.at[r], basis.at[r], sems.at[r]) for r in range(8)]
+    for copy in copies:
+        copy.start()
+    first.wait()
+    send_residual(zone[0], data, basis, out, (total(data[...] * data[...]),), copies)
 
 
 def gather_projected(zone, recv, basis, p):
@@ -432,17 +577,22 @@
 
 VM = pl.BlockSpec(memory_space=pltpu.VMEM)
 SM = pl.BlockSpec(memory_space=pltpu.SMEM)
+FAR = pl.BlockSpec(memory_space=pltpu.HBM)
 
 
 def shape(*dims, dtype=F32):
     return jax.ShapeDtypeStruct(dims, dtype)
 
 
-def call(kernel, outs, ins, scratch=(), out_specs=None, scalars=0, limit=4):
+def call(kernel, outs, ins, scratch=(), out_specs=None, scalars=0, far=(), limit=4):
+    specs = [SM] * scalars + [VM] * (len(ins) - scalars)
+    for at in far:
+        specs[at] = FAR
+    ins = [pltpu.with_memory_space_constraint(a, pltpu.HBM) if k in far else a for k, a in enumerate(ins)]
     return pl.pallas_call(
         kernel,
         out_shape=outs,
-        in_specs=[SM] * scalars + [VM] * (len(ins) - scalars),
+        in_specs=specs,
         out_specs=out_specs or [VM] * len(outs),
         scratch_shapes=list(scratch),
         compiler_params=pltpu.CompilerParams(vmem_limit_bytes=limit * MIB),
@@ -457,32 +607,62 @@
     index = lax.axis_index(SRC).astype(jnp.int32)
     column = index.reshape(1)
     zone = (index % 4).reshape(1)
-    near = near_pairs.reshape(-1)
     obs_message = shape(16, 8, 896)
     src_message = shape(8, 8, 384)
     row = shape(8, 128)
+    dma = pltpu.SemaphoreType.DMA
 
     def bf(*dims):
         return shape(*dims, dtype=BF16)
 
-    kh, kl, pq, count, oo, oot, ost, os, fot, fst = call(
+    (message,) = call(
+        start_obs,
+        [obs_message],
+        [zone, data, obs_basis],
+        scalars=1,
+        far=(1, 2),
+        scratch=[pltpu.VMEM((8, 1536), F32), pltpu.VMEM((8, 64, 1536), F32), dma, dma((8,))],
+        limit=LIMIT0,
+    )
+    received = exchange(message, SRC)
+    kh_far, kl_far, pq, count, oo, oot, ost, os, fot, fst = call(
         setup_near,
         [
-            bf(PAIRS, 256, 256), bf(PAIRS, 256, 256), shape(6, PAIRS, 256), shape(1, dtype=jnp.int32),
+            *[pltpu.HBM((PAIRS, 256, 256), BF16)] * 2, shape(6, PAIRS, 256), shape(2, dtype=jnp.int32),
             bf(128, 16), bf(16, 128), bf(64, 128), bf(128, 64), bf(128, 384), bf(64, 384),
         ],
         [
-            near, column, near_pairs.reshape(1, 72), far_pairs.reshape(1, 320),
+            column, near_pairs.reshape(1, 72), far_pairs.reshape(1, 320),
             jnp.transpose(obs_points, (1, 0, 2)), jnp.transpose(src_points, (1, 0, 2)),
         ],
+        scalars=1,
+        far=(1, 2, 3, 4),
+        out_specs=[FAR] * 2 + [VM] + [SM] + [VM] * 6,
+        scratch=[
+            pltpu.SMEM((1, 72), jnp.int32), pltpu.VMEM((1, 72), jnp.int32), pltpu.VMEM((1, 320), jnp.int32),
+            pltpu.VMEM((1, 128), jnp.int32), pltpu.VMEM((1, 384), jnp.int32), pltpu.VMEM((3, 128, 256), F32),
+            pltpu.VMEM((3, 64, 256), F32), pltpu.VMEM((64, 256), F32), pltpu.VMEM((64, 256), F32),
+            pltpu.VMEM((2, 2, 8, 256, 256), BF16), dma((5,)), dma((2, 2)),
+        ],
+        limit=LIMIT0,
+    )
+    matrices = jnp.transpose(couplings[0, 0], (1, 2, 0))
+    matrix_scratch = [pltpu.VMEM((64, 64, 320), F32), dma]
+    adjoint_scratch = [
+        pltpu.VMEM((16, 1536), F32), pltpu.VMEM((80, 1536), F32), pltpu.VMEM((2, 80 * ROWS, 128), F32),
+        pltpu.VMEM((2, 80 * ROWS, 128), F32), pltpu.VMEM((128, 256), F32), pltpu.VMEM((128, 384), F32),
+        pltpu.VMEM((64, 384), F32), *matrix_scratch,
+    ]
+    out, kh, kl = call(
+        first_adjoint_block,
+        [shape(64, 384), bf(PAIRS, 256, 256), bf(PAIRS, 256, 256)],
+        [count, column, received, kh_far, kl_far, pq, oo, ost, fot, fst, matrices],
         scalars=2,
-        out_specs=[VM] * 3 + [SM] + [VM] * 6,
-        scratch=[pltpu.VMEM((1, 128), jnp.int32), pltpu.VMEM((1, 384), jnp.int32)],
-        limit=LIMIT0,
-    )
-    matrices = jnp.transpose(couplings[0, 0], (1, 2, 0))
-    (message,) = call(start_obs, [obs_message], [zone, count, data, obs_basis], scalars=2)
-    received = exchange(message, SRC)
+        far=(3, 4, 10),
+        scratch=[*adjoint_scratch, dma((2, 9))],
+        limit=LIMIT,
+    )
+    received = exchange(out.reshape(8, 8, 384), OBS)
 
     def adjoint(message):
         (out,) = call(
@@ -490,11 +670,8 @@
             [shape(64, 384)],
             [count, column, message, kh, kl, pq, oo, ost, fot, fst, matrices],
             scalars=2,
-            scratch=[
-                pltpu.VMEM((16, 1536), F32), pltpu.VMEM((80, 1536), F32), pltpu.VMEM((2, 80 * ROWS, 128), F32),
-                pltpu.VMEM((2, 80 * ROWS, 128), F32), pltpu.VMEM((128, 256), F32), pltpu.VMEM((128, 384), F32),
-                pltpu.VMEM((64, 384), F32),
-            ],
+            far=(10,),
+            scratch=adjoint_scratch,
             limit=LIMIT,
         )
         return exchange(out.reshape(8, 8, 384), OBS)
@@ -505,16 +682,18 @@
             [obs_message],
             [count, column, exchange(message, OBS).reshape(64, 384), kh, kl, pq, os, oot, fot, fst, matrices],
             scalars=2,
+            far=(10,),
             scratch=[
                 pltpu.VMEM((80, 256), F32), pltpu.VMEM((2, 80 * ROWS, 128), F32), pltpu.VMEM((2, 80 * ROWS, 128), F32),
                 pltpu.VMEM((128, 1536), F32), pltpu.VMEM((16, 1536), F32), pltpu.VMEM((128, 384), F32),
+                *matrix_scratch,
             ],
             limit=LIMIT,
         )
         return exchange(out, SRC)
 
     plane, line = shape(8, 1536), shape(8, 256)
-    n0, sums0, message = call(first_src, [line, row, src_message], [adjoint(received), src_basis])
+    n0, sums0, message = call(first_src, [line, row, src_message], [received, src_basis])
     p0, gamma0, message = call(
         first_obs, [plane, row, obs_message], [zone, forward(message), data, obs_basis], scalars=1
     )

time: 172 us -> 155 us (0.901); the launches traced: 170 us -> 154 us
  blocking collectives: 123 us -> 104 us
  local copies, waits for them, and re-layouts: 9.25 us -> 0.52 us
  starting transfers between devices: 0 us -> 8.43 us
  Pallas kernels: 36.6 us -> 38.6 us
  waiting for transfers between devices: 0 us -> 1.93 us
    all_to_all x10 -> x9, blocking collectives: 123 us -> 104 us  [exchange(): return lax.all_to_all(value, axes, split_axis=0, concat_axis=0, tiled=True)]
    unnamed x24 -> x6, local copies, waits for them, and re-layouts: 8.74 us -> 0.01 us
    all_to_all x0 -> x1, starting transfers between devices: none -> 8.43 us  [exchange(): return lax.all_to_all(value, axes, split_axis=0, concat_axis=0, tiled=True)]
    pallas_call x12, Pallas kernels: 36.6 us -> 38.6 us  [call(): pl.pallas_call(kernel, out_shape=outs, in_specs=specs, out_specs=out_spec...]
    all_to_all x0 -> x1, waiting for transfers between devices: none -> 1.93 us  [exchange(): return lax.all_to_all(value, axes, split_axis=0, concat_axis=0, tiled=True)]
  transfers between devices with their start and end apart: 0 -> 1, of which waited for: 0 -> 1; matrix products, arithmetic and copies ran while one was open for 0% -> 0% of each run, Pallas kernels for 0% -> 5%
where the time goes in v3:
time: 155 us; the launch traced here: 154 us
  blocking collectives  104 us (67%)
  Pallas kernels  38.6 us (25%)
  starting transfers between devices  8.43 us (5%)
  waiting for transfers between devices  1.93 us (1%)
    all_to_all x9, blocking collectives, exchange(): return lax.all_to_all(value, axes, split_axis=0, concat_axis=0, tiled=True)  104 us
    pallas_call x12, Pallas kernels, call(): pl.pallas_call(kernel, out_shape=outs, in_specs=specs, out_specs=out_spec...  38.6 us
    all_to_all x1, starting transfers between devices, exchange(): return lax.all_to_all(value, axes, split_axis=0, concat_axis=0, tiled=True)  8.43 us
  transfers between devices with their start and end apart: 1, of which 1 were waited for; matrix products, arithmetic and copies ran while one was open for 0% of the time, Pallas kernels for 5%

profile of v3, /device:TPU:1, one launch (start us, length us, event | category | flops | bytes accessed | tf_op | source)
XLA Modules:
  0.0 154.5 jit_solution(11214970359283991474)
XLA Ops:
  0.6 3.5 %shard_map.112 = f32[16,8,896]{2,1,0:T(8,128)} custom-call(s32[1]{0:T(128)} %bitcast.5.zone, f32[8,1536]{1,0:T(8,128)} %data.3, f32[8,64,1536]{2,1,0:T(8,128)} %basis.8), custom_call_target="tpu_custom_call" | custom-call | tf_op jit(solution)/shard_map/pallas_call | solution.py:592
  4.2 8.4 %all-to-all-start = ((f32[16,8,896]{2,1,0:T(8,128)}), f32[16,8,896]{2,1,0:T(8,128)S(1)}, u32[]{:S(2)}, u32[]{:S(2)}) async-start(f32[16,8,896]{2,1,0:T(8,128)} %shard_map.112), calls=%async_computation | async-start | bytes 917504 | tf_op jit(solution)/shard_map/all_to_all | solution.py:603
  12.6 7.7 %shard_map.111 = (bf16[72,256,256]{2,1,0:T(8,128)(2,1)}, bf16[72,256,256]{2,1,0:T(8,128)(2,1)}, f32[6,72,256]{2,1,0:T(8,128)S(1)}, s32[2]{0:T(128)S(1)}, bf16[12...) custom-call(s32[1]{0:T(128)} %bitcast.column, ...), custom_call_target="tpu_custom_call" | custom-call | tf_op jit(solution)/shard_map/pallas_call | solution.py:592
  20.3 1.9 %all-to-all-done.recv = f32[16,8,896]{2,1,0:T(8,128)S(1)} async-done(((f32[16,8,896]{2,1,0:T(8,128)}), f32[16,8,896]{2,1,0:T(8,128)S(1)}, u32[]{:S(2)}, u32[]{:S(2)}) %all-to-all-start) | async-done | bytes 458784 | tf_op jit(solution)/shard_map/all_to_all | solution.py:603
  22.2 0.0 copy-start.1
  22.2 6.2 %shard_map.113 = (f32[64,384]{1,0:T(8,128)S(1)}, bf16[72,256,256]{2,1,0:T(8,128)(2,1)S(1)}, bf16[72,256,256]{2,1,0:T(8,128)(2,1)S(1)}) custom-call(s32[2]{0:T(128)S(1)} %get-tuple-element.34.count, s32[1]{0:T(128)} %bitcast.column, f32[16,8,896]{2,1,0:T(8,128)S(1)} %all-to-all-done.recv, bf16[72,256,256]{2,1,0:T(8,128)(2,1)} %get-tuple-element.35.kh_far, ...), custom_call_target="tpu_custom_call" | custom-call | tf_op jit(solution)/shard_map/pallas_call | solution.py:592
  28.5 11.4 %all_to_all.50.recv = f32[8,8,384]{2,1,0:T(8,128)S(1)} all-to-all(f32[8,8,384]{2,1,0:T(8,128)S(1)} %bitcast.20), channel_id=1, replica_groups=mesh['obs_0'=4,'obs_1'=2,'src_0'=4,'src_1'=4] {'obs_0','obs_1'}, dimensions={0} | all-to-all | bytes 196608 | tf_op jit(solution)/shard_map/all_to_all | solution.py:603
  39.8 0.0 copy-done.1
  39.9 0.5 shard_map.114
  40.3 8.2 %all_to_all.51 = f32[8,8,384]{2,1,0:T(8,128)S(1)} all-to-all(f32[8,8,384]{2,1,0:T(8,128)S(1)} %get-tuple-element.43), channel_id=1, replica_groups=mesh['obs_0'=4,'obs_1'=2,'src_0'=4,'src_1'=4] {'obs_0','obs_1'}, dimensions={0} | all-to-all | bytes 196608 | tf_op jit(solution)/shard_map/all_to_all | solution.py:603
  48.5 0.0 copy-start
  48.5 0.0 copy-start.2
  48.5 4.9 %shard_map.115 = f32[16,8,896]{2,1,0:T(8,128)S(1)} custom-call(s32[2]{0:T(128)S(1)} %get-tuple-element.34.count, s32[1]{0:T(128)} %bitcast.column, f32[64,384]{1,0:T(8,128)S(1)} %bitcast.17, bf16[72,256,256]{2,1,0:T(8,128)(2,1)S(1)} %get-tuple-element.44.kh, bf16[72,256,256]{2,1,0:T(8,128)(2,1)S(1)} %get-tuple-element.45.kl, ...), custom_call_target="tpu_custom_call" | custom-call | tf_op jit(solution)/shard_map/pallas_call | solution.py:592
  53.4 15.6 %all_to_all.52.recv = f32[16,8,896]{2,1,0:T(8,128)S(1)} all-to-all(f32[16,8,896]{2,1,0:T(8,128)S(1)} %shard_map.115), channel_id=1, replica_groups=mesh['obs_0'=4,'obs_1'=2,'src_0'=4,'src_1'=4] {'src_0','src_1'}, dimensions={0} | all-to-all | bytes 917504 | tf_op jit(solution)/shard_map/all_to_all | solution.py:603
  69.0 0.0 copy-done
  69.0 0.0 copy-done.2
  69.0 1.0 shard_map.116
  70.0 12.8 %all_to_all.53.recv = f32[16,8,896]{2,1,0:T(8,128)S(1)} all-to-all(f32[16,8,896]{2,1,0:T(8,128)S(1)} %get-tuple-element.48), channel_id=1, replica_groups=mesh['obs_0'=4,'obs_1'=2,'src_0'=4,'src_1'=4] {'src_0','src_1'}, dimensions={0} | all-to-all | bytes 917504 | tf_op jit(solution)/shard_map/all_to_all | solution.py:603
  82.8 3.7 %shard_map.117 = f32[64,384]{1,0:T(8,128)S(1)} custom-call(s32[2]{0:T(128)S(1)} %get-tuple-element.34.count, s32[1]{0:T(128)} %bitcast.column, f32[16,8,896]{2,1,0:T(8,128)S(1)} %all_to_all.53.recv, bf16[72,256,256]{2,1,0:T(8,128)(2,1)S(1)} %get-tuple-element.44.kh, bf16[72,256,256]{2,1,0:T(8,128)(2,1)S(1)} %get-tuple-element.45.kl, ...), custom_call_target="tpu_custom_call" | custom-call | tf_op jit(solution)/shard_map/pallas_call | solution.py:592
  86.5 11.2 %all_to_all.54.recv = f32[8,8,384]{2,1,0:T(8,128)S(1)} all-to-all(f32[8,8,384]{2,1,0:T(8,128)S(1)} %bitcast.19), channel_id=1, replica_groups=mesh['obs_0'=4,'obs_1'=2,'src_0'=4,'src_1'=4] {'obs_0','obs_1'}, dimensions={0} | all-to-all | bytes 196608 | tf_op jit(solution)/shard_map/all_to_all | solution.py:603
  97.8 0.5 shard_map.118
  98.3 8.2 %all_to_all.55 = f32[8,8,384]{2,1,0:T(8,128)S(1)} all-to-all(f32[8,8,384]{2,1,0:T(8,128)S(1)} %get-tuple-element.51), channel_id=1, replica_groups=mesh['obs_0'=4,'obs_1'=2,'src_0'=4,'src_1'=4] {'obs_0','obs_1'}, dimensions={0} | all-to-all | bytes 196608 | tf_op jit(solution)/shard_map/all_to_all | solution.py:603
  106.4 4.9 %shard_map.119 = f32[16,8,896]{2,1,0:T(8,128)S(1)} custom-call(s32[2]{0:T(128)S(1)} %get-tuple-element.34.count, s32[1]{0:T(128)} %bitcast.column, f32[64,384]{1,0:T(8,128)S(1)} %bitcast.18, bf16[72,256,256]{2,1,0:T(8,128)(2,1)S(1)} %get-tuple-element.44.kh, bf16[72,256,256]{2,1,0:T(8,128)(2,1)S(1)} %get-tuple-element.45.kl, ...), custom_call_target="tpu_custom_call" | custom-call | tf_op jit(solution)/shard_map/pallas_call | solution.py:592
  111.3 12.9 %all_to_all.56.recv = f32[16,8,896]{2,1,0:T(8,128)S(1)} all-to-all(f32[16,8,896]{2,1,0:T(8,128)S(1)} %shard_map.119), channel_id=1, replica_groups=mesh['obs_0'=4,'obs_1'=2,'src_0'=4,'src_1'=4] {'src_0','src_1'}, dimensions={0} | all-to-all | bytes 917504 | tf_op jit(solution)/shard_map/all_to_all | solution.py:603
  124.2 1.0 shard_map.120
  125.3 13.0 %all_to_all.57.recv = f32[16,8,896]{2,1,0:T(8,128)S(1)} all-to-all(f32[16,8,896]{2,1,0:T(8,128)S(1)} %get-tuple-element.54), channel_id=1, replica_groups=mesh['obs_0'=4,'obs_1'=2,'src_0'=4,'src_1'=4] {'src_0','src_1'}, dimensions={0} | all-to-all | bytes 917504 | tf_op jit(solution)/shard_map/all_to_all | solution.py:603
  138.3 3.7 %shard_map.121 = f32[64,384]{1,0:T(8,128)S(1)} custom-call(s32[2]{0:T(128)S(1)} %get-tuple-element.34.count, s32[1]{0:T(128)} %bitcast.column, f32[16,8,896]{2,1,0:T(8,128)S(1)} %all_to_all.57.recv, bf16[72,256,256]{2,1,0:T(8,128)(2,1)S(1)} %get-tuple-element.44.kh, bf16[72,256,256]{2,1,0:T(8,128)(2,1)S(1)} %get-tuple-element.45.kl, ...), custom_call_target="tpu_custom_call" | custom-call | tf_op jit(solution)/shard_map/pallas_call | solution.py:592
  142.0 11.0 %all_to_all.58.recv = f32[8,8,384]{2,1,0:T(8,128)S(1)} all-to-all(f32[8,8,384]{2,1,0:T(8,128)S(1)} %bitcast.16), channel_id=1, replica_groups=mesh['obs_0'=4,'obs_1'=2,'src_0'=4,'src_1'=4] {'obs_0','obs_1'}, dimensions={0} | all-to-all | bytes 196608 | tf_op jit(solution)/shard_map/all_to_all | solution.py:603
  153.0 0.9 shard_map.122
  153.9 0.5 slice_bitcast_fusion
Async XLA Ops:
  4.2 18.1 %all-to-all-start = ((f32[16,8,896]{2,1,0:T(8,128)}), f32[16,8,896]{2,1,0:T(8,128)S(1)}, u32[]{:S(2)}, u32[]{:S(2)}) async-start(f32[16,8,896]{2,1,0:T(8,128)} %shard_map.112), calls=%async_computation | async-start | bytes 917504 | tf_op jit(solution)/shard_map/all_to_all | solution.py:603
  22.2 17.6 %copy-start.1 = (f32[8,64,256]{2,1,0:T(8,128)S(1)}, f32[8,64,256]{2,1,0:T(8,128)}, u32[]{:S(2)}) copy-start(f32[8,64,256]{2,1,0:T(8,128)} %basis.9) | copy-start | bytes 1572868
  48.5 20.5 %copy-start = (f32[8,64,1536]{2,1,0:T(8,128)S(1)}, f32[8,64,1536]{2,1,0:T(8,128)}, u32[]{:S(2)}) copy-start(f32[8,64,1536]{2,1,0:T(8,128)} %basis.8) | copy-start | bytes 9437188
  48.5 20.5 %copy-start.2 = (f32[8,1536]{1,0:T(8,128)S(1)}, f32[8,1536]{1,0:T(8,128)}, u32[]{:S(2)}) copy-start(f32[8,1536]{1,0:T(8,128)} %data.3) | copy-start | bytes 147460

commit v4 on v3

--- a/solution.py
+++ b/solution.py
@@ -63,13 +63,13 @@
 
 
 def setup_near(
-    column, near, far, obs, src, kh, kl, pq, count, oo, oot, ost, os, fot, fst,
-    slots, near_part, far_part, near_row, far_row, points, sources, left, right, built, sems, out_sems
+    column, near, far, points, sources, kh, kl, pq, count, oo, oot, ost, os, fot, fst,
+    slots, near_part, far_part, near_row, far_row, left, right, built, sems, out_sems
 ):
     copies = [
         pltpu.make_async_copy(a, b, sems.at[k])
         for k, (a, b) in enumerate(
-            ((near, slots), (near, near_part), (far, far_part), (obs, points), (src, sources))
+            ((near, slots), (near, near_part), (far, far_part))
         )
     ]
     for copy in copies:
@@ -105,18 +105,25 @@
     fst[...] = (iota((64, 384), 0) == s).astype(F32).astype(BF16)
     groups = lax.shift_right_logical(n + 7, 3)
 
-    def leaving(g):
-        at = pl.ds(8 * g, 8)
+    def leaving(g, part):
+        at = pl.ds(8 * g + 4 * part, 4)
         return [
-            pltpu.make_async_copy(built.at[g & 1, k], out.at[at], out_sems.at[g & 1, k])
+            pltpu.make_async_copy(built.at[g & 1, k, pl.ds(4 * part, 4)], out.at[at], out_sems.at[g & 1, k, part])
             for k, out in enumerate((kh, kl))
         ]
+
+    def left_behind(g):
+        for part in range(2):
+
+            @pl.when(n > 8 * g + 4 * part)
+            def _():
+                for copy in leaving(g, part):
+                    copy.wait()
 
     def eight(g, carry):
         @pl.when(g >= 2)
         def _():
-            for copy in leaving(g - 2):
-                copy.wait()
+            left_behind(g - 2)
 
         def one(b):
             t = 8 * g + b
@@ -147,7 +154,7 @@
             factor_p = jnp.concatenate([p1, p1, p2, p2, p1, p3, end_p, jnp.zeros((8, 256), F32)], axis=0)
             factor_q = jnp.concatenate([q1, q2, q1, q2, q3, q1, end_q, jnp.zeros((8, 256), F32)], axis=0)
             factor_q = factor_q.astype(BF16)
-            factor_p = factor_p.T.astype(BF16)
+            factor_p = factor_p.astype(BF16).T
             for r in range(0, 256, 64):
                 inverse = lax.rsqrt(mm(factor_p[r : r + 64], factor_q))
                 square = inverse * inverse
@@ -157,14 +164,16 @@
 
         for b in range(4):
             one(b)
+        for copy in leaving(g, 0):
+            copy.start()
 
         @pl.when(n > 8 * g + 4)
         def _():
             for b in range(4, 8):
                 one(b)
-
-        for copy in leaving(g):
-            copy.start()
+            for copy in leaving(g, 1):
+                copy.start()
+
         return carry
 
     lax.fori_loop(0, groups, eight, 0)
@@ -172,8 +181,7 @@
 
         @pl.when(groups >= back)
         def _():
-            for copy in leaving(groups - back):
-                copy.wait()
+            left_behind(groups - back)
 
 
 def far_inputs(x, pick):
@@ -260,7 +268,8 @@
 
     def eight(g, carry):
         if arrive is not None:
-            arrive(g)
+            arrive(g, 0)
+            arrive(g, 1)
         four(8 * g)
         four(8 * g + 4)
         return carry
@@ -271,11 +280,13 @@
     @pl.when((n & 7) > 0)
     def _():
         if arrive is not None:
-            arrive(whole)
+            arrive(whole, 0)
         four(8 * whole)
 
         @pl.when((n & 7) > 4)
         def _():
+            if arrive is not None:
+                arrive(whole, 1)
             four(8 * whole + 4)
 
 
@@ -296,22 +307,28 @@
 ):
     n = count[0]
 
-    def arriving(g):
-        at = pl.ds(8 * g, 8)
+    def arriving(g, part):
+        at = pl.ds(8 * g + 4 * part, 4)
         return [
-            pltpu.make_async_copy(a.at[at], b.at[at], sems.at[k, g])
+            pltpu.make_async_copy(a.at[at], b.at[at], sems.at[k, part, g])
             for k, (a, b) in enumerate(((kh_far, kh), (kl_far, kl)))
         ]
 
     def start(g, carry):
-        for copy in arriving(g):
-            copy.start()
+        for part in range(2):
+
+            @pl.when(n > 8 * g + 4 * part)
+            def _():
+                for copy in arriving(g, part):
+                    copy.start()
+
         return carry
 
-    def arrive(g):
-        for copy in arriving(g):
+    def arrive(g, part):
+        for copy in arriving(g, part):
             copy.wait()
 
+    far_copies(count[1], c, matrices, sem, lambda copy: copy.start())
     lax.fori_loop(0, lax.shift_right_logical(n + 7, 3), start, 0)
     adjoint_block(
         count, column, recv, kh, kl, pq, oo, ost, fot, fst, c, out,
@@ -323,7 +340,8 @@
     count, column, recv, kh, kl, pq, oo, ost, fot, fst, c, out,
     yb, yp, moments, results, values, terms, held, matrices, sem, arrive=None
 ):
-    far_copies(count[1], c, matrices, sem, lambda copy: copy.start())
+    if arrive is None:
+        far_copies(count[1], c, matrices, sem, lambda copy: copy.start())
     n = count[0]
     j = column[0]
     for t in range(4):
@@ -332,10 +350,10 @@
         holder = lax.shift_right_logical(jnp.clip(col, 0, 31), 3)
         for row in range(4):
             for half in range(2):
-                piece = recv[row * 4 + holder, 2 * t + half : 2 * t + half + 1, 0:768]
+                piece = recv[row * 4 + holder, 2 * t + half : 2 * t + half + 1, 0:640]
                 if t in (0, 3):
                     piece = jnp.where(inside, piece, 0.0)
-                yb[4 * row + t : 4 * row + t + 1, 768 * half : 768 * half + 768] = piece
+                yb[4 * row + t : 4 * row + t + 1, 640 * half : 640 * half + 640] = piece
     high, low = split(yb[...])
     yp[...] = mm(oo[0:80, :], high) + mm(oo[0:80, :], low)
     values[...] = jnp.zeros_like(values)
@@ -343,11 +361,9 @@
 
     def enter(g, carry):
         at = pl.ds(pl.multiple_of(g * 8, 8), 8)
-        y = [yp[at, 256 * a : 256 * a + 256] for a in range(6)]
+        hxx, hxy, hxz, hyy, hyz = (yp[at, 256 * a : 256 * a + 256] for a in range(5))
+        hzz = -(hxx + hyy)
         px, py, pz = (pq[c, at, :] for c in range(3))
-        trace = y[0] + y[3] + y[5]
-        hxx, hyy, hzz = (3.0 * y[a] - trace for a in (0, 3, 5))
-        hxy, hxz, hyz = (3.0 * y[a] for a in (1, 2, 4))
         ax, ay, az = hxx * px, hyy * py, hzz * pz
         bx, by, bz = hxy * py + hxz * pz, hxy * px + hyz * pz, hxz * px + hyz * py
         constant = px * (ax + hxy * py) + py * (ay + hyz * pz) + pz * (az + hxz * px)
@@ -357,6 +373,18 @@
         return carry
 
     lax.fori_loop(0, groups, enter, 0)
+    tails = [recv[k, :, 640:768] for k in range(16)]
+
+    def far():
+        far_copies(count[1], c, matrices, sem, lambda copy: copy.wait())
+        coeffs = far_adjoint(count[1], jnp.concatenate(tails, axis=0), fot[...], fst[...], matrices, terms, held)
+        sums = functools.reduce(jnp.add, tails)
+        for k in range(8):
+            part = coeffs[8 * k : 8 * k + 8]
+            out[8 * k : 8 * k + 8, 256:384] = jnp.where(iota((8, 128), 1) < 64, part, sums)
+
+    if arrive is not None:
+        far()
     near_products(n, moments, results, kh, kl, False, arrive)
 
     def leave(g, carry):
@@ -371,13 +399,8 @@
     lax.fori_loop(0, groups, leave, 0)
     high, low = split(values[...])
     out[:, 0:256] = mm(ost[...], high) + mm(ost[...], low)
-    tails = [recv[k, :, 768:896] for k in range(16)]
-    far_copies(count[1], c, matrices, sem, lambda copy: copy.wait())
-    coeffs = far_adjoint(count[1], jnp.concatenate(tails, axis=0), fot[...], fst[...], matrices, terms, held)
-    sums = functools.reduce(jnp.add, tails)
-    for k in range(8):
-        part = coeffs[8 * k : 8 * k + 8]
-        out[8 * k : 8 * k + 8, 256:384] = jnp.where(iota((8, 128), 1) < 64, part, sums)
+    if arrive is None:
+        far()
 
 
 def forward_block(
@@ -418,7 +441,7 @@
         zz = pz * (az - s[3]) + s[9]
         trace = xx + yy + zz
         inside = iota((8, 256), 0) + g * 8 < n
-        parts = (3.0 * xx - trace, 3.0 * xy, 3.0 * xz, 3.0 * yy - trace, 3.0 * yz, 3.0 * zz - trace)
+        parts = (3.0 * xx - trace, 3.0 * xy, 3.0 * xz, 3.0 * yy - trace, 3.0 * yz)
         for a, part in enumerate(parts):
             values[at, 256 * a : 256 * a + 256] = jnp.where(inside, part * (1.0 / 256.0), 0.0)
         return carry
@@ -430,17 +453,41 @@
         holder = lax.shift_right_logical(jnp.clip(2 * j - 1 + t, 0, 31), 3)
         for row in range(4):
             for half in range(2):
-                piece = yb[4 * row + t : 4 * row + t + 1, 768 * half : 768 * half + 768]
-                out[row * 4 + holder, 2 * t + half : 2 * t + half + 1, 0:768] = piece
+                piece = yb[4 * row + t : 4 * row + t + 1, 640 * half : 640 * half + 640]
+                out[row * 4 + holder, 2 * t + half : 2 * t + half + 1, 0:640] = piece
     tails = [recv[8 * k : 8 * k + 8, 256:384] for k in range(8)]
     far_copies(count[1], c, matrices, sem, lambda copy: copy.wait())
     coeffs = far_forward(count[1], recv[:, 256:384], fst[...], fot[...], matrices, terms)
     sums = functools.reduce(jnp.add, tails)
     for k in range(16):
-        out[k, :, 768:896] = jnp.where(iota((8, 128), 1) < 64, coeffs[8 * k : 8 * k + 8], sums)
-
-
-def send_residual(zone, values, basis, out, scalars, copies=()):
+        out[k, :, 640:768] = jnp.where(iota((8, 128), 1) < 64, coeffs[8 * k : 8 * k + 8], sums)
+
+
+def send_residual(zone, values, basis, out, weights, scalars, copies=()):
+    y = [values[:, 256 * a : 256 * a + 256] for a in range(6)]
+    trace = y[0] + y[3] + y[5]
+    for a, part in enumerate((3.0 * y[0] - trace, 3.0 * y[1], 3.0 * y[2], 3.0 * y[3] - trace, 3.0 * y[4])):
+        weights[:, 256 * a : 256 * a + 256] = part
+
+    def rows(d):
+        for t in range(4):
+            r = 2 * d - 1 + t
+            if 0 <= r < 8:
+                for half in range(2):
+                    piece = weights[r : r + 1, 640 * half : 640 * half + 640]
+                    out[4 * zone + d, 2 * t + half : 2 * t + half + 1, 0:640] = piece
+
+    for d in range(4):
+        rows(d)
+
+    @pl.when(zone > 0)
+    def _():
+        rows(-1)
+
+    @pl.when(zone < 3)
+    def _():
+        rows(4)
+
     lanes = iota((64, 128), 1)
     columns = jnp.zeros((64, 128), F32)
     for r in range(8):
@@ -451,75 +498,64 @@
     columns = jnp.concatenate([columns, jnp.zeros((64, 128), F32)], axis=0)
     tail = with_scalars(columns.T[0:8, :], scalars)
     for k in range(16):
-        out[k, :, 768:896] = tail
-
-    def rows(d):
-        for t in range(4):
-            r = 2 * d - 1 + t
-            if 0 <= r < 8:
-                for half in range(2):
-                    piece = values[r : r + 1, 768 * half : 768 * half + 768]
-                    out[4 * zone + d, 2 * t + half : 2 * t + half + 1, 0:768] = piece
-
-    for d in range(4):
-        rows(d)
-
-    @pl.when(zone > 0)
-    def _():
-        rows(-1)
-
-    @pl.when(zone < 3)
-    def _():
-        rows(4)
-
-
-def start_obs(zone, data_far, basis_far, out, data, basis, sem, sems):
+        out[k, :, 640:768] = tail
+
+
+def start_obs(zone, data_far, basis_far, obs, src, out, points, sources, weights, data, basis, sem, sems):
     first = pltpu.make_async_copy(data_far, data, sem)
     first.start()
     copies = [pltpu.make_async_copy(basis_far.at[r], basis.at[r], sems.at[r]) for r in range(8)]
     for copy in copies:
         copy.start()
+    others = [pltpu.make_async_copy(a, b, sems.at[k]) for k, a, b in ((8, obs, points), (9, src, sources))]
+    for copy in others:
+        copy.start()
     first.wait()
-    send_residual(zone[0], data, basis, out, (total(data[...] * data[...]),), copies)
-
-
-def gather_projected(zone, recv, basis, p):
-    tail = functools.reduce(jnp.add, [recv[k, :, 768:896] for k in range(16)])
-    columns = jnp.where(iota((8, 128), 1) < 64, tail, 0.0).T
+    send_residual(zone[0], data, basis, out, weights, (total(data[...] * data[...]),), copies)
+    for copy in others:
+        copy.wait()
+
+
+def gather_projected(zone, recv, basis, near, p):
+    tail = functools.reduce(jnp.add, [recv[k, :, 640:768] for k in range(16)])
     for r in range(8):
-        far = jnp.sum(basis[r] * columns[0:64, r : r + 1], axis=0, keepdims=True)
         for half in range(2):
-            value = far[:, 768 * half : 768 * half + 768]
+            value = 0.0
             for t in range(4):
                 if (r + 1 - t) % 2 == 0:
                     d = (r + 1 - t) // 2
-                    piece = recv[jnp.clip(4 * zone + d, 0, 15), 2 * t + half : 2 * t + half + 1, 0:768]
+                    piece = recv[jnp.clip(4 * zone + d, 0, 15), 2 * t + half : 2 * t + half + 1, 0:640]
                     if d == -1:
                         piece = jnp.where(zone > 0, piece, 0.0)
                     if d == 4:
                         piece = jnp.where(zone < 3, piece, 0.0)
                     value = value + piece
-            p[r : r + 1, 768 * half : 768 * half + 768] = value
+            near[r : r + 1, 640 * half : 640 * half + 640] = value
+    columns = jnp.where(iota((8, 128), 1) < 64, tail, 0.0).T
+    for r in range(8):
+        p[r : r + 1, :] = jnp.sum(basis[r] * columns[0:64, r : r + 1], axis=0, keepdims=True)
+    p[:, 0:1280] = p[:, 0:1280] + near[...]
+    p[:, 1280:1536] = p[:, 1280:1536] - (near[:, 0:256] + near[:, 768:1024])
     return tail
 
 
-def first_obs(zone, recv, data, basis, p, gammas, out):
+def first_obs(zone, recv, data, basis, p, gammas, out, weights):
     z = zone[0]
-    gammas[...] = gather_projected(z, recv, basis, p)
+    gammas[...] = gather_projected(z, recv, basis, weights, p)
     pv, dv = p[...], data[...]
-    send_residual(z, p, basis, out, (total(pv * pv), total(dv * pv)))
-
-
-def second_obs(zone, recv, data, p0, gamma0, sums1, basis, p, r, gammas, out):
+    send_residual(z, p, basis, out, weights, (total(pv * pv), total(dv * pv)))
+
+
+def second_obs(zone, recv, data, p0, gamma0, sums1, basis, p, r, gammas, out, weights):
     z = zone[0]
-    tail = gather_projected(z, recv, basis, p)
+    tail = gather_projected(z, recv, basis, weights, p)
     gammas[...] = tail
     g0 = lane_scalar(gamma0[...], 0)
     pv = p[...] + (lane_scalar(tail, 0) / g0) * p0[...]
     rv = data[...] - (g0 / lane_scalar(sums1[...], 0)) * p0[...]
     p[...] = pv
     r[...] = rv
-    send_residual(z, p, basis, out, (total(pv * pv), total(rv * pv)))
+    send_residual(z, p, basis, out, weights, (total(pv * pv), total(rv * pv)))
 
 
 def gather_normal(recv, basis, q):
@@ -571,8 +607,8 @@
     m0 = lane_scalar(sums0[...], 0)
     m1 = m0 - 2.0 * step0 * cross0 + step0 * step0 * curve0
     m2 = m1 - 2.0 * step1 * cross1 + step1 * step1 * curve1
-    lanes = iota((8, 128), 1)
-    misfit[...] = jnp.where(lanes == 0, m0, jnp.where(lanes == 1, m1, m2))
+    for k, value in enumerate((m0, m1, m2)):
+        misfit[k] = value[0, 0]
 
 
 VM = pl.BlockSpec(memory_space=pltpu.VMEM)
@@ -607,7 +643,7 @@
     index = lax.axis_index(SRC).astype(jnp.int32)
     column = index.reshape(1)
     zone = (index % 4).reshape(1)
-    obs_message = shape(16, 8, 896)
+    obs_message = shape(16, 8, 768)
     src_message = shape(8, 8, 384)
     row = shape(8, 128)
     dma = pltpu.SemaphoreType.DMA
@@ -615,13 +651,16 @@
     def bf(*dims):
         return shape(*dims, dtype=BF16)
 
-    (message,) = call(
+    message, points, sources = call(
         start_obs,
-        [obs_message],
-        [zone, data, obs_basis],
+        [obs_message, shape(3, 128, 256), shape(3, 64, 256)],
+        [
+            zone, data, obs_basis,
+            jnp.transpose(obs_points, (1, 0, 2)), jnp.transpose(src_points, (1, 0, 2)),
+        ],
         scalars=1,
-        far=(1, 2),
-        scratch=[pltpu.VMEM((8, 1536), F32), pltpu.VMEM((8, 64, 1536), F32), dma, dma((8,))],
+        far=(1, 2, 3, 4),
+        scratch=[pltpu.VMEM((8, 1280), F32), pltpu.VMEM((8, 1536), F32), pltpu.VMEM((8, 64, 1536), F32), dma, dma((10,))],
         limit=LIMIT0,
     )
     received = exchange(message, SRC)
@@ -632,24 +671,22 @@
             bf(128, 16), bf(16, 128), bf(64, 128), bf(128, 64), bf(128, 384), bf(64, 384),
         ],
         [
-            column, near_pairs.reshape(1, 72), far_pairs.reshape(1, 320),
-            jnp.transpose(obs_points, (1, 0, 2)), jnp.transpose(src_points, (1, 0, 2)),
+            column, near_pairs.reshape(1, 72), far_pairs.reshape(1, 320), points, sources,
         ],
         scalars=1,
-        far=(1, 2, 3, 4),
+        far=(1, 2),
         out_specs=[FAR] * 2 + [VM] + [SM] + [VM] * 6,
         scratch=[
             pltpu.SMEM((1, 72), jnp.int32), pltpu.VMEM((1, 72), jnp.int32), pltpu.VMEM((1, 320), jnp.int32),
-            pltpu.VMEM((1, 128), jnp.int32), pltpu.VMEM((1, 384), jnp.int32), pltpu.VMEM((3, 128, 256), F32),
-            pltpu.VMEM((3, 64, 256), F32), pltpu.VMEM((64, 256), F32), pltpu.VMEM((64, 256), F32),
-            pltpu.VMEM((2, 2, 8, 256, 256), BF16), dma((5,)), dma((2, 2)),
+            pltpu.VMEM((1, 128), jnp.int32), pltpu.VMEM((1, 384), jnp.int32), pltpu.VMEM((64, 256), F32), pltpu.VMEM((64, 256), F32),
+            pltpu.VMEM((2, 2, 8, 256, 256), BF16), dma((3,)), dma((2, 2, 2)),
         ],
         limit=LIMIT0,
     )
     matrices = jnp.transpose(couplings[0, 0], (1, 2, 0))
     matrix_scratch = [pltpu.VMEM((64, 64, 320), F32), dma]
     adjoint_scratch = [
-        pltpu.VMEM((16, 1536), F32), pltpu.VMEM((80, 1536), F32), pltpu.VMEM((2, 80 * ROWS, 128), F32),
+        pltpu.VMEM((16, 1280), F32), pltpu.VMEM((80, 1280), F32), pltpu.VMEM((2, 80 * ROWS, 128), F32),
         pltpu.VMEM((2, 80 * ROWS, 128), F32), pltpu.VMEM((128, 256), F32), pltpu.VMEM((128, 384), F32),
         pltpu.VMEM((64, 384), F32), *matrix_scratch,
     ]
@@ -659,7 +696,7 @@
         [count, column, received, kh_far, kl_far, pq, oo, ost, fot, fst, matrices],
         scalars=2,
         far=(3, 4, 10),
-        scratch=[*adjoint_scratch, dma((2, 9))],
+        scratch=[*adjoint_scratch, dma((2, 2, 9))],
         limit=LIMIT,
     )
     received = exchange(out.reshape(8, 8, 384), OBS)
@@ -685,7 +722,7 @@
             far=(10,),
             scratch=[
                 pltpu.VMEM((80, 256), F32), pltpu.VMEM((2, 80 * ROWS, 128), F32), pltpu.VMEM((2, 80 * ROWS, 128), F32),
-                pltpu.VMEM((128, 1536), F32), pltpu.VMEM((16, 1536), F32), pltpu.VMEM((128, 384), F32),
+                pltpu.VMEM((128, 1280), F32), pltpu.VMEM((16, 1280), F32), pltpu.VMEM((128, 384), F32),
                 *matrix_scratch,
             ],
             limit=LIMIT,
@@ -695,7 +732,8 @@
     plane, line = shape(8, 1536), shape(8, 256)
     n0, sums0, message = call(first_src, [line, row, src_message], [received, src_basis])
     p0, gamma0, message = call(
-        first_obs, [plane, row, obs_message], [zone, forward(message), data, obs_basis], scalars=1
+        first_obs, [plane, row, obs_message], [zone, forward(message), data, obs_basis], scalars=1,
+        scratch=[pltpu.VMEM((8, 1280), F32)],
     )
     n1, sums1, message = call(
         second_src, [line, row, src_message], [adjoint(exchange(message, SRC)), src_basis, n0, gamma0]
@@ -705,13 +743,15 @@
         [plane, plane, row, obs_message],
         [zone, forward(message), data, p0, gamma0, sums1, obs_basis],
         scalars=1,
+        scratch=[pltpu.VMEM((8, 1280), F32)],
     )
     found, residual, normal, misfit = call(
         last_src,
-        [line, plane, line, row],
+        [line, plane, line, shape(3)],
         [adjoint(exchange(message, SRC)), src_basis, n0, n1, gamma0, gamma1, sums0, sums1, r1, p1],
-    )
-    return found, residual, normal, misfit[0, 0:3]
+        out_specs=[VM] * 3 + [SM],
+    )
+    return found, residual, normal, misfit
 
 
 def solution(mesh):

time: 155 us -> 152 us (0.981)
  blocking collectives: 104 us -> 102 us
    all_to_all x9, blocking collectives: 104 us -> 102 us  [exchange(): return lax.all_to_all(value, axes, split_axis=0, concat_axis=0, tiled=True)]
where the time goes in v4:
time: 152 us; the launch traced here: 151 us
  blocking collectives  102 us (67%)
  Pallas kernels  37.7 us (25%)
  starting transfers between devices  8.42 us (6%)
    all_to_all x9, blocking collectives, exchange(): return lax.all_to_all(value, axes, split_axis=0, concat_axis=0, tiled=True)  102 us
    pallas_call x12, Pallas kernels, call(): pl.pallas_call(kernel, out_shape=outs, in_specs=specs, out_specs=out_spec...  37.7 us
    all_to_all x1, starting transfers between devices, exchange(): return lax.all_to_all(value, axes, split_axis=0, concat_axis=0, tiled=True)  8.42 us
  transfers between devices with their start and end apart: 1, of which 1 were waited for; matrix products, arithmetic and copies ran while one was open for 0% of the time, Pallas kernels for 5%

profile of v4, /device:TPU:1, one launch (start us, length us, event | category | flops | bytes accessed | tf_op | source)
XLA Modules:
  0.0 150.7 jit_solution(9650343604428462489)
XLA Ops:
  0.6 3.7 %shard_map.111 = (f32[16,8,768]{2,1,0:T(8,128)}, f32[3,128,256]{2,1,0:T(8,128)S(1)}, f32[3,64,256]{2,1,0:T(8,128)S(1)}) custom-call(s32[1]{0:T(128)} %bitcast.3.zone, f32[8,1536]{1,0:T(8,128)} %data.3, f32[8,64,1536]{2,1,0:T(8,128)} %basis.8, f32[3,128,256]{2,1,0:T(8,128)} %bitcast.24, f32[3,64,256]{2,1,0:T(8,128)} %bitcast.25), custom_call_target="tpu_custom_call" | custom-call | tf_op jit(solution)/shard_map/pallas_call | solution.py:628
  4.4 8.4 %all-to-all-start = ((f32[16,8,768]{2,1,0:T(8,128)}), f32[16,8,768]{2,1,0:T(8,128)S(1)}, u32[]{:S(2)}, u32[]{:S(2)}) async-start(f32[16,8,768]{2,1,0:T(8,128)} %get-tuple-element.36), calls=%async_computation | async-start | bytes 786432 | tf_op jit(solution)/shard_map/all_to_all | solution.py:639
  12.8 6.9 %shard_map.112 = (bf16[72,256,256]{2,1,0:T(8,128)(2,1)}, bf16[72,256,256]{2,1,0:T(8,128)(2,1)}, f32[6,72,256]{2,1,0:T(8,128)S(1)}, s32[2]{0:T(128)S(1)}, bf16[12...) custom-call(s32[1]{0:T(128)} %bitcast.column, ...), custom_call_target="tpu_custom_call" | custom-call | tf_op jit(solution)/shard_map/pallas_call | solution.py:628
  19.7 1.4 all-to-all-done.recv
  21.1 0.0 copy-start.1
  21.1 5.9 %shard_map.113 = (f32[64,384]{1,0:T(8,128)S(1)}, bf16[72,256,256]{2,1,0:T(8,128)(2,1)S(1)}, bf16[72,256,256]{2,1,0:T(8,128)(2,1)S(1)}) custom-call(s32[2]{0:T(128)S(1)} %get-tuple-element.35.count, s32[1]{0:T(128)} %bitcast.column, f32[16,8,768]{2,1,0:T(8,128)S(1)} %all-to-all-done.recv, bf16[72,256,256]{2,1,0:T(8,128)(2,1)} %get-tuple-element.37.kh_far, ...), custom_call_target="tpu_custom_call" | custom-call | tf_op jit(solution)/shard_map/pallas_call | solution.py:628
  27.0 12.2 %all_to_all.50.recv = f32[8,8,384]{2,1,0:T(8,128)S(1)} all-to-all(f32[8,8,384]{2,1,0:T(8,128)S(1)} %bitcast.18), channel_id=1, replica_groups=mesh['obs_0'=4,'obs_1'=2,'src_0'=4,'src_1'=4] {'obs_0','obs_1'}, dimensions={0} | all-to-all | bytes 196608 | tf_op jit(solution)/shard_map/all_to_all | solution.py:639
  39.2 0.0 copy-done.1
  39.2 0.5 shard_map.114
  39.7 8.2 %all_to_all.51 = f32[8,8,384]{2,1,0:T(8,128)S(1)} all-to-all(f32[8,8,384]{2,1,0:T(8,128)S(1)} %get-tuple-element.45), channel_id=1, replica_groups=mesh['obs_0'=4,'obs_1'=2,'src_0'=4,'src_1'=4] {'obs_0','obs_1'}, dimensions={0} | all-to-all | bytes 196608 | tf_op jit(solution)/shard_map/all_to_all | solution.py:639
  47.8 0.0 copy-start
  47.8 0.0 copy-start.2
  47.8 4.9 %shard_map.115 = f32[16,8,768]{2,1,0:T(8,128)S(1)} custom-call(s32[2]{0:T(128)S(1)} %get-tuple-element.35.count, s32[1]{0:T(128)} %bitcast.column, f32[64,384]{1,0:T(8,128)S(1)} %bitcast.15, bf16[72,256,256]{2,1,0:T(8,128)(2,1)S(1)} %get-tuple-element.46.kh, bf16[72,256,256]{2,1,0:T(8,128)(2,1)S(1)} %get-tuple-element.47.kl, ...), custom_call_target="tpu_custom_call" | custom-call | tf_op jit(solution)/shard_map/pallas_call | solution.py:628
  52.7 16.4 %all_to_all.52.recv = f32[16,8,768]{2,1,0:T(8,128)S(1)} all-to-all(f32[16,8,768]{2,1,0:T(8,128)S(1)} %shard_map.115), channel_id=1, replica_groups=mesh['obs_0'=4,'obs_1'=2,'src_0'=4,'src_1'=4] {'src_0','src_1'}, dimensions={0} | all-to-all | bytes 786432 | tf_op jit(solution)/shard_map/all_to_all | solution.py:639
  69.1 0.0 copy-done
  69.1 0.0 copy-done.2
  69.1 1.1 shard_map.116
  70.2 11.2 %all_to_all.53.recv = f32[16,8,768]{2,1,0:T(8,128)S(1)} all-to-all(f32[16,8,768]{2,1,0:T(8,128)S(1)} %get-tuple-element.50), channel_id=1, replica_groups=mesh['obs_0'=4,'obs_1'=2,'src_0'=4,'src_1'=4] {'src_0','src_1'}, dimensions={0} | all-to-all | bytes 786432 | tf_op jit(solution)/shard_map/all_to_all | solution.py:639
  81.4 3.7 %shard_map.117 = f32[64,384]{1,0:T(8,128)S(1)} custom-call(s32[2]{0:T(128)S(1)} %get-tuple-element.35.count, s32[1]{0:T(128)} %bitcast.column, f32[16,8,768]{2,1,0:T(8,128)S(1)} %all_to_all.53.recv, bf16[72,256,256]{2,1,0:T(8,128)(2,1)S(1)} %get-tuple-element.46.kh, bf16[72,256,256]{2,1,0:T(8,128)(2,1)S(1)} %get-tuple-element.47.kl, ...), custom_call_target="tpu_custom_call" | custom-call | tf_op jit(solution)/shard_map/pallas_call | solution.py:628
  85.1 10.3 %all_to_all.54.recv = f32[8,8,384]{2,1,0:T(8,128)S(1)} all-to-all(f32[8,8,384]{2,1,0:T(8,128)S(1)} %bitcast.17), channel_id=1, replica_groups=mesh['obs_0'=4,'obs_1'=2,'src_0'=4,'src_1'=4] {'obs_0','obs_1'}, dimensions={0} | all-to-all | bytes 196608 | tf_op jit(solution)/shard_map/all_to_all | solution.py:639
  95.4 0.5 shard_map.118
  95.9 8.2 %all_to_all.55 = f32[8,8,384]{2,1,0:T(8,128)S(1)} all-to-all(f32[8,8,384]{2,1,0:T(8,128)S(1)} %get-tuple-element.53), channel_id=1, replica_groups=mesh['obs_0'=4,'obs_1'=2,'src_0'=4,'src_1'=4] {'obs_0','obs_1'}, dimensions={0} | all-to-all | bytes 196608 | tf_op jit(solution)/shard_map/all_to_all | solution.py:639
  104.1 4.9 %shard_map.119 = f32[16,8,768]{2,1,0:T(8,128)S(1)} custom-call(s32[2]{0:T(128)S(1)} %get-tuple-element.35.count, s32[1]{0:T(128)} %bitcast.column, f32[64,384]{1,0:T(8,128)S(1)} %bitcast.16, bf16[72,256,256]{2,1,0:T(8,128)(2,1)S(1)} %get-tuple-element.46.kh, bf16[72,256,256]{2,1,0:T(8,128)(2,1)S(1)} %get-tuple-element.47.kl, ...), custom_call_target="tpu_custom_call" | custom-call | tf_op jit(solution)/shard_map/pallas_call | solution.py:628
  109.0 13.0 %all_to_all.56.recv = f32[16,8,768]{2,1,0:T(8,128)S(1)} all-to-all(f32[16,8,768]{2,1,0:T(8,128)S(1)} %shard_map.119), channel_id=1, replica_groups=mesh['obs_0'=4,'obs_1'=2,'src_0'=4,'src_1'=4] {'src_0','src_1'}, dimensions={0} | all-to-all | bytes 786432 | tf_op jit(solution)/shard_map/all_to_all | solution.py:639
  122.0 1.0 shard_map.120
  123.0 11.5 %all_to_all.57.recv = f32[16,8,768]{2,1,0:T(8,128)S(1)} all-to-all(f32[16,8,768]{2,1,0:T(8,128)S(1)} %get-tuple-element.56), channel_id=1, replica_groups=mesh['obs_0'=4,'obs_1'=2,'src_0'=4,'src_1'=4] {'src_0','src_1'}, dimensions={0} | all-to-all | bytes 786432 | tf_op jit(solution)/shard_map/all_to_all | solution.py:639
  134.5 3.7 %shard_map.121 = f32[64,384]{1,0:T(8,128)S(1)} custom-call(s32[2]{0:T(128)S(1)} %get-tuple-element.35.count, s32[1]{0:T(128)} %bitcast.column, f32[16,8,768]{2,1,0:T(8,128)S(1)} %all_to_all.57.recv, bf16[72,256,256]{2,1,0:T(8,128)(2,1)S(1)} %get-tuple-element.46.kh, bf16[72,256,256]{2,1,0:T(8,128)(2,1)S(1)} %get-tuple-element.47.kl, ...), custom_call_target="tpu_custom_call" | custom-call | tf_op jit(solution)/shard_map/pallas_call | solution.py:628
  138.2 11.6 %all_to_all.58.recv = f32[8,8,384]{2,1,0:T(8,128)S(1)} all-to-all(f32[8,8,384]{2,1,0:T(8,128)S(1)} %bitcast.14), channel_id=1, replica_groups=mesh['obs_0'=4,'obs_1'=2,'src_0'=4,'src_1'=4] {'obs_0','obs_1'}, dimensions={0} | all-to-all | bytes 196608 | tf_op jit(solution)/shard_map/all_to_all | solution.py:639
  149.8 0.9 shard_map.122
Async XLA Ops:
  4.4 16.7 %all-to-all-start = ((f32[16,8,768]{2,1,0:T(8,128)}), f32[16,8,768]{2,1,0:T(8,128)S(1)}, u32[]{:S(2)}, u32[]{:S(2)}) async-start(f32[16,8,768]{2,1,0:T(8,128)} %get-tuple-element.36), calls=%async_computation | async-start | bytes 786432 | tf_op jit(solution)/shard_map/all_to_all | solution.py:639
  21.1 18.1 %copy-start.1 = (f32[8,64,256]{2,1,0:T(8,128)S(1)}, f32[8,64,256]{2,1,0:T(8,128)}, u32[]{:S(2)}) copy-start(f32[8,64,256]{2,1,0:T(8,128)} %basis.9) | copy-start | bytes 1572868
  47.8 21.3 %copy-start = (f32[8,64,1536]{2,1,0:T(8,128)S(1)}, f32[8,64,1536]{2,1,0:T(8,128)}, u32[]{:S(2)}) copy-start(f32[8,64,1536]{2,1,0:T(8,128)} %basis.8) | copy-start | bytes 9437188
  47.8 21.3 %copy-start.2 = (f32[8,1536]{1,0:T(8,128)S(1)}, f32[8,1536]{1,0:T(8,128)}, u32[]{:S(2)}) copy-start(f32[8,1536]{1,0:T(8,128)} %data.3) | copy-start | bytes 147460

commit v5 on v4

--- a/solution.py
+++ b/solution.py
@@ -19,7 +19,7 @@
 ROWS = 16
 MIB = 1 << 20
 LIMIT0 = 8
-LIMIT = 18
+LIMIT = 10
 
 
 def split(value):
@@ -207,51 +207,36 @@
         act(pltpu.make_async_copy(c, matrices, sem))
 
 
-def far_forward(n, x, pick, place, c, terms):
-    v = far_inputs(x, pick)
-    terms[...] = jnp.zeros_like(terms)
-
-    def part(lanes):
-        def eight(g, carry):
-            rows = [jnp.sum(c[8 * g + b, :, lanes] * v[:, lanes], axis=0, keepdims=True) for b in range(8)]
-            terms[pl.ds(pl.multiple_of(8 * g, 8), 8), lanes] = jnp.concatenate(rows, axis=0)
+def far_forward_group(g, c, lanes, terms, held):
+    v = held[:, lanes]
+    rows = [jnp.sum(c[8 * g + b, :, lanes] * v, axis=0, keepdims=True) for b in range(8)]
+    terms[pl.ds(pl.multiple_of(8 * g, 8), 8), lanes] = jnp.concatenate(rows, axis=0)
+
+
+def far_adjoint_group(g, c, lanes, terms, held):
+    rows = held[pl.ds(pl.multiple_of(8 * g, 8), 8), lanes.start : (lanes.stop + 127) // 128 * 128]
+    value = terms[0:64, lanes]
+    for b in range(8):
+        value = value + c[8 * g + b, :, lanes] * rows[b : b + 1, 0 : lanes.stop - lanes.start]
+    terms[0:64, lanes] = value
+
+
+def far_rest(first, n, group, c, terms, held):
+    def some(lanes, first):
+        def one(g, carry):
+            group(g, c, lanes, terms, held)
             return carry
 
-        lax.fori_loop(0, 8, eight, 0)
-
-    part(slice(0, WIDE))
+        lax.fori_loop(first, 8, one, 0)
+
+    some(slice(0, WIDE), first)
 
     @pl.when(n > WIDE)
     def _():
-        part(slice(WIDE, 320))
-
-    return far_outputs(terms[...], place)
-
-
-def far_adjoint(n, x, pick, place, c, terms, held):
-    held[...] = far_inputs(x, pick)
-    terms[...] = jnp.zeros_like(terms)
-
-    def part(lanes):
-        def eight(g, carry):
-            rows = held[pl.ds(pl.multiple_of(8 * g, 8), 8), lanes.start : (lanes.stop + 127) // 128 * 128]
-            for b in range(8):
-                carry = carry + c[8 * g + b, :, lanes] * rows[b : b + 1, 0 : lanes.stop - lanes.start]
-            return carry
-
-        zeros = jnp.zeros((64, lanes.stop - lanes.start), F32)
-        terms[0:64, lanes] = lax.fori_loop(0, 8, eight, zeros)
-
-    part(slice(0, WIDE))
-
-    @pl.when(n > WIDE)
-    def _():
-        part(slice(WIDE, 320))
-
-    return far_outputs(terms[...], place)
-
-
-def near_products(n, moments, results, kh, kl, forward, arrive=None):
+        some(slice(WIDE, 320), 0)
+
+
+def near_products(n, moments, results, kh, kl, forward, arrive=None, beside=None):
     def four(first):
         for b in range(4):
             t = first + b
@@ -259,7 +244,7 @@
             high, low = split(jnp.concatenate([moments[0, at, :], moments[1, at, :]], axis=1))
             both = jnp.concatenate([high, low], axis=0)
             if forward:
-                both = (mm_nt(kh[t], both) + mm_nt(kl[t], both)).T
+                both = mm_nt(both, kh[t]) + mm_nt(both, kl[t])
             else:
                 both = mm(both, kh[t]) + mm(both, kl[t])
             both = both[:ROWS] + both[ROWS:]
@@ -271,11 +256,21 @@
             arrive(g, 0)
             arrive(g, 1)
         four(8 * g)
+        if beside is not None:
+            beside(g)
         four(8 * g + 4)
         return carry
 
     whole = lax.shift_right_logical(n, 3)
-    lax.fori_loop(0, whole, eight, 0)
+    lax.fori_loop(0, jnp.minimum(whole, 8), eight, 0)
+
+    @pl.when(whole == 9)
+    def _():
+        if arrive is not None:
+            arrive(8, 0)
+            arrive(8, 1)
+        four(64)
+        four(68)
 
     @pl.when((n & 7) > 0)
     def _():
@@ -302,8 +297,8 @@
 
 
 def first_adjoint_block(
-    count, column, recv, kh_far, kl_far, pq, oo, ost, fot, fst, c, out, kh, kl,
-    yb, yp, moments, results, values, terms, held, matrices, sem, sems
+    count, column, recv, kh_far, kl_far, pq, oo, ost, fot, fst, matrices, out, kh, kl, c,
+    yb, yp, moments, results, values, terms, held, sem, sems
 ):
     n = count[0]
 
@@ -328,20 +323,18 @@
         for copy in arriving(g, part):
             copy.wait()
 
-    far_copies(count[1], c, matrices, sem, lambda copy: copy.start())
+    far_copies(count[1], matrices, c, sem, lambda copy: copy.start())
     lax.fori_loop(0, lax.shift_right_logical(n + 7, 3), start, 0)
     adjoint_block(
         count, column, recv, kh, kl, pq, oo, ost, fot, fst, c, out,
-        yb, yp, moments, results, values, terms, held, matrices, sem, arrive=arrive
+        yb, yp, moments, results, values, terms, held, matrices, sem, arrive
     )
 
 
 def adjoint_block(
     count, column, recv, kh, kl, pq, oo, ost, fot, fst, c, out,
-    yb, yp, moments, results, values, terms, held, matrices, sem, arrive=None
+    yb, yp, moments, results, values, terms, held, matrices=None, sem=None, arrive=None
 ):
-    if arrive is None:
-        far_copies(count[1], c, matrices, sem, lambda copy: copy.start())
     n = count[0]
     j = column[0]
     for t in range(4):
@@ -374,18 +367,24 @@
 
     lax.fori_loop(0, groups, enter, 0)
     tails = [recv[k, :, 640:768] for k in range(16)]
-
-    def far():
-        far_copies(count[1], c, matrices, sem, lambda copy: copy.wait())
-        coeffs = far_adjoint(count[1], jnp.concatenate(tails, axis=0), fot[...], fst[...], matrices, terms, held)
-        sums = functools.reduce(jnp.add, tails)
-        for k in range(8):
-            part = coeffs[8 * k : 8 * k + 8]
-            out[8 * k : 8 * k + 8, 256:384] = jnp.where(iota((8, 128), 1) < 64, part, sums)
-
-    if arrive is not None:
-        far()
-    near_products(n, moments, results, kh, kl, False, arrive)
+    held[...] = far_inputs(jnp.concatenate(tails, axis=0), fot[...])
+    terms[...] = jnp.zeros_like(terms)
+
+    def beside(g):
+        far_adjoint_group(g, c, slice(0, WIDE), terms, held)
+
+    if arrive is None:
+        near_products(n, moments, results, kh, kl, False, None, beside)
+        far_rest(lax.shift_right_logical(n, 3), count[1], far_adjoint_group, c, terms, held)
+    else:
+        far_copies(count[1], matrices, c, sem, lambda copy: copy.wait())
+        far_rest(0, count[1], far_adjoint_group, c, terms, held)
+        near_products(n, moments, results, kh, kl, False, arrive)
+    coeffs = far_outputs(terms[...], fst[...])
+    sums = functools.reduce(jnp.add, tails)
+    for k in range(8):
+        part = coeffs[8 * k : 8 * k + 8]
+        out[8 * k : 8 * k + 8, 256:384] = jnp.where(iota((8, 128), 1) < 64, part, sums)
 
     def leave(g, carry):
         at = pl.ds(pl.multiple_of(g * 8, 8), 8)
@@ -398,16 +397,13 @@
 
     lax.fori_loop(0, groups, leave, 0)
     high, low = split(values[...])
-    out[:, 0:256] = mm(ost[...], high) + mm(ost[...], low)
-    if arrive is None:
-        far()
+    out[:, 0:256] = mm(ost[:, 0:80], high) + mm(ost[:, 0:80], low)
 
 
 def forward_block(
     count, column, recv, kh, kl, pq, os, oot, fot, fst, c, out,
-    xp, moments, results, values, yb, terms, matrices, sem
+    xp, moments, results, values, yb, terms, held
 ):
-    far_copies(count[1], c, matrices, sem, lambda copy: copy.start())
     n = count[0]
     j = column[0]
     high, low = split(recv[:, 0:256])
@@ -426,7 +422,13 @@
         return carry
 
     lax.fori_loop(0, groups, enter, 0)
-    near_products(n, moments, results, kh, kl, True)
+    held[...] = far_inputs(recv[:, 256:384], fst[...])
+    terms[...] = jnp.zeros_like(terms)
+    near_products(
+        n, moments, results, kh, kl, True, None,
+        lambda g: far_forward_group(g, c, slice(0, WIDE), terms, held),
+    )
+    far_rest(lax.shift_right_logical(n, 3), count[1], far_forward_group, c, terms, held)
 
     def leave(g, carry):
         at = pl.ds(pl.multiple_of(g * 8, 8), 8)
@@ -448,7 +450,7 @@
 
     lax.fori_loop(0, groups, leave, 0)
     high, low = split(values[...])
-    yb[...] = mm(oot[...], high) + mm(oot[...], low)
+    yb[...] = mm(oot[:, 0:80], high) + mm(oot[:, 0:80], low)
     for t in range(4):
         holder = lax.shift_right_logical(jnp.clip(2 * j - 1 + t, 0, 31), 3)
         for row in range(4):
@@ -456,8 +458,7 @@
                 piece = yb[4 * row + t : 4 * row + t + 1, 640 * half : 640 * half + 640]
                 out[row * 4 + holder, 2 * t + half : 2 * t + half + 1, 0:640] = piece
     tails = [recv[8 * k : 8 * k + 8, 256:384] for k in range(8)]
-    far_copies(count[1], c, matrices, sem, lambda copy: copy.wait())
-    coeffs = far_forward(count[1], recv[:, 256:384], fst[...], fot[...], matrices, terms)
+    coeffs = far_outputs(terms[...], fot[...])
     sums = functools.reduce(jnp.add, tails)
     for k in range(16):
         out[k, :, 640:768] = jnp.where(iota((8, 128), 1) < 64, coeffs[8 * k : 8 * k + 8], sums)
@@ -684,19 +685,18 @@
         limit=LIMIT0,
     )
     matrices = jnp.transpose(couplings[0, 0], (1, 2, 0))
-    matrix_scratch = [pltpu.VMEM((64, 64, 320), F32), dma]
     adjoint_scratch = [
         pltpu.VMEM((16, 1280), F32), pltpu.VMEM((80, 1280), F32), pltpu.VMEM((2, 80 * ROWS, 128), F32),
-        pltpu.VMEM((2, 80 * ROWS, 128), F32), pltpu.VMEM((128, 256), F32), pltpu.VMEM((128, 384), F32),
-        pltpu.VMEM((64, 384), F32), *matrix_scratch,
+        pltpu.VMEM((2, 80 * ROWS, 128), F32), pltpu.VMEM((80, 256), F32), pltpu.VMEM((128, 384), F32),
+        pltpu.VMEM((64, 384), F32),
     ]
-    out, kh, kl = call(
+    out, kh, kl, held = call(
         first_adjoint_block,
-        [shape(64, 384), bf(PAIRS, 256, 256), bf(PAIRS, 256, 256)],
+        [shape(64, 384), bf(PAIRS, 256, 256), bf(PAIRS, 256, 256), shape(64, 64, 320)],
         [count, column, received, kh_far, kl_far, pq, oo, ost, fot, fst, matrices],
         scalars=2,
         far=(3, 4, 10),
-        scratch=[*adjoint_scratch, dma((2, 2, 9))],
+        scratch=[*adjoint_scratch, dma, dma((2, 2, 9))],
         limit=LIMIT,
     )
     received = exchange(out.reshape(8, 8, 384), OBS)
@@ -705,9 +705,8 @@
         (out,) = call(
             adjoint_block,
             [shape(64, 384)],
-            [count, column, message, kh, kl, pq, oo, ost, fot, fst, matrices],
+            [count, column, message, kh, kl, pq, oo, ost, fot, fst, held],
             scalars=2,
-            far=(10,),
             scratch=adjoint_scratch,
             limit=LIMIT,
         )
@@ -717,13 +716,12 @@
         (out,) = call(
             forward_block,
             [obs_message],
-            [count, column, exchange(message, OBS).reshape(64, 384), kh, kl, pq, os, oot, fot, fst, matrices],
+            [count, column, exchange(message, OBS).reshape(64, 384), kh, kl, pq, os, oot, fot, fst, held],
             scalars=2,
-            far=(10,),
             scratch=[
                 pltpu.VMEM((80, 256), F32), pltpu.VMEM((2, 80 * ROWS, 128), F32), pltpu.VMEM((2, 80 * ROWS, 128), F32),
-                pltpu.VMEM((128, 1280), F32), pltpu.VMEM((16, 1280), F32), pltpu.VMEM((128, 384), F32),
-                *matrix_scratch,
+                pltpu.VMEM((80, 1280), F32), pltpu.VMEM((16, 1280), F32), pltpu.VMEM((128, 384), F32),
+                pltpu.VMEM((64, 384), F32),
             ],
             limit=LIMIT,
         )

time: 152 us -> 150 us (0.987)
    all_to_all x9, blocking collectives: 102 us -> 101 us  [exchange(): return lax.all_to_all(value, axes, split_axis=0, concat_axis=0, tiled=True)]
where the time goes in v5:
time: 150 us
  blocking collectives  101 us (67%)
  Pallas kernels  39 us (26%)
  starting transfers between devices  8.42 us (6%)
    all_to_all x9, blocking collectives, exchange(): return lax.all_to_all(value, axes, split_axis=0, concat_axis=0, tiled=True)  101 us
    pallas_call x12, Pallas kernels, call(): pl.pallas_call(kernel, out_shape=outs, in_specs=specs, out_specs=out_spec...  39 us
    all_to_all x1, starting transfers between devices, exchange(): return lax.all_to_all(value, axes, split_axis=0, concat_axis=0, tiled=True)  8.42 us
  transfers between devices with their start and end apart: 1, of which 1 were waited for; matrix products, arithmetic and copies ran while one was open for 0% of the time, Pallas kernels for 5%

profile of v5, /device:TPU:1, one launch (start us, length us, event | category | flops | bytes accessed | tf_op | source)
XLA Modules:
  0.0 149.6 jit_solution(11418611617263740409)
XLA Ops:
  0.6 3.7 %shard_map.111 = (f32[16,8,768]{2,1,0:T(8,128)}, f32[3,128,256]{2,1,0:T(8,128)S(1)}, f32[3,64,256]{2,1,0:T(8,128)S(1)}) custom-call(s32[1]{0:T(128)} %bitcast.3.zone, f32[8,1536]{1,0:T(8,128)} %data.3, f32[8,64,1536]{2,1,0:T(8,128)} %basis.8, f32[3,128,256]{2,1,0:T(8,128)} %bitcast.20, f32[3,64,256]{2,1,0:T(8,128)} %bitcast.21), custom_call_target="tpu_custom_call" | custom-call | tf_op jit(solution)/shard_map/pallas_call | solution.py:629
  4.4 8.4 %all-to-all-start = ((f32[16,8,768]{2,1,0:T(8,128)}), f32[16,8,768]{2,1,0:T(8,128)S(1)}, u32[]{:S(2)}, u32[]{:S(2)}) async-start(f32[16,8,768]{2,1,0:T(8,128)} %get-tuple-element.37), calls=%async_computation | async-start | bytes 786432 | tf_op jit(solution)/shard_map/all_to_all | solution.py:640
  12.8 7.5 %shard_map.112 = (bf16[72,256,256]{2,1,0:T(8,128)(2,1)}, bf16[72,256,256]{2,1,0:T(8,128)(2,1)}, f32[6,72,256]{2,1,0:T(8,128)S(1)}, s32[2]{0:T(128)S(1)}, bf16[12...) custom-call(s32[1]{0:T(128)} %bitcast.column, ...), custom_call_target="tpu_custom_call" | custom-call | tf_op jit(solution)/shard_map/pallas_call | solution.py:629
  20.4 0.8 all-to-all-done.recv
  21.1 0.0 copy-start.1
  21.1 6.4 %shard_map.113 = (f32[64,384]{1,0:T(8,128)S(1)}, bf16[72,256,256]{2,1,0:T(8,128)(2,1)S(1)}, bf16[72,256,256]{2,1,0:T(8,128)(2,1)S(1)}, f32[64,64,320]{2,1,0:T(8,128)S(1)}) custom-call(s32[2]{0:T(128)S(1)} %get-tuple-element.36.count, s32[1]{0:T(128)} %bitcast.column, f32[16,8,768]{2,1,0:T(8,128)S(1)} %all-to-all-done.recv, ...), custom_call_target="tpu_custom_call" | custom-call | tf_op jit(solution)/shard_map/pallas_call | solution.py:629
  27.5 11.6 %all_to_all.50.recv = f32[8,8,384]{2,1,0:T(8,128)S(1)} all-to-all(f32[8,8,384]{2,1,0:T(8,128)S(1)} %bitcast.18), channel_id=1, replica_groups=mesh['obs_0'=4,'obs_1'=2,'src_0'=4,'src_1'=4] {'obs_0','obs_1'}, dimensions={0} | all-to-all | bytes 196608 | tf_op jit(solution)/shard_map/all_to_all | solution.py:640
  39.0 0.0 copy-done.1
  39.1 0.5 shard_map.114
  39.5 8.2 %all_to_all.51 = f32[8,8,384]{2,1,0:T(8,128)S(1)} all-to-all(f32[8,8,384]{2,1,0:T(8,128)S(1)} %get-tuple-element.46), channel_id=1, replica_groups=mesh['obs_0'=4,'obs_1'=2,'src_0'=4,'src_1'=4] {'obs_0','obs_1'}, dimensions={0} | all-to-all | bytes 196608 | tf_op jit(solution)/shard_map/all_to_all | solution.py:640
  47.7 0.0 copy-start
  47.7 0.0 copy-start.2
  47.7 4.7 %shard_map.115 = f32[16,8,768]{2,1,0:T(8,128)S(1)} custom-call(s32[2]{0:T(128)S(1)} %get-tuple-element.36.count, s32[1]{0:T(128)} %bitcast.column, f32[64,384]{1,0:T(8,128)S(1)} %bitcast.15, bf16[72,256,256]{2,1,0:T(8,128)(2,1)S(1)} %get-tuple-element.47.kh, bf16[72,256,256]{2,1,0:T(8,128)(2,1)S(1)} %get-tuple-element.48.kl, ...), custom_call_target="tpu_custom_call" | custom-call | tf_op jit(solution)/shard_map/pallas_call | solution.py:629
  52.4 15.1 %all_to_all.52.recv = f32[16,8,768]{2,1,0:T(8,128)S(1)} all-to-all(f32[16,8,768]{2,1,0:T(8,128)S(1)} %shard_map.115), channel_id=1, replica_groups=mesh['obs_0'=4,'obs_1'=2,'src_0'=4,'src_1'=4] {'src_0','src_1'}, dimensions={0} | all-to-all | bytes 786432 | tf_op jit(solution)/shard_map/all_to_all | solution.py:640
  67.6 0.0 copy-done
  67.6 0.0 copy-done.2
  67.6 1.1 shard_map.116
  68.6 11.7 %all_to_all.53.recv = f32[16,8,768]{2,1,0:T(8,128)S(1)} all-to-all(f32[16,8,768]{2,1,0:T(8,128)S(1)} %get-tuple-element.52), channel_id=1, replica_groups=mesh['obs_0'=4,'obs_1'=2,'src_0'=4,'src_1'=4] {'src_0','src_1'}, dimensions={0} | all-to-all | bytes 786432 | tf_op jit(solution)/shard_map/all_to_all | solution.py:640
  80.4 4.0 %shard_map.117 = f32[64,384]{1,0:T(8,128)S(1)} custom-call(s32[2]{0:T(128)S(1)} %get-tuple-element.36.count, s32[1]{0:T(128)} %bitcast.column, f32[16,8,768]{2,1,0:T(8,128)S(1)} %all_to_all.53.recv, bf16[72,256,256]{2,1,0:T(8,128)(2,1)S(1)} %get-tuple-element.47.kh, bf16[72,256,256]{2,1,0:T(8,128)(2,1)S(1)} %get-tuple-element.48.kl, ...), custom_call_target="tpu_custom_call" | custom-call | tf_op jit(solution)/shard_map/pallas_call | solution.py:629
  84.3 11.1 %all_to_all.54.recv = f32[8,8,384]{2,1,0:T(8,128)S(1)} all-to-all(f32[8,8,384]{2,1,0:T(8,128)S(1)} %bitcast.17), channel_id=1, replica_groups=mesh['obs_0'=4,'obs_1'=2,'src_0'=4,'src_1'=4] {'obs_0','obs_1'}, dimensions={0} | all-to-all | bytes 196608 | tf_op jit(solution)/shard_map/all_to_all | solution.py:640
  95.5 0.5 shard_map.118
  95.9 8.2 %all_to_all.55 = f32[8,8,384]{2,1,0:T(8,128)S(1)} all-to-all(f32[8,8,384]{2,1,0:T(8,128)S(1)} %get-tuple-element.55), channel_id=1, replica_groups=mesh['obs_0'=4,'obs_1'=2,'src_0'=4,'src_1'=4] {'obs_0','obs_1'}, dimensions={0} | all-to-all | bytes 196608 | tf_op jit(solution)/shard_map/all_to_all | solution.py:640
  104.1 4.7 %shard_map.119 = f32[16,8,768]{2,1,0:T(8,128)S(1)} custom-call(s32[2]{0:T(128)S(1)} %get-tuple-element.36.count, s32[1]{0:T(128)} %bitcast.column, f32[64,384]{1,0:T(8,128)S(1)} %bitcast.16, bf16[72,256,256]{2,1,0:T(8,128)(2,1)S(1)} %get-tuple-element.47.kh, bf16[72,256,256]{2,1,0:T(8,128)(2,1)S(1)} %get-tuple-element.48.kl, ...), custom_call_target="tpu_custom_call" | custom-call | tf_op jit(solution)/shard_map/pallas_call | solution.py:629
  108.9 12.0 %all_to_all.56.recv = f32[16,8,768]{2,1,0:T(8,128)S(1)} all-to-all(f32[16,8,768]{2,1,0:T(8,128)S(1)} %shard_map.119), channel_id=1, replica_groups=mesh['obs_0'=4,'obs_1'=2,'src_0'=4,'src_1'=4] {'src_0','src_1'}, dimensions={0} | all-to-all | bytes 786432 | tf_op jit(solution)/shard_map/all_to_all | solution.py:640
  120.9 1.1 shard_map.120
  122.0 11.7 %all_to_all.57.recv = f32[16,8,768]{2,1,0:T(8,128)S(1)} all-to-all(f32[16,8,768]{2,1,0:T(8,128)S(1)} %get-tuple-element.58), channel_id=1, replica_groups=mesh['obs_0'=4,'obs_1'=2,'src_0'=4,'src_1'=4] {'src_0','src_1'}, dimensions={0} | all-to-all | bytes 786432 | tf_op jit(solution)/shard_map/all_to_all | solution.py:640
  133.7 4.0 %shard_map.121 = f32[64,384]{1,0:T(8,128)S(1)} custom-call(s32[2]{0:T(128)S(1)} %get-tuple-element.36.count, s32[1]{0:T(128)} %bitcast.column, f32[16,8,768]{2,1,0:T(8,128)S(1)} %all_to_all.57.recv, bf16[72,256,256]{2,1,0:T(8,128)(2,1)S(1)} %get-tuple-element.47.kh, bf16[72,256,256]{2,1,0:T(8,128)(2,1)S(1)} %get-tuple-element.48.kl, ...), custom_call_target="tpu_custom_call" | custom-call | tf_op jit(solution)/shard_map/pallas_call | solution.py:629
  137.6 11.0 %all_to_all.58.recv = f32[8,8,384]{2,1,0:T(8,128)S(1)} all-to-all(f32[8,8,384]{2,1,0:T(8,128)S(1)} %bitcast.14), channel_id=1, replica_groups=mesh['obs_0'=4,'obs_1'=2,'src_0'=4,'src_1'=4] {'obs_0','obs_1'}, dimensions={0} | all-to-all | bytes 196608 | tf_op jit(solution)/shard_map/all_to_all | solution.py:640
  148.7 0.9 shard_map.122
Async XLA Ops:
  4.4 16.7 %all-to-all-start = ((f32[16,8,768]{2,1,0:T(8,128)}), f32[16,8,768]{2,1,0:T(8,128)S(1)}, u32[]{:S(2)}, u32[]{:S(2)}) async-start(f32[16,8,768]{2,1,0:T(8,128)} %get-tuple-element.37), calls=%async_computation | async-start | bytes 786432 | tf_op jit(solution)/shard_map/all_to_all | solution.py:640
  21.1 17.9 %copy-start.1 = (f32[8,64,256]{2,1,0:T(8,128)S(1)}, f32[8,64,256]{2,1,0:T(8,128)}, u32[]{:S(2)}) copy-start(f32[8,64,256]{2,1,0:T(8,128)} %basis.9) | copy-start | bytes 1572868
  47.7 19.9 %copy-start = (f32[8,64,1536]{2,1,0:T(8,128)S(1)}, f32[8,64,1536]{2,1,0:T(8,128)}, u32[]{:S(2)}) copy-start(f32[8,64,1536]{2,1,0:T(8,128)} %basis.8) | copy-start | bytes 9437188
  47.7 19.9 %copy-start.2 = (f32[8,1536]{1,0:T(8,128)S(1)}, f32[8,1536]{1,0:T(8,128)}, u32[]{:S(2)}) copy-start(f32[8,1536]{1,0:T(8,128)} %data.3) | copy-start | bytes 147460
